TPU v7x, 32 devices: a whole 2x2x4 slice. The times are simulated.
32 devices in a mesh: seq: 8 (over z, y), head: 4 (over x, core).
Axes of the slice: x: 2, y: 2, z: 4, core: 2. Of those that a mesh axis runs over, the one named last changes fastest.
Arguments:
- hidden_in: bfloat16 [4096, 1536], P('seq', 'head'), may hold values from -6 to 6
- norm_gain: bfloat16 [1536], P('head'), may hold values from 0.5 to 1.5
- gate_weight: bfloat16 [1536, 3072], P(None, 'head'), may hold values from -0.15625 to 0.15625
- value_weight: bfloat16 [1536, 3072], P(None, 'head'), may hold values from -0.15625 to 0.15625
- step_weight: bfloat16 [1536, 48], P(None, 'head'), may hold values from -0.15625 to 0.15625
- state_weight: bfloat16 [1536, 256], replicated, may hold values from -0.15625 to 0.15625
- value_filter: float32 [4, 3072], P(None, 'head'), may hold values from -3 to 3
- value_offset: float32 [3072], P('head'), may hold values from -0.5 to 0.5
- state_filter: float32 [4, 256], replicated, may hold values from -3 to 3
- state_offset: float32 [256], replicated, may hold values from -0.5 to 0.5
- step_bias: float32 [48], P('head'), may hold values from -1 to 0.5
- decay_log: float32 [48], P('head'), as said below
- skip_gain: float32 [48], P('head'), may hold values from 0.5 to 1.5
- mix_gain: float32 [3072], P('head'), may hold values from 0.5 to 1.5
- out_weight: bfloat16 [3072, 1536], P('head'), may hold values from -0.109375 to 0.109375
- lengths: int32 [4], replicated, may hold values from 1 to 2048, 4096 in all
- cotangent: bfloat16 [4096, 1536], P('seq', 'head'), may hold values from -6 to 6
Outputs:
- block_out: bfloat16 [4096, 1536], P('seq', 'head')
- delta_hidden: float32 [4096, 1536], P('seq', 'head')
- delta_norm_gain: float32 [1536], P('head')
- delta_gate_weight: float32 [1536, 3072], P(None, 'head')
- delta_value_weight: float32 [1536, 3072], P(None, 'head')
- delta_step_weight: float32 [1536, 48], P(None, 'head')
- delta_state_weight: float32 [1536, 256], replicated
- delta_value_filter: float32 [4, 3072], P(None, 'head')
- delta_value_offset: float32 [3072], P('head')
- delta_state_filter: float32 [4, 256], replicated
- delta_state_offset: float32 [256], replicated
- delta_step_bias: float32 [48], P('head')
- delta_decay_log: float32 [48], P('head')
- delta_skip_gain: float32 [48], P('head')
- delta_mix_gain: float32 [3072], P('head')
- delta_out_weight: float32 [3072, 1536], P('head')
Inputs may be any that keep to these rules, and one draw needn't show every extreme that they name: `lengths`: they sum to 4096; the longest has exactly 2048 tokens. `decay_log`: one value for each head, between log(0.25 / 4096) and log(1 / 25).
All inputs are finite; a program needn't handle non-finite values.
Results may differ from a plain program's by a relative error of at most 0.01.
Values may be sent and summed in bfloat16 or wider, within the bound.
A program may use at most 128 MiB of HBM per device.

v0:
```python
import jax
import jax.numpy as jnp
from jax import lax
from jax.sharding import PartitionSpec as P

D = 1536
CONV_WIDTH = 4
SPAN = 256
INNER = 3072


EPS = 1e-05
HIGH = lax.Precision.HIGHEST


def shifted(value, axis, steps):
    count = lax.axis_size(axis)
    leading, last = (max(0, -steps), min(count, count - steps))
    return lax.ppermute(value, axis, [(source, source + steps) for source in range(leading, last)])


def sequence_of(places, lengths):
    bounds = jnp.cumsum(lengths, dtype=jnp.int32)
    return jnp.sum((places[:, None] >= bounds[None, :]).astype(jnp.int32), axis=1, dtype=jnp.int32)


def filter_apply(mixed_in, edge_rows, segment, edge_segment, filters, offsets):
    extended = jnp.concatenate([edge_rows, mixed_in], axis=0)
    ext_segment = jnp.concatenate([edge_segment, segment], axis=0)
    count = mixed_in.shape[0]
    summed = jnp.zeros_like(mixed_in) + offsets[None, :]
    for position in range(CONV_WIDTH):
        same_seq = (ext_segment[position : position + count] == segment).astype(jnp.float32)[
            :, None
        ]
        summed = (
            summed + filters[position][None, :] * extended[position : position + count] * same_seq
        )
    return jax.nn.silu(summed)


def span_states(values, inflow, step_size, running, grouped, entering):
    last_sum = running[:, -1:, :]
    tail_mask = (grouped == grouped[:, -1:]).astype(jnp.float32)
    toward_end = jnp.exp(last_sum - running) * tail_mask[:, :, None] * step_size
    span_sums = jnp.einsum("cqh,cqhp,cqn->chpn", toward_end, values, inflow, precision=HIGH)
    passing = jnp.exp(running[:, -1, :]) * (grouped[:, -1] == entering).astype(jnp.float32)[:, None]

    def advance(carried, element):
        state_now, product_now = carried
        span_sum, factor = element
        return (
            (factor[:, None, None] * state_now + span_sum, factor * product_now),
            (state_now, product_now),
        )

    initial = (
        jnp.zeros(span_sums.shape[1:], jnp.float32),
        jnp.ones(passing.shape[1:], jnp.float32),
    )
    (state_end, product_end), (entries, products) = lax.scan(advance, initial, (span_sums, passing))
    return (entries, products, product_end, state_end)


def span_outputs(
    values, inflow, readout, step_size, running, grouped, entering, entries, products, incoming
):
    starts = entries + products[:, :, None, None] * incoming[None]
    lower = jnp.arange(SPAN)[:, None] >= jnp.arange(SPAN)[None, :]
    together = (grouped[:, :, None] == grouped[:, None, :]) & lower[None]
    gaps = running[:, :, None, :] - running[:, None, :, :]
    decays = jnp.exp(jnp.where(together[..., None], gaps, 0.0)) * together[..., None].astype(
        jnp.float32
    )
    intersections = jnp.einsum("cin,cjn->cij", readout, inflow, precision=HIGH)
    mixing = decays * intersections[..., None] * step_size[:, None, :, :]
    result = jnp.einsum("cijh,cjhp->cihp", mixing, values, precision=HIGH)
    entering_mask = (grouped == entering[:, None]).astype(jnp.float32)
    carried = jnp.exp(running) * entering_mask[:, :, None]
    return result + carried[..., None] * jnp.einsum(
        "cin,chpn->cihp", readout, starts, precision=HIGH
    )


def carry_chain(factors, pushed, direction):

    def relay_turn(counter, incoming):
        return shifted(factors[:, None, None] * incoming + pushed, "seq", direction)

    return lax.fori_loop(0, lax.axis_size("seq") - 1, relay_turn, jnp.zeros_like(pushed))


def contract_rows(left, right):
    return lax.dot_general(
        left, right, (((0,), (0,)), ((), ())), preferred_element_type=jnp.float32
    )


def contract_cols(left, right):
    return lax.dot_general(
        left, right, (((1,), (1,)), ((), ())), preferred_element_type=jnp.float32
    )


def local(
    hidden_in,
    norm_gain,
    gate_weight,
    value_weight,
    step_weight,
    state_weight,
    value_filter,
    value_offset,
    state_filter,
    state_offset,
    step_bias,
    decay_log,
    skip_gain,
    mix_gain,
    out_weight,
    lengths,
    cotangent,
):
    tokens_dev = hidden_in.shape[0]
    width_dev = hidden_in.shape[1]
    heads_dev = step_weight.shape[1]
    inner_dev = value_weight.shape[1]
    head_size = inner_dev // heads_dev
    state_size = state_weight.shape[1] // 2
    spans = tokens_dev // SPAN
    tail_rows = CONV_WIDTH - 1
    anchor = lax.axis_index("seq") * tokens_dev
    segment = sequence_of(anchor + jnp.arange(tokens_dev, dtype=jnp.int32), lengths)
    edge_segment = sequence_of(anchor - tail_rows + jnp.arange(tail_rows, dtype=jnp.int32), lengths)
    before = sequence_of(jnp.reshape(anchor - 1, (1,)), lengths)
    grouped = segment.reshape(spans, SPAN)
    entering = jnp.concatenate([before, segment[:-1]]).reshape(spans, SPAN)[:, 0]
    gathered, gain_full = (
        lax.all_gather(hidden_in, "head", axis=1, tiled=True),
        lax.all_gather(norm_gain, "head", axis=0, tiled=True),
    )
    gathered_f = gathered.astype(jnp.float32)
    scale_in = lax.rsqrt(jnp.mean(gathered_f * gathered_f, axis=1, keepdims=True) + EPS)
    normed = (gathered_f * scale_in * gain_full.astype(jnp.float32)[None, :]).astype(jnp.bfloat16)
    gate_in = jnp.dot(normed, gate_weight, preferred_element_type=jnp.float32)
    value_in = jnp.dot(normed, value_weight, preferred_element_type=jnp.float32)
    state_in = jnp.dot(normed, state_weight, preferred_element_type=jnp.float32)
    step_in = jnp.dot(normed, step_weight, preferred_element_type=jnp.float32)
    mixed_in = jnp.concatenate([value_in, state_in], axis=1)
    edge_rows = shifted(mixed_in[tokens_dev - tail_rows :], "seq", 1)
    filters = jnp.concatenate([value_filter, state_filter], axis=1)
    offsets = jnp.concatenate([value_offset, state_offset], axis=0)

    def front(mixed_part, edge_part, filter_part, offset_part, step_part, bias_part, rate_part):
        activated = filter_apply(
            mixed_part, edge_part, segment, edge_segment, filter_part, offset_part
        )
        step_size = jax.nn.softplus(step_part + bias_part[None, :])
        return (activated, step_size, -jnp.exp(rate_part)[None, :] * step_size)

    (activated, step_size, log_decay), front_back = jax.vjp(
        front, mixed_in, edge_rows, filters, offsets, step_in, step_bias, decay_log
    )
    values = activated[:, :inner_dev].reshape(spans, SPAN, heads_dev, head_size)
    inflow = activated[:, inner_dev : inner_dev + state_size].reshape(spans, SPAN, state_size)
    readout = activated[:, inner_dev + state_size :].reshape(spans, SPAN, state_size)
    steps_c = step_size.reshape(spans, SPAN, heads_dev)
    logs_c = log_decay.reshape(spans, SPAN, heads_dev)

    def state_part(values_p, inflow_p, steps_p, logs_p):
        return span_states(
            values_p, inflow_p, steps_p, jnp.cumsum(logs_p, axis=1), grouped, entering
        )

    def output_part(
        values_p, inflow_p, readout_p, steps_p, logs_p, entries_p, products_p, incoming_p
    ):
        return span_outputs(
            values_p,
            inflow_p,
            readout_p,
            steps_p,
            jnp.cumsum(logs_p, axis=1),
            grouped,
            entering,
            entries_p,
            products_p,
            incoming_p,
        )

    (entries, products, product_end, state_end), states_back = jax.vjp(
        state_part, values, inflow, steps_c, logs_c
    )
    incoming = carry_chain(product_end, state_end, 1)
    scanned, outputs_back = jax.vjp(
        output_part, values, inflow, readout, steps_c, logs_c, entries, products, incoming
    )
    values_flat = values.reshape(tokens_dev, heads_dev, head_size)
    mixer = (
        scanned.reshape(tokens_dev, heads_dev, head_size) + skip_gain[None, :, None] * values_flat
    ).reshape(tokens_dev, inner_dev)
    gate_act = jax.nn.silu(gate_in)
    gated = mixer * gate_act
    square_sum = lax.psum(jnp.sum(gated * gated, axis=1), "head")
    scale_mix = lax.rsqrt(square_sum / INNER + EPS)[:, None]
    mix_out = (gated * scale_mix * mix_gain[None, :]).astype(jnp.bfloat16)
    partial_out = jnp.dot(mix_out, out_weight, preferred_element_type=jnp.float32)
    mixed_sum = lax.psum_scatter(
        partial_out.astype(jnp.bfloat16), "head", scatter_dimension=1, tiled=True
    ).astype(jnp.float32)
    own_rows = hidden_in.astype(jnp.float32)
    block_out = (own_rows + mixed_sum).astype(jnp.bfloat16)
    cot_full = lax.all_gather(cotangent, "head", axis=1, tiled=True)
    delta_out_weight = contract_rows(mix_out, cot_full)
    d_mix = contract_cols(cot_full, out_weight)
    delta_mix_gain = jnp.sum(d_mix * gated * scale_mix, axis=0)
    weighted_mix = d_mix * mix_gain[None, :]
    mix_dot = lax.psum(jnp.sum(weighted_mix * gated, axis=1), "head")
    d_gated = scale_mix * weighted_mix - gated * scale_mix**3 * (mix_dot / INNER)[:, None]
    d_mixer = d_gated * gate_act
    sigmoid_gate = jax.nn.sigmoid(gate_in)
    d_gate = (d_gated * mixer * sigmoid_gate * (1.0 + gate_in * (1.0 - sigmoid_gate))).astype(
        jnp.bfloat16
    )
    d_mixer3 = d_mixer.reshape(tokens_dev, heads_dev, head_size)
    delta_skip_gain = jnp.sum(d_mixer3 * values_flat, axis=(0, 2))
    d_values_a, d_inflow_a, d_readout, d_steps_a, d_logs_a, d_entries, d_products, d_incoming = (
        outputs_back(d_mixer3.reshape(spans, SPAN, heads_dev, head_size))
    )
    costate = carry_chain(product_end, d_incoming, -1)
    d_factor = jnp.sum(costate * incoming, axis=(1, 2))
    d_values_b, d_inflow_b, d_steps_b, d_logs_b = states_back(
        (d_entries, d_products, d_factor, costate)
    )
    d_shared = jnp.concatenate(
        [
            (d_inflow_a + d_inflow_b).reshape(tokens_dev, state_size),
            d_readout.reshape(tokens_dev, state_size),
        ],
        axis=1,
    )
    d_shared = lax.psum(d_shared, "head")
    d_values = (d_values_a + d_values_b).reshape(tokens_dev, inner_dev) + (
        skip_gain[None, :, None] * d_mixer3
    ).reshape(tokens_dev, inner_dev)
    d_activated = jnp.concatenate([d_values, d_shared], axis=1)
    d_steps = (d_steps_a + d_steps_b).reshape(tokens_dev, heads_dev)
    d_logs = (d_logs_a + d_logs_b).reshape(tokens_dev, heads_dev)
    d_mixed, d_edge, d_filters, d_offsets, d_step_in, delta_step_bias, delta_decay_log = front_back(
        (d_activated, d_steps, d_logs)
    )
    back_edge = shifted(d_edge, "seq", -1)
    d_mixed = d_mixed + jnp.pad(back_edge, ((tokens_dev - tail_rows, 0), (0, 0)))
    d_value = d_mixed[:, :inner_dev].astype(jnp.bfloat16)
    d_state = d_mixed[:, inner_dev:].astype(jnp.bfloat16)
    d_step_raw = d_step_in.astype(jnp.bfloat16)
    delta_gate_weight = contract_rows(normed, d_gate)
    delta_value_weight = contract_rows(normed, d_value)
    delta_state_weight = contract_rows(normed, d_state)
    delta_step_weight = contract_rows(normed, d_step_raw)
    d_normed_part = (
        contract_cols(d_gate, gate_weight)
        + contract_cols(d_value, value_weight)
        + contract_cols(d_step_raw, step_weight)
    )
    d_normed = lax.psum_scatter(
        d_normed_part.astype(jnp.bfloat16), "head", scatter_dimension=1, tiled=True
    ).astype(jnp.float32)
    state_rows = lax.dynamic_slice_in_dim(
        state_weight, lax.axis_index("head") * width_dev, width_dev, 0
    )
    d_normed = d_normed + contract_cols(d_state, state_rows)
    gain_own = norm_gain.astype(jnp.float32)[None, :]
    delta_norm_gain = jnp.sum(d_normed * own_rows * scale_in, axis=0)
    weighted_in = d_normed * gain_own
    input_dot = lax.psum(jnp.sum(weighted_in * own_rows, axis=1), "head")
    delta_hidden = (
        cotangent.astype(jnp.float32)
        + scale_in * weighted_in
        - own_rows * scale_in**3 * (input_dot / D)[:, None]
    )
    summed = lax.psum(
        (
            delta_norm_gain,
            delta_gate_weight,
            delta_value_weight,
            delta_step_weight,
            delta_state_weight,
            d_filters[:, :inner_dev],
            d_offsets[:inner_dev],
            d_filters[:, inner_dev:],
            d_offsets[inner_dev:],
            delta_step_bias,
            delta_decay_log,
            delta_skip_gain,
            delta_mix_gain,
            delta_out_weight,
        ),
        "seq",
    )
    return (
        block_out,
        delta_hidden,
        summed[0],
        summed[1],
        summed[2],
        summed[3],
        summed[4],
        summed[5],
        summed[6],
        summed[7],
        summed[8],
        summed[9],
        summed[10],
        summed[11],
        summed[12],
        summed[13],
    )


def solution(mesh):
    in_specs = (
        P("seq", "head"),
        P("head"),
        P(None, "head"),
        P(None, "head"),
        P(None, "head"),
        P(),
        P(None, "head"),
        P("head"),
        P(),
        P(),
        P("head"),
        P("head"),
        P("head"),
        P("head"),
        P("head", None),
        P(),
        P("seq", "head"),
    )
    out_specs = (
        P("seq", "head"),
        P("seq", "head"),
        P("head"),
        P(None, "head"),
        P(None, "head"),
        P(None, "head"),
        P(),
        P(None, "head"),
        P("head"),
        P(),
        P(),
        P("head"),
        P("head"),
        P("head"),
        P("head"),
        P("head", None),
    )
    return jax.shard_map(local, mesh=mesh, in_specs=in_specs, out_specs=out_specs, check_vma=False)
```

profile of v0, /device:TPU:0, one launch (start us, length us, event | category | flops | bytes accessed | tf_op | source)
XLA Modules:
  0.0 970.3 jit_solution(10257609495007890905)
XLA Ops:
  13.2 6.1 all-gather
  24.0 7.9 all-gather.4.cloned.1.call-done
  66.1 8.6 while.62
  77.5 78.8 %while.59 = (s32[]{:T(128)}, f32[12,64,128]{2,1,0:T(8,128)S(1)}, f32[12]{0:T(128)S(1)}, f32[12,64,128]{2,1,0:T(8,128)S(1)}, s32[]{:T(128)}) while((s32[]{:T(128)}, f32[12,64,128]{2,1,0:T(8,128)S(1)}, f32[12]{0:T(128)S(1)}, f32[12,64,128]{2,1,0:T(8,128)S(1)}, s32[]{:T(128)}) %tuple.142), condition=%wide.region_10.11_spmd, body=%wide.region_9.10_spmd.sunk | while | flops 196610 | bytes 2752661 | solution.py:90
  81.7 8.0 collective-permute-done
  89.8 4.4 collective-permute-start
  94.2 7.1 collective-permute-done
  101.5 4.5 collective-permute-start
  106.0 6.2 collective-permute-done
  112.2 5.1 collective-permute-start
  117.3 5.2 collective-permute-done
  122.7 5.3 collective-permute-start
  128.0 5.2 collective-permute-done
  133.3 5.5 collective-permute-start
  138.9 6.3 collective-permute-done
  145.3 5.6 collective-permute-start
  151.0 5.2 collective-permute-done
  159.1 8.0 bitcast_add_fusion.3
  172.6 5.7 multiply_reduce_fusion.10
  178.3 5.6 psum.126
  184.0 4.7 convolution_convert_fusion
  188.7 5.8 multiply_reduce_fusion.6
  194.6 6.0 psum.127
  200.6 5.5 multiply_reduce_fusion.7
  215.1 4.2 fusion.63
  223.0 89.0 %while.60 = (s32[]{:T(128)}, f32[12,64,128]{2,1,0:T(8,128)S(1)}, f32[12]{0:T(128)S(1)}, f32[12,64,128]{2,1,0:T(8,128)S(1)}, s32[]{:T(128)}) while((s32[]{:T(128)}, f32[12,64,128]{2,1,0:T(8,128)S(1)}, f32[12]{0:T(128)S(1)}, f32[12,64,128]{2,1,0:T(8,128)S(1)}, s32[]{:T(128)}) %tuple.166), condition=%wide.region_18.19_spmd, body=%wide.region_17.18_spmd.sunk | while | flops 196610 | bytes 2752661 | solution.py:90
  225.2 12.9 %collective-permute-done.1 = f32[12,64,128]{2,1,0:T(8,128)S(1)} collective-permute-done((f32[12,64,128]{2,1,0:T(8,128)}, f32[12,64,128]{2,1,0:T(8,128)S(1)}, u32[]{:S(2)}, u32[]{:S(2)}) %collective-permute-start.1) | collective-permute-done | bytes 393248 | tf_op jit(solution)/shard_map/while/body/eval_jaxpr/ppermute | solution.py:19
  240.2 12.3 %collective-permute-done.1 = f32[12,64,128]{2,1,0:T(8,128)S(1)} collective-permute-done((f32[12,64,128]{2,1,0:T(8,128)}, f32[12,64,128]{2,1,0:T(8,128)S(1)}, u32[]{:S(2)}, u32[]{:S(2)}) %collective-permute-start.1) | collective-permute-done | bytes 393248 | tf_op jit(solution)/shard_map/while/body/eval_jaxpr/ppermute | solution.py:19
  254.7 10.7 %collective-permute-done.1 = f32[12,64,128]{2,1,0:T(8,128)S(1)} collective-permute-done((f32[12,64,128]{2,1,0:T(8,128)}, f32[12,64,128]{2,1,0:T(8,128)S(1)}, u32[]{:S(2)}, u32[]{:S(2)}) %collective-permute-start.1) | collective-permute-done | bytes 393248 | tf_op jit(solution)/shard_map/while/body/eval_jaxpr/ppermute | solution.py:19
  267.6 9.9 %collective-permute-done.1 = f32[12,64,128]{2,1,0:T(8,128)S(1)} collective-permute-done((f32[12,64,128]{2,1,0:T(8,128)}, f32[12,64,128]{2,1,0:T(8,128)S(1)}, u32[]{:S(2)}, u32[]{:S(2)}) %collective-permute-start.1) | collective-permute-done | bytes 393248 | tf_op jit(solution)/shard_map/while/body/eval_jaxpr/ppermute | solution.py:19
  279.6 9.2 collective-permute-done.1
  290.9 9.5 collective-permute-done.1
  302.5 9.5 collective-permute-done.1
  313.3 8.9 while.61
  322.3 4.9 fusion.64
  328.7 11.3 %fusion.22 = (f32[2,256,12]{1,2,0:T(8,128)}, f32[2,256,12]{1,2,0:T(8,128)}, f32[2,256,12]{1,2,0:T(8,128)}, f32[2,256,256]{2,1,0:T(8,128)S(1)}) fusion(f32[2,256,12]{1,2,0:T(8,128)S(1)} %copy-done.72, f32[2,256,256]{2,1,0:T(8,128)S(1)} %copy-done.39, f32[2,256,256]{2,1,0:T(8,128)S(1)} %copy-done.37, f32[2,256,12]{1,2,0:T(8,128)S(1)} %bitcast.227, ...), kind=kOutput, calls=%fused_computation.42 | convolution fusion | flops 1231403008 | bytes 4972544 | tf_op jit(solution)/shard_map/transpose(jvp(cijh,cjhp->cihp))/dot_general | solution.py:77
  341.3 6.7 bitcast_add_fusion.2
  353.6 5.7 reduce-window.29
  372.2 5.2 reduce-window.31
  381.9 4.3 fusion.123
  386.2 12.6 %all-reduce.16.cloned.1.call-done = f32[512,256]{1,0:T(8,128)} async-done(((f32[512,256]{1,0:T(8,128)}), f32[512,256]{1,0:T(8,128)}) %all-reduce.16.cloned.1.call-update) | async-done | bytes 524304 | tf_op jit(solution)/shard_map/psum | solution.py:242
  398.8 6.6 multiply_reduce_fusion.3
  420.7 5.2 fusion.125
  441.3 18.5 %reduce-scatter.9.cloned.1.call-done = bf16[384,512]{1,0:T(8,128)(2,1)} async-done(((bf16[1536,512]{1,0:T(8,128)(2,1)}), bf16[384,512]{1,0:T(8,128)(2,1)}) %reduce-scatter.9.cloned.1.call-update) | async-done | bytes 393232
  464.7 40.6 %all-reduce.11 = (f32[384]{0:T(512)}, f32[4,768]{1,0:T(4,128)}, f32[768]{0:T(1024)}, f32[4,256]{1,0:T(4,128)}, f32[256]{0:T(256)}, /*index=5*/f32[12]{0:T(128)}, f32[12]{0:T(128)}, f32[12]{0:T(128)}, f32[768]{0:T(1024)}) all-reduce(f32[384]{0:T(512)} %get-tuple-element.371, ...), channel_id=1, replica_groups=mesh['seq'=8,'head'=4] {'seq'}, use_global_device_ids=true, to_apply=%region_39.40 | all-reduce | flops 6308 | bytes 50464 | tf_op jit(solution)/shard_map/psum | solution.py:282
  505.3 6.2 psum.129
  514.0 437.0 %all-reduce.18.cloned.1.call-done = (f32[1536,768]{1,0:T(8,128)}, f32[1536,768]{1,0:T(8,128)}, f32[1536,12]{0,1:T(8,128)}, f32[1536,256]{1,0:T(8,128)}, f32[768,1536]{1,0:T(8,128)}) async-done(((f32[1536,768]{1,0:T(8,128)}, f32[1536,768]{1,0:T(8,128)}, f32[1536,12]{0,1:T(8,128)}, f32[1536,256]{1,0:T(8,128)}, f32[768,1536]{1,0:T(8,128)}), (f32[1536,768]{1,0:T(8,128)}, f32[1536,768]{1,0:T(8,128)}, ...) | async-done | bytes 15802384 | tf_op jit(solution)/shard_map/psum | solution.py:282
  950.9 5.2 copy.353
  (409 shorter events, 177.1 us)
Async XLA Ops:
  7.2 165.4 %copy-start = (bf16[1536,768]{1,0:T(8,128)(2,1)S(1)}, bf16[1536,768]{1,0:T(8,128)(2,1)}, u32[]{:S(2)}) copy-start(bf16[1536,768]{1,0:T(8,128)(2,1)} %param.27) | copy-start | bytes 7077892
  7.2 24.8 %all-gather.4.cloned.1.call-start = ((), (), s32[]{:S(2)}) async-start(), calls=%async_computation.2 | async-start | bytes 1966080 | tf_op jit(solution)/shard_map/all_gather | solution.py:139
  7.9 180.8 %all-gather.6.cloned.1.call-start = ((), (), s32[]{:S(2)}) async-start(), calls=%async_computation.3 | async-start | bytes 1966080 | tf_op jit(solution)/shard_map/all_gather | solution.py:213
  8.7 390.1 %all-reduce.16.cloned.1.call-start = ((), (), s32[]{:S(2)}) async-start(), calls=%async_computation.4 | async-start | bytes 1048576 | tf_op jit(solution)/shard_map/psum | solution.py:242
  11.3 37.7 %copy-start.90 = (f32[2]{0:T(128)}, f32[2]{0:T(128)S(1)}, u32[]{:S(2)}) copy-start(f32[2]{0:T(128)S(1)} %fusion.104) | copy-start | bytes 28
  12.3 22.5 %copy-start.93 = (f32[12]{0:T(128)}, f32[12]{0:T(128)S(1)}, u32[]{:S(2)}) copy-start(f32[12]{0:T(128)S(1)} %exponential_negate_fusion) | copy-start | bytes 148
  13.2 36.7 %copy-start.74 = (f32[512]{0:T(512)}, f32[512]{0:T(512)S(1)}, u32[]{:S(2)}) copy-start(f32[512]{0:T(512)S(1)} %get-tuple-element.482) | copy-start | bytes 6148
  13.2 36.7 %copy-start.76 = (f32[512]{0:T(512)}, f32[512]{0:T(512)S(1)}, u32[]{:S(2)}) copy-start(f32[512]{0:T(512)S(1)} %get-tuple-element.483) | copy-start | bytes 6148
  13.2 36.7 %copy-start.78 = (f32[512]{0:T(512)}, f32[512]{0:T(512)S(1)}, u32[]{:S(2)}) copy-start(f32[512]{0:T(512)S(1)} %get-tuple-element.484) | copy-start | bytes 6148
  22.2 27.7 %copy-start.53 = (f32[1,1024]{1,0:T(1,128)}, f32[1,1024]{1,0:T(1,128)S(1)}, u32[]{:S(2)}) copy-start(f32[1,1024]{1,0:T(1,128)S(1)} %get-tuple-element.479) | copy-start | bytes 12292
  22.2 27.7 %copy-start.55 = (f32[1,1024]{1,0:T(1,128)}, f32[1,1024]{1,0:T(1,128)S(1)}, u32[]{:S(2)}) copy-start(f32[1,1024]{1,0:T(1,128)S(1)} %get-tuple-element.480) | copy-start | bytes 12292
  22.2 27.7 %copy-start.57 = (f32[1,1024]{1,0:T(1,128)}, f32[1,1024]{1,0:T(1,128)S(1)}, u32[]{:S(2)}) copy-start(f32[1,1024]{1,0:T(1,128)S(1)} %get-tuple-element.481) | copy-start | bytes 12292
  23.3 25.0 %copy-start.69 = (f32[2,256]{1,0:T(2,128)}, f32[2,256]{1,0:T(2,128)S(1)}, u32[]{:S(2)}) copy-start(f32[2,256]{1,0:T(2,128)S(1)} %get-tuple-element.490) | copy-start | bytes 6148
  23.3 25.0 %copy-start.80 = (f32[2,256]{1,0:T(2,128)}, f32[2,256]{1,0:T(2,128)S(1)}, u32[]{:S(2)}) copy-start(f32[2,256]{1,0:T(2,128)S(1)} %get-tuple-element.489) | copy-start | bytes 6148
  24.0 12.0 %copy-start.96 = (f32[12]{0:T(128)S(1)}, f32[12]{0:T(128)}, u32[]{:S(2)}) copy-start(f32[12]{0:T(128)} %param.35) | copy-start | bytes 148
  44.7 4.9 collective-permute-start.2
  48.9 12.7 %copy-start.43 = (f32[2,256,12]{1,2,0:T(8,128)}, f32[2,256,12]{1,2,0:T(8,128)S(1)}, u32[]{:S(2)}) copy-start(f32[2,256,12]{1,2,0:T(8,128)S(1)} %get-tuple-element.474) | copy-start | bytes 73732
  77.6 12.1 %collective-permute-start = (f32[12,64,128]{2,1,0:T(8,128)S(1)}, f32[12,64,128]{2,1,0:T(8,128)S(1)}, u32[]{:S(2)}, u32[]{:S(2)}) collective-permute-start(f32[12,64,128]{2,1,0:T(8,128)S(1)} %multiply_add_fusion.11), channel_id=1, source_target_pairs={{0,4},{4,8},{8,12},{12,16},{16,20},{20,24},{24,28},{1,5},{5,9},{9,... | collective-permute-start | bytes 1179656 | tf_op jit(solution)/shard_map/while/body/eval_jaxpr/ppermute | solution.py:19
  89.8 11.5 %collective-permute-start = (f32[12,64,128]{2,1,0:T(8,128)S(1)}, f32[12,64,128]{2,1,0:T(8,128)S(1)}, u32[]{:S(2)}, u32[]{:S(2)}) collective-permute-start(f32[12,64,128]{2,1,0:T(8,128)S(1)} %multiply_add_fusion.11), channel_id=1, source_target_pairs={{0,4},{4,8},{8,12},{12,16},{16,20},{20,24},{24,28},{1,5},{5,9},{9,... | collective-permute-start | bytes 1179656 | tf_op jit(solution)/shard_map/while/body/eval_jaxpr/ppermute | solution.py:19
  101.5 10.7 %collective-permute-start = (f32[12,64,128]{2,1,0:T(8,128)S(1)}, f32[12,64,128]{2,1,0:T(8,128)S(1)}, u32[]{:S(2)}, u32[]{:S(2)}) collective-permute-start(f32[12,64,128]{2,1,0:T(8,128)S(1)} %multiply_add_fusion.11), channel_id=1, source_target_pairs={{0,4},{4,8},{8,12},{12,16},{16,20},{20,24},{24,28},{1,5},{5,9},{9,... | collective-permute-start | bytes 1179656 | tf_op jit(solution)/shard_map/while/body/eval_jaxpr/ppermute | solution.py:19
  112.2 10.3 %collective-permute-start = (f32[12,64,128]{2,1,0:T(8,128)S(1)}, f32[12,64,128]{2,1,0:T(8,128)S(1)}, u32[]{:S(2)}, u32[]{:S(2)}) collective-permute-start(f32[12,64,128]{2,1,0:T(8,128)S(1)} %multiply_add_fusion.11), channel_id=1, source_target_pairs={{0,4},{4,8},{8,12},{12,16},{16,20},{20,24},{24,28},{1,5},{5,9},{9,... | collective-permute-start | bytes 1179656 | tf_op jit(solution)/shard_map/while/body/eval_jaxpr/ppermute | solution.py:19
  122.7 10.6 %collective-permute-start = (f32[12,64,128]{2,1,0:T(8,128)S(1)}, f32[12,64,128]{2,1,0:T(8,128)S(1)}, u32[]{:S(2)}, u32[]{:S(2)}) collective-permute-start(f32[12,64,128]{2,1,0:T(8,128)S(1)} %multiply_add_fusion.11), channel_id=1, source_target_pairs={{0,4},{4,8},{8,12},{12,16},{16,20},{20,24},{24,28},{1,5},{5,9},{9,... | collective-permute-start | bytes 1179656 | tf_op jit(solution)/shard_map/while/body/eval_jaxpr/ppermute | solution.py:19
  133.3 11.9 %collective-permute-start = (f32[12,64,128]{2,1,0:T(8,128)S(1)}, f32[12,64,128]{2,1,0:T(8,128)S(1)}, u32[]{:S(2)}, u32[]{:S(2)}) collective-permute-start(f32[12,64,128]{2,1,0:T(8,128)S(1)} %multiply_add_fusion.11), channel_id=1, source_target_pairs={{0,4},{4,8},{8,12},{12,16},{16,20},{20,24},{24,28},{1,5},{5,9},{9,... | collective-permute-start | bytes 1179656 | tf_op jit(solution)/shard_map/while/body/eval_jaxpr/ppermute | solution.py:19
  145.3 10.9 %collective-permute-start = (f32[12,64,128]{2,1,0:T(8,128)S(1)}, f32[12,64,128]{2,1,0:T(8,128)S(1)}, u32[]{:S(2)}, u32[]{:S(2)}) collective-permute-start(f32[12,64,128]{2,1,0:T(8,128)S(1)} %multiply_add_fusion.11), channel_id=1, source_target_pairs={{0,4},{4,8},{8,12},{12,16},{16,20},{20,24},{24,28},{1,5},{5,9},{9,... | collective-permute-start | bytes 1179656 | tf_op jit(solution)/shard_map/while/body/eval_jaxpr/ppermute | solution.py:19
  184.0 16.6 %copy-start.67 = (f32[512]{0:T(512)}, f32[512]{0:T(512)S(1)}, u32[]{:S(2)}) copy-start(f32[512]{0:T(512)S(1)} %get-tuple-element.488) | copy-start | bytes 6148
  223.9 14.2 %collective-permute-start.1 = (f32[12,64,128]{2,1,0:T(8,128)}, f32[12,64,128]{2,1,0:T(8,128)S(1)}, u32[]{:S(2)}, u32[]{:S(2)}) collective-permute-start(f32[12,64,128]{2,1,0:T(8,128)} %multiply_add_fusion.12), channel_id=1, source_target_pairs={{4,0},{8,4},{12,8},{16,12},{20,16},{24,20},{28,24},{5,1},{9,5},{13... | collective-permute-start | bytes 1179656 | tf_op jit(solution)/shard_map/while/body/eval_jaxpr/ppermute | solution.py:19
  238.9 13.6 %collective-permute-start.1 = (f32[12,64,128]{2,1,0:T(8,128)}, f32[12,64,128]{2,1,0:T(8,128)S(1)}, u32[]{:S(2)}, u32[]{:S(2)}) collective-permute-start(f32[12,64,128]{2,1,0:T(8,128)} %multiply_add_fusion.12), channel_id=1, source_target_pairs={{4,0},{8,4},{12,8},{16,12},{20,16},{24,20},{28,24},{5,1},{9,5},{13... | collective-permute-start | bytes 1179656 | tf_op jit(solution)/shard_map/while/body/eval_jaxpr/ppermute | solution.py:19
  253.4 12.0 %collective-permute-start.1 = (f32[12,64,128]{2,1,0:T(8,128)}, f32[12,64,128]{2,1,0:T(8,128)S(1)}, u32[]{:S(2)}, u32[]{:S(2)}) collective-permute-start(f32[12,64,128]{2,1,0:T(8,128)} %multiply_add_fusion.12), channel_id=1, source_target_pairs={{4,0},{8,4},{12,8},{16,12},{20,16},{24,20},{28,24},{5,1},{9,5},{13... | collective-permute-start | bytes 1179656 | tf_op jit(solution)/shard_map/while/body/eval_jaxpr/ppermute | solution.py:19
  266.3 11.2 %collective-permute-start.1 = (f32[12,64,128]{2,1,0:T(8,128)}, f32[12,64,128]{2,1,0:T(8,128)S(1)}, u32[]{:S(2)}, u32[]{:S(2)}) collective-permute-start(f32[12,64,128]{2,1,0:T(8,128)} %multiply_add_fusion.12), channel_id=1, source_target_pairs={{4,0},{8,4},{12,8},{16,12},{20,16},{24,20},{28,24},{5,1},{9,5},{13... | collective-permute-start | bytes 1179656 | tf_op jit(solution)/shard_map/while/body/eval_jaxpr/ppermute | solution.py:19
  278.3 10.5 %collective-permute-start.1 = (f32[12,64,128]{2,1,0:T(8,128)}, f32[12,64,128]{2,1,0:T(8,128)S(1)}, u32[]{:S(2)}, u32[]{:S(2)}) collective-permute-start(f32[12,64,128]{2,1,0:T(8,128)} %multiply_add_fusion.12), channel_id=1, source_target_pairs={{4,0},{8,4},{12,8},{16,12},{20,16},{24,20},{28,24},{5,1},{9,5},{13... | collective-permute-start | bytes 1179656 | tf_op jit(solution)/shard_map/while/body/eval_jaxpr/ppermute | solution.py:19
  289.6 10.8 %collective-permute-start.1 = (f32[12,64,128]{2,1,0:T(8,128)}, f32[12,64,128]{2,1,0:T(8,128)S(1)}, u32[]{:S(2)}, u32[]{:S(2)}) collective-permute-start(f32[12,64,128]{2,1,0:T(8,128)} %multiply_add_fusion.12), channel_id=1, source_target_pairs={{4,0},{8,4},{12,8},{16,12},{20,16},{24,20},{28,24},{5,1},{9,5},{13... | collective-permute-start | bytes 1179656 | tf_op jit(solution)/shard_map/while/body/eval_jaxpr/ppermute | solution.py:19
  301.3 10.8 %collective-permute-start.1 = (f32[12,64,128]{2,1,0:T(8,128)}, f32[12,64,128]{2,1,0:T(8,128)S(1)}, u32[]{:S(2)}, u32[]{:S(2)}) collective-permute-start(f32[12,64,128]{2,1,0:T(8,128)} %multiply_add_fusion.12), channel_id=1, source_target_pairs={{4,0},{8,4},{12,8},{16,12},{20,16},{24,20},{28,24},{5,1},{9,5},{13... | collective-permute-start | bytes 1179656 | tf_op jit(solution)/shard_map/while/body/eval_jaxpr/ppermute | solution.py:19
  348.1 11.9 %copy-start.60 = (f32[2,12]{1,0:T(2,128)S(1)}, f32[2,12]{1,0:T(2,128)}, u32[]{:S(2)}) copy-start(f32[2,12]{1,0:T(2,128)} %copy-done.59) | copy-start | bytes 292
  348.1 11.9 %copy-start.91 = (f32[2]{0:T(128)S(1)}, f32[2]{0:T(128)}, u32[]{:S(2)}) copy-start(f32[2]{0:T(128)} %copy-done.90) | copy-start | bytes 28
  348.1 12.0 %copy-start.21 = (f32[512,128]{1,0:T(8,128)S(1)}, f32[512,128]{1,0:T(8,128)}, u32[]{:S(2)}) copy-start(f32[512,128]{1,0:T(8,128)} %copy-done.19) | copy-start | bytes 786436
  348.1 13.6 %copy-start.18 = (f32[512,128]{1,0:T(8,128)S(1)}, f32[512,128]{1,0:T(8,128)}, u32[]{:S(2)}) copy-start(f32[512,128]{1,0:T(8,128)} %get-tuple-element.465) | copy-start | bytes 786436
  364.5 75.5 %reduce-scatter.7.cloned.1.call-start = ((), (), s32[]{:S(2)}) async-start(), calls=%async_computation.5 | async-start | bytes 1966080
  381.1 78.6 %reduce-scatter.9.cloned.1.call-start = ((), (), s32[]{:S(2)}) async-start(), calls=%async_computation.6 | async-start | bytes 1966080
  381.9 16.9 %copy-start.14 = (f32[512,256]{1,0:T(8,128)S(1)}, f32[512,256]{1,0:T(8,128)}, u32[]{:S(2)}) copy-start(f32[512,256]{1,0:T(8,128)} %copy-done.13) | copy-start | bytes 1572868
  381.9 16.9 %copy-start.75 = (f32[512]{0:T(512)S(1)}, f32[512]{0:T(512)}, u32[]{:S(2)}) copy-start(f32[512]{0:T(512)} %copy-done.74) | copy-start | bytes 6148
  381.9 16.9 %copy-start.77 = (f32[512]{0:T(512)S(1)}, f32[512]{0:T(512)}, u32[]{:S(2)}) copy-start(f32[512]{0:T(512)} %copy-done.76) | copy-start | bytes 6148
  381.9 16.9 %copy-start.79 = (f32[512]{0:T(512)S(1)}, f32[512]{0:T(512)}, u32[]{:S(2)}) copy-start(f32[512]{0:T(512)} %copy-done.78) | copy-start | bytes 6148
  405.4 32.7 %copy-start.63 = (f32[1024]{0:T(1024)}, f32[1024]{0:T(1024)S(1)}, u32[]{:S(2)}) copy-start(f32[1024]{0:T(1024)S(1)} %get-tuple-element.364) | copy-start | bytes 12292
  406.1 5.6 collective-permute-start.3
  418.0 533.0 %all-reduce.18.cloned.1.call-start = ((), (), s32[]{:S(2)}) async-start(), calls=%async_computation.7 | async-start | bytes 31653888 | tf_op jit(solution)/shard_map/psum | solution.py:282
  435.0 26.6 %copy-start.31 = (bf16[512,384]{1,0:T(8,128)(2,1)S(1)}, bf16[512,384]{1,0:T(8,128)(2,1)}, u32[]{:S(2)}) copy-start(bf16[512,384]{1,0:T(8,128)(2,1)} %param.25) | copy-start | bytes 1179652
  435.0 26.6 %copy-start.85 = (f32[512]{0:T(512)S(1)}, f32[512]{0:T(512)}, u32[]{:S(2)}) copy-start(f32[512]{0:T(512)} %copy-done.84) | copy-start | bytes 6148
  435.6 75.8 %copy-start.32 = (bf16[512,384]{1,0:T(8,128)(2,1)S(1)}, bf16[512,384]{1,0:T(8,128)(2,1)}, u32[]{:S(2)}) copy-start(bf16[512,384]{1,0:T(8,128)(2,1)} %param.41) | copy-start | bytes 1179652
  (78 other events, 337.8 us)
Sparse Core Ops, SparseCore 0:
  9.6 22.3 all-gather.3
  33.5 19.5 all-gather.5
  364.7 34.0 all-reduce.15
  401.1 28.1 reduce-scatter.6
  431.7 27.9 reduce-scatter.8
  465.9 485.0 all-reduce.17
where the time goes:
time: 976 us; the launch traced here: 970 us
  waiting for transfers between devices  598 us (61%)
  matrix products  103 us (11%)
  other arithmetic  70.6 us (7%)
  local copies, waits for them, and re-layouts  69.3 us (7%)
  blocking collectives  64.6 us (7%)
  starting transfers between devices  48.9 us (5%)
  between operations  15.6 us (2%)
    psum x1, waiting for transfers between devices, local(): lax.psum((delta_norm_gain, delta_gate_weight, delta_value_weight, delta_s...  437 us
    ppermute x16, waiting for transfers between devices, shifted(): lax.ppermute(value, axis, [(source, source + steps) for source in range(l...  120 us
    ppermute x16, starting transfers between devices, shifted(): lax.ppermute(value, axis, [(source, source + steps) for source in range(l...  48.4 us
    psum x1, blocking collectives, local(): lax.psum((delta_norm_gain, delta_gate_weight, delta_value_weight, delta_s...  40.6 us
    unnamed x214, local copies, waits for them, and re-layouts  27.4 us
    dot_general x3, matrix products, span_outputs(): result = jnp.einsum('cijh,cjhp->cihp', mixing, values, precision=HIGH)  26 us
    unnamed x8, waiting for transfers between devices  19.9 us
  transfers between devices with their start and end apart: 22, of which 19 were waited for; matrix products, arithmetic and copies ran while one was open for 15% of the time, Pallas kernels for 0%

commit v1 on v0

--- a/solution.py
+++ b/solution.py
@@ -1,6 +1,10 @@
+import functools
+
 import jax
 import jax.numpy as jnp
 from jax import lax
+from jax.experimental import pallas as pl
+from jax.experimental.pallas import tpu as pltpu
 from jax.sharding import PartitionSpec as P
 
 D = 1536
@@ -11,6 +15,214 @@
 
 EPS = 1e-05
 HIGH = lax.Precision.HIGHEST
+
+
+MESH = pl.DeviceIdType.MESH
+LINE = 4
+
+
+def sum_rows(jobs, lines, count_in, *refs):
+    ins, outs = refs[:count_in], refs[count_in : 2 * count_in]
+    scratch = refs[2 * count_in :]
+    count = len(jobs)
+    own, y_in, z_in, final = (scratch[k * count : (k + 1) * count] for k in range(4))
+    (own_sem, ys, yr, zs, zr, gzs, gzr, gys, gyr, keep_sem) = scratch[4 * count :]
+    seq = lax.axis_index("seq")
+    z, y = seq // lines, seq % lines
+    barrier = pltpu.get_barrier_semaphore()
+
+    def at(zz, yy):
+        return {"seq": zz * lines + yy}
+
+    peers = [at(z, lax.rem(y + d, lines)) for d in range(1, lines)]
+    peers += [at(lax.rem(z + d, LINE), y) for d in range(1, LINE)]
+    for peer in peers:
+        pl.semaphore_signal(barrier, inc=1, device_id=peer, device_id_type=MESH)
+    pl.semaphore_wait(barrier, len(peers))
+
+    def remote(src, dst, send, recv, peer):
+        return pltpu.make_async_remote_copy(
+            src_ref=src, dst_ref=dst, send_sem=send, recv_sem=recv, device_id=peer, device_id_type=MESH
+        )
+
+    sizes = []
+    for which, start, rows in jobs:
+        sizes.append((which, start, rows, rows // lines, rows // lines // LINE))
+
+    def y_copies(j):
+        which, start, rows, part, piece = sizes[j]
+        copies = []
+        for d in range(1, lines):
+            to = lax.rem(y + d, lines)
+            copies.append(
+                remote(
+                    ins[which].at[pl.ds(start + to * part, part)],
+                    y_in[j].at[d - 1],
+                    ys.at[j, d - 1],
+                    yr.at[j, d - 1],
+                    at(z, to),
+                )
+            )
+        return copies
+
+    def own_copy(j):
+        which, start, rows, part, piece = sizes[j]
+        return pltpu.make_async_copy(
+            ins[which].at[pl.ds(start + y * part, part)], own[j], own_sem.at[j]
+        )
+
+    def z_copies(j):
+        piece = sizes[j][4]
+        copies = []
+        for d in (1, LINE - 1, 2):
+            to = lax.rem(z + d, LINE)
+            copies.append(
+                remote(
+                    own[j].at[pl.ds(to * piece, piece)],
+                    z_in[j].at[d - 1],
+                    zs.at[j, d - 1],
+                    zr.at[j, d - 1],
+                    at(to, y),
+                )
+            )
+        return copies
+
+    def place(j, zz, yy):
+        which, start, rows, part, piece = sizes[j]
+        return outs[which].at[pl.ds(start + yy * part + zz * piece, piece)]
+
+    def gather_z(j):
+        return [
+            remote(final[j], place(j, z, y), gzs.at[j, d - 1], gzr.at[j, d - 1], at(lax.rem(z + d, LINE), y))
+            for d in (1, LINE - 1, 2)
+        ]
+
+    def gather_y(j, d):
+        source = lax.rem(z + LINE - d, LINE)
+        src = final[j] if d == 0 else place(j, source, y)
+        return [
+            remote(
+                src,
+                place(j, source, y),
+                gys.at[j, d, e - 1],
+                gyr.at[j, d, e - 1],
+                at(z, lax.rem(y + e, lines)),
+            )
+            for e in range(1, lines)
+        ]
+
+    def keep(j):
+        return pltpu.make_async_copy(final[j], place(j, z, y), keep_sem.at[j])
+
+    for j in range(count):
+        own_copy(j).start()
+        for copy in y_copies(j):
+            copy.start()
+
+    def reduce_y(j):
+        own_copy(j).wait()
+        for copy in y_copies(j):
+            copy.wait_recv()
+        part = sizes[j][3]
+        tile = 16 if part % 16 == 0 else 8
+
+        def step(i, carry):
+            rows = pl.ds(pl.multiple_of(i * tile, tile), tile)
+            total = own[j][rows].astype(jnp.float32)
+            for d in range(lines - 1):
+                total = total + y_in[j][d, rows].astype(jnp.float32)
+            own[j][rows] = total.astype(jnp.bfloat16)
+            return carry
+
+        lax.fori_loop(0, part // tile, step, 0)
+        for copy in z_copies(j):
+            copy.start()
+
+    def reduce_z(j):
+        for copy in z_copies(j):
+            copy.wait_recv()
+        piece = sizes[j][4]
+        tile = 16 if piece % 16 == 0 else 8
+        base = z * piece
+
+        def step(i, carry):
+            rows = pl.ds(pl.multiple_of(i * tile, tile), tile)
+            mine = pl.ds(pl.multiple_of(base + i * tile, tile), tile)
+            total = own[j][mine].astype(jnp.float32)
+            for d in range(LINE - 1):
+                total = total + z_in[j][d, rows].astype(jnp.float32)
+            final[j][rows] = total.astype(jnp.bfloat16)
+            return carry
+
+        lax.fori_loop(0, piece // tile, step, 0)
+        keep(j).start()
+        for copy in gather_z(j):
+            copy.start()
+        for copy in gather_y(j, 0):
+            copy.start()
+
+    def forward(j):
+        copies = dict(zip((1, LINE - 1, 2), gather_z(j)))
+        for d in (1, LINE - 1, 2):
+            copies[d].wait_recv()
+            for copy in gather_y(j, d):
+                copy.start()
+
+    for i in range(count + 2):
+        if i < count:
+            reduce_y(i)
+        if 0 <= i - 1 < count:
+            reduce_z(i - 1)
+        if 0 <= i - 2 < count:
+            forward(i - 2)
+    for j in range(count):
+        keep(j).wait()
+        for copy in y_copies(j) + z_copies(j) + gather_z(j):
+            copy.wait_send()
+        for d in range(LINE):
+            for copy in gather_y(j, d):
+                copy.wait_recv()
+                copy.wait_send()
+
+
+def sum_over_seq(arrays, lines, split, collective_id):
+    jobs = []
+    for which, (array, parts) in enumerate(zip(arrays, split)):
+        rows = array.shape[0] // parts
+        jobs += [(which, k * rows, rows) for k in range(parts)]
+    count = len(jobs)
+    widths = [arrays[job[0]].shape[1] for job in jobs]
+    bf16 = jnp.bfloat16
+    scratch = [pltpu.VMEM((job[2] // lines, w), bf16) for job, w in zip(jobs, widths)]
+    scratch += [pltpu.VMEM((lines - 1, job[2] // lines, w), bf16) for job, w in zip(jobs, widths)]
+    scratch += [
+        pltpu.VMEM((LINE - 1, job[2] // lines // LINE, w), bf16) for job, w in zip(jobs, widths)
+    ]
+    scratch += [pltpu.VMEM((job[2] // lines // LINE, w), bf16) for job, w in zip(jobs, widths)]
+    dma = pltpu.SemaphoreType.DMA
+    scratch += [
+        dma((count,)),
+        dma((count, lines - 1)),
+        dma((count, lines - 1)),
+        dma((count, LINE - 1)),
+        dma((count, LINE - 1)),
+        dma((count, LINE - 1)),
+        dma((count, LINE - 1)),
+        dma((count, LINE, lines - 1)),
+        dma((count, LINE, lines - 1)),
+        dma((count,)),
+    ]
+    anywhere = pl.BlockSpec(memory_space=pl.ANY)
+    return pl.pallas_call(
+        functools.partial(sum_rows, jobs, lines, len(arrays)),
+        out_shape=[jax.ShapeDtypeStruct(array.shape, bf16) for array in arrays],
+        in_specs=[anywhere] * len(arrays),
+        out_specs=[anywhere] * len(arrays),
+        scratch_shapes=scratch,
+        compiler_params=pltpu.CompilerParams(
+            collective_id=collective_id, has_side_effects=True, vmem_limit_bytes=60 * 1024 * 1024
+        ),
+    )(*arrays)
 
 
 def shifted(value, axis, steps):
@@ -83,11 +295,21 @@
 
 
 def carry_chain(factors, pushed, direction):
-
-    def relay_turn(counter, incoming):
-        return shifted(factors[:, None, None] * incoming + pushed, "seq", direction)
-
-    return lax.fori_loop(0, lax.axis_size("seq") - 1, relay_turn, jnp.zeros_like(pushed))
+    count = lax.axis_size("seq")
+    window = count // 2
+    factor, total, width = factors, pushed, 1
+    while width < window // 2:
+        from_far, factor_far = (
+            shifted(total, "seq", direction * width),
+            shifted(factor, "seq", direction * width),
+        )
+        total = total + factor[:, None, None] * from_far
+        factor = factor * factor_far
+        width *= 2
+    near = shifted(total, "seq", direction)
+    near_factor = shifted(factor, "seq", direction)
+    far = shifted(total, "seq", direction * (1 + width))
+    return near + near_factor[:, None, None] * far
 
 
 def contract_rows(left, right):
@@ -201,7 +423,13 @@
     ).reshape(tokens_dev, inner_dev)
     gate_act = jax.nn.silu(gate_in)
     gated = mixer * gate_act
-    square_sum = lax.psum(jnp.sum(gated * gated, axis=1), "head")
+    cot_full = lax.all_gather(cotangent, "head", axis=1, tiled=True)
+    d_mix = contract_cols(cot_full, out_weight)
+    weighted_mix = d_mix * mix_gain[None, :]
+    row_sums = lax.psum(
+        jnp.stack([jnp.sum(gated * gated, axis=1), jnp.sum(weighted_mix * gated, axis=1)]), "head"
+    )
+    square_sum, mix_dot = row_sums[0], row_sums[1]
     scale_mix = lax.rsqrt(square_sum / INNER + EPS)[:, None]
     mix_out = (gated * scale_mix * mix_gain[None, :]).astype(jnp.bfloat16)
     partial_out = jnp.dot(mix_out, out_weight, preferred_element_type=jnp.float32)
@@ -210,12 +438,11 @@
     ).astype(jnp.float32)
     own_rows = hidden_in.astype(jnp.float32)
     block_out = (own_rows + mixed_sum).astype(jnp.bfloat16)
-    cot_full = lax.all_gather(cotangent, "head", axis=1, tiled=True)
-    delta_out_weight = contract_rows(mix_out, cot_full)
-    d_mix = contract_cols(cot_full, out_weight)
+    half = cot_full.shape[1] // 2
+    out_part = jnp.concatenate(
+        [contract_rows(mix_out, cot_full[:, :half]), contract_rows(mix_out, cot_full[:, half:])]
+    ).astype(jnp.bfloat16)
     delta_mix_gain = jnp.sum(d_mix * gated * scale_mix, axis=0)
-    weighted_mix = d_mix * mix_gain[None, :]
-    mix_dot = lax.psum(jnp.sum(weighted_mix * gated, axis=1), "head")
     d_gated = scale_mix * weighted_mix - gated * scale_mix**3 * (mix_dot / INNER)[:, None]
     d_mixer = d_gated * gate_act
     sigmoid_gate = jax.nn.sigmoid(gate_in)
@@ -254,9 +481,10 @@
     d_value = d_mixed[:, :inner_dev].astype(jnp.bfloat16)
     d_state = d_mixed[:, inner_dev:].astype(jnp.bfloat16)
     d_step_raw = d_step_in.astype(jnp.bfloat16)
-    delta_gate_weight = contract_rows(normed, d_gate)
-    delta_value_weight = contract_rows(normed, d_value)
-    delta_state_weight = contract_rows(normed, d_state)
+    gate_part = contract_rows(normed, d_gate).astype(jnp.bfloat16)
+    value_part = contract_rows(normed, d_value).astype(jnp.bfloat16)
+    own_columns = lax.dynamic_slice_in_dim(normed, lax.axis_index("head") * width_dev, width_dev, 1)
+    state_part_sum = contract_rows(own_columns, d_state)
     delta_step_weight = contract_rows(normed, d_step_raw)
     d_normed_part = (
         contract_cols(d_gate, gate_weight)
@@ -279,42 +507,55 @@
         + scale_in * weighted_in
         - own_rows * scale_in**3 * (input_dot / D)[:, None]
     )
-    summed = lax.psum(
-        (
-            delta_norm_gain,
-            delta_gate_weight,
-            delta_value_weight,
-            delta_step_weight,
-            delta_state_weight,
-            d_filters[:, :inner_dev],
-            d_offsets[:inner_dev],
-            d_filters[:, inner_dev:],
-            d_offsets[inner_dev:],
-            delta_step_bias,
-            delta_decay_log,
-            delta_skip_gain,
-            delta_mix_gain,
-            delta_out_weight,
-        ),
-        "seq",
-    )
+    small = (
+        delta_norm_gain,
+        delta_step_weight,
+        d_filters,
+        d_offsets,
+        delta_step_bias,
+        delta_decay_log,
+        delta_skip_gain,
+        delta_mix_gain,
+    )
+    packed = jnp.concatenate([jnp.reshape(part, (-1,)) for part in small])
+    state_rows_packed = state_part_sum.size // inner_dev
+    packed = jnp.pad(packed, (0, state_part_sum.size - packed.size))
+    extra = jnp.concatenate(
+        [state_part_sum.reshape(-1, inner_dev), packed.reshape(-1, inner_dev)]
+    ).astype(jnp.bfloat16)
+    lines = lax.axis_size("seq") // LINE
+    extra, out_sum, gate_sum, value_sum = sum_over_seq(
+        [extra, out_part, gate_part, value_part], lines, (1, 3, 3, 3), 3
+    )
+    delta_state_weight = lax.all_gather(
+        extra[:state_rows_packed].reshape(width_dev, -1), "head", axis=0, tiled=True
+    ).astype(jnp.float32)
+    packed = extra[state_rows_packed:].reshape(-1).astype(jnp.float32)
+    delta_out_weight = jnp.concatenate(jnp.split(out_sum, 2, axis=0), axis=1).astype(jnp.float32)
+    delta_gate_weight = gate_sum.astype(jnp.float32)
+    delta_value_weight = value_sum.astype(jnp.float32)
+    pieces, start = [], 0
+    for part in small:
+        pieces.append(jnp.reshape(packed[start : start + part.size], part.shape))
+        start += part.size
+    norm_sum, step_sum, filter_sum, offset_sum, bias_sum, decay_sum, skip_sum, gain_sum = pieces
     return (
         block_out,
         delta_hidden,
-        summed[0],
-        summed[1],
-        summed[2],
-        summed[3],
-        summed[4],
-        summed[5],
-        summed[6],
-        summed[7],
-        summed[8],
-        summed[9],
-        summed[10],
-        summed[11],
-        summed[12],
-        summed[13],
+        norm_sum,
+        delta_gate_weight,
+        delta_value_weight,
+        step_sum,
+        delta_state_weight,
+        filter_sum[:, :inner_dev],
+        offset_sum[:inner_dev],
+        filter_sum[:, inner_dev:],
+        offset_sum[inner_dev:],
+        bias_sum,
+        decay_sum,
+        skip_sum,
+        gain_sum,
+        delta_out_weight,
     )
 
 

time: 976 us -> 581 us (0.60)
  waiting for transfers between devices: 598 us -> 80.6 us
  Pallas kernels: 0 us -> 182 us
  blocking collectives: 64.6 us -> 27.3 us
  matrix products: 103 us -> 84.5 us
  starting transfers between devices: 48.9 us -> 32.6 us
    psum x1 -> x0, waiting for transfers between devices: 437 us -> none  [local(): lax.psum((delta_norm_gain, delta_gate_weight, delta_value_weight, delta_s...]
    pallas_call x0 -> x1, Pallas kernels: none -> 182 us  [sum_over_seq(): pl.pallas_call(functools.partial(sum_rows, jobs, lines, len(arrays)), out...]
    ppermute x16 -> x12, waiting for transfers between devices: 120 us -> 25.2 us  [shifted(): lax.ppermute(value, axis, [(source, source + steps) for source in range(l...]
    psum x3 -> x1, blocking collectives: 52.3 us -> 7 us  [local(): lax.psum(jnp.stack([jnp.sum(gated * gated, axis=1), jnp.sum(weighted_mix...]
    ppermute x16 -> x12, starting transfers between devices: 48.4 us -> 32.2 us  [shifted(): lax.ppermute(value, axis, [(source, source + steps) for source in range(l...]
    unnamed x8 -> x7, waiting for transfers between devices: 19.9 us -> 31.7 us
    convert_element_type x0 -> x4, other arithmetic: none -> 11.1 us  [the longest x1 4.36 us: local(): delta_gate_weight = gate_sum.astype(jnp.float32)]
    unnamed x214 -> x221, local copies, waits for them, and re-layouts: 27.4 us -> 18.2 us
  transfers between devices with their start and end apart: 22 -> 17, of which waited for: 19 -> 8; matrix products, arithmetic and copies ran while one was open for 15% -> 32% of each run, Pallas kernels for 0% -> 0%
where the time goes in v1:
time: 581 us; the launch traced here: 571 us
  Pallas kernels  182 us (31%)
  matrix products  84.5 us (15%)
  waiting for transfers between devices  80.6 us (14%)
  other arithmetic  75.4 us (13%)
  local copies, waits for them, and re-layouts  72.8 us (13%)
  starting transfers between devices  32.6 us (6%)
  blocking collectives  27.3 us (5%)
  between operations  16 us (3%)
    pallas_call x1, Pallas kernels, sum_over_seq(): pl.pallas_call(functools.partial(sum_rows, jobs, lines, len(arrays)), out...  182 us
    ppermute x12, starting transfers between devices, shifted(): lax.ppermute(value, axis, [(source, source + steps) for source in range(l...  32.2 us
    unnamed x7, waiting for transfers between devices  31.7 us
    dot_general x3, matrix products, span_outputs(): result = jnp.einsum('cijh,cjhp->cihp', mixing, values, precision=HIGH)  25.5 us
    ppermute x12, waiting for transfers between devices, shifted(): lax.ppermute(value, axis, [(source, source + steps) for source in range(l...  25.2 us
    unnamed x221, local copies, waits for them, and re-layouts  18.2 us
    psum x1, waiting for transfers between devices, local(): d_shared = lax.psum(d_shared, 'head')  15.2 us
    dot_general x5, matrix products, contract_cols(): lax.dot_general(left, right, (((1,), (1,)), ((), ())), preferred_element_...  15.1 us
  transfers between devices with their start and end apart: 17, of which 8 were waited for; matrix products, arithmetic and copies ran while one was open for 32% of the time, Pallas kernels for 0%

profile of v1, /device:TPU:0, one launch (start us, length us, event | category | flops | bytes accessed | tf_op | source)
XLA Modules:
  0.0 570.9 jit_solution(5891030061701771182)
XLA Ops:
  12.2 6.1 %all-gather = bf16[4,1,384]{2,1,0:T(2,128)(2,1)S(1)} all-gather(bf16[1,1,384]{2,1,0:T(2,128)(2,1)S(1)} %reshape.388), channel_id=1, replica_groups=mesh['seq'=8,'head'=4] {'head'}, dimensions={0}, use_global_device_ids=true | all-gather | bytes 3840 | tf_op jit(solution)/shard_map/all_gather | solution.py:362
  23.4 8.5 %all-gather.4.cloned.1.call-done = bf16[512,1536]{1,0:T(8,128)(2,1)} async-done(((bf16[512,384]{1,0:T(8,128)(2,1)}), bf16[512,1536]{1,0:T(8,128)(2,1)}) %all-gather.4.cloned.1.call-update) | async-done | bytes 1572880 | tf_op jit(solution)/shard_map/all_gather | solution.py:361
  38.6 3.5 collective-permute-start
  48.4 2.8 fusion.44
  53.9 3.1 copy.185
  57.0 3.1 reshape.358
  60.0 3.8 fusion.55
  64.5 9.7 %while.40 = (s32[]{:T(128)}, f32[12,64,128]{2,1,0:T(8,128)S(1)}, f32[12]{0:T(128)}, f32[2,12,64,128]{3,2,1,0:T(8,128)S(1)}, f32[2,12]{1,0:T(2,128)}, /*index=5*/...) while((s32[]{:T(128)}, f32[12,64,128]{2,1,0:T(8,128)S(1)}, ...), condition=%wide.region_8.9_spmd.clone, body=%wide.region_7.8_spmd.clone.sunk | while | flops 393243 | bytes 1967629 | solution.py:273
  74.2 3.5 collective-permute-start.1
  77.8 4.8 fusion.131
  83.9 4.5 collective-permute-start.3
  88.6 4.3 collective-permute-start.2
  92.9 3.5 collective-permute-start.5
  97.6 4.2 collective-permute-start.4
  105.4 7.5 %bitcast_add_fusion.3 = f32[2,256,12,64]{1,3,2,0:T(8,128)S(1)} fusion(f32[2,256,12,64]{1,3,2,0:T(8,128)S(1)} %fusion.80, f32[2,256,12]{1,2,0:T(8,128)S(1)} %copy-done.75, f32[2,256,256]{2,1,0:T(8,128)S(1)} %fusion.130, f32[2,256,256]{2,1,0:T(8,128)S(1)} %copy-done.46, f32[2,256,12]{1,2,0:T(8,128)S(1)} %bitcast.233, pred[2,256,256]{2,1,0:T(8,128)(4,1)S(1)} %copy-done.62, ...), kind=kOutput, calls=%fused_computation.88 | convolution fusion | flops 1216610304 | bytes 5971968 | tf_op jit(solution)/shard_map/jvp(cijh,cjhp->cihp)/dot_general | solution.py:289
  115.4 3.0 copy.194
  118.5 6.0 %multiply_reduce_fusion.10 = (f32[512]{0:T(512)S(1)}, f32[512]{0:T(512)S(1)}, f32[512,768]{1,0:T(8,128)}, f32[512,768]{1,0:T(8,128)}) fusion(f32[768]{0:T(1024)} %param.34, f32[512,768]{1,0:T(8,128)} %fusion.131, f32[512,768]{1,0:T(8,128)} %copy.194, f32[512,1024]{1,0:T(8,128)} %copy-done.13, f32[768]{0:T(1024)S(1)} %mul.663, ...), kind=kOutput, calls=%fused_computation.98 | convolution fusion | flops 1212677120 | bytes 11806720 | tf_op jit(solution)/shard_map/dot_general | solution.py:322
  125.1 7.0 %psum.21 = f32[2,512]{1,0:T(2,128)} all-reduce(f32[2,512]{1,0:T(2,128)} %pad_maximum_fusion.6), channel_id=1, replica_groups=mesh['seq'=8,'head'=4] {'head'}, use_global_device_ids=true, to_apply=%region_11.12 | all-reduce | flops 1024 | bytes 8192 | tf_op jit(solution)/shard_map/psum | solution.py:429
  132.9 5.8 %multiply_reduce_fusion.7 = (f32[768]{0:T(1024)}, f32[512,768]{1,0:T(8,128)}, bf16[512,768]{1,0:T(8,128)(2,1)}, bf16[768]{0:T(1024)(128)(2,1)}, bf16[512,768]{1,0:T(8,128)(2,1)}) fusion(f32[512,1024]{1,0:T(8,128)} %copy-done.13, f32[512,768]{1,0:T(8,128)} %fusion.131, f32[512]{0:T(512)S(1)} %bitcast.262, f32[512,768]{1,0:T(8,128)} %get-tuple-element.464, ...), kind=kLoop, calls=%fused_computation.91 | loop fusion | flops 10615296 | bytes 11026944 | tf_op jit(solution)/shard_map/reduce_sum | solution.py:453
  138.8 3.0 copy.195
  141.8 3.1 reshape_reshape.4
  144.8 4.7 multiply_reduce_fusion.11
  151.3 11.3 %fusion.22 = (f32[2,256,12]{1,2,0:T(8,128)S(1)}, f32[2,256,12]{1,2,0:T(8,128)S(1)}, f32[2,256,12]{1,2,0:T(8,128)}, f32[2,256,256]{2,1,0:T(8,128)}) fusion(f32[2,256,12]{1,2,0:T(8,128)S(1)} %copy-done.76, f32[2,256,256]{2,1,0:T(8,128)S(1)} %copy-done.50, f32[2,256,256]{2,1,0:T(8,128)S(1)} %copy-done.47, f32[2,256,12]{1,2,0:T(8,128)S(1)} %bitcast.234, ...), kind=kOutput, calls=%fused_computation.42 | convolution fusion | flops 1231403008 | bytes 4972544 | tf_op jit(solution)/shard_map/transpose(jvp(cijh,cjhp->cihp))/dot_general | solution.py:289
  167.2 6.2 %reduce-window.29 = f32[2,12,2,128]{3,1,2,0:T(8,128)} reduce-window(f32[2,12,2,128]{3,1,2,0:T(8,128)} %copy.207, f32[]{:T(128)} %constant.119.clone.1), window={size=1x1x1x128 pad=0_0x0_0x0_0x0_127}, to_apply=%region_25.26 | reduce-window | flops 780288 | bytes 49156 | tf_op jit(solution)/shard_map/reduce-window.3
  177.4 3.7 convolution_convert_fusion.2
  181.1 2.7 copy.235
  187.9 3.5 fusion.63
  192.8 9.7 %collective-permute-done.7 = f32[12,64,128]{2,1,0:T(8,128)S(1)} collective-permute-done((f32[12,64,128]{2,1,0:T(8,128)S(1)}, f32[12,64,128]{2,1,0:T(8,128)S(1)}, u32[]{:S(2)}, u32[]{:S(2)}) %collective-permute-start.7) | collective-permute-done | bytes 393248 | tf_op jit(solution)/shard_map/ppermute | solution.py:231
  202.5 11.3 %collective-permute-done.10 = f32[12,64,128]{2,1,0:T(8,128)S(1)} collective-permute-done((f32[12,64,128]{2,1,0:T(8,128)S(1)}, f32[12,64,128]{2,1,0:T(8,128)S(1)}, u32[]{:S(2)}, u32[]{:S(2)}) %collective-permute-start.10) | collective-permute-done | bytes 393248 | tf_op jit(solution)/shard_map/ppermute | solution.py:231
  215.6 5.5 while.39
  221.2 4.3 fusion.64
  227.6 4.8 fusion.132
  235.0 6.7 %bitcast_add_fusion.2 = f32[2,256,12,64]{1,3,2,0:T(8,128)} fusion(f32[2,256,12,64]{1,3,2,0:T(8,128)S(1)} %fusion.133, f32[2,256,12]{1,2,0:T(8,128)S(1)} %copy-done.77, f32[2,256,256]{2,1,0:T(8,128)S(1)} %copy-done.51, f32[2,256,256]{2,1,0:T(8,128)S(1)} %copy-done.48, f32[2,256,12]{1,2,0:T(8,128)S(1)} %bitcast.235, pred[2,256,256]{2,1,0:T(8,128)(4,1)S(1)} %copy-done.64, ...), kind=kOutput, calls=%fused_computation.87 | convolution fusion | flops 1216610304 | bytes 5971968 | tf_op jit(solution)/shard_map/transpose(jvp(cijh,cjhp->cihp))/dot_general | solution.py:289
  244.0 5.0 reduce-window.31
  253.5 3.0 copy.199
  256.5 3.4 multiply_add_fusion.1
  259.9 15.2 %all-reduce.14.cloned.1.call-done = f32[512,256]{1,0:T(8,128)} async-done(((f32[512,256]{1,0:T(8,128)}), f32[512,256]{1,0:T(8,128)}) %all-reduce.14.cloned.1.call-update) | async-done | bytes 524304 | tf_op jit(solution)/shard_map/psum | solution.py:469
  275.2 3.9 multiply_reduce_fusion.3
  282.5 4.1 collective-permute-done.11
  297.1 2.8 convolution_convert_fusion.1.refs_2_
  301.7 2.8 convolution_convert_fusion.refs_3_
  307.7 29.1 %reduce-scatter.9.cloned.1.call-done = bf16[384,512]{1,0:T(8,128)(2,1)} async-done(((bf16[1536,512]{1,0:T(8,128)(2,1)}), bf16[384,512]{1,0:T(8,128)(2,1)}) %reduce-scatter.9.cloned.1.call-update) | async-done | bytes 393232
  341.3 181.7 %shard_map.288 = (bf16[256,768]{1,0:T(8,128)(2,1)}, bf16[1536,768]{1,0:T(8,128)(2,1)}, bf16[1536,768]{1,0:T(8,128)(2,1)}, bf16[1536,768]{1,0:T(8,128)(2,1)}) custom-call(bf16[256,768]{1,0:T(8,128)(2,1)} %pad_maximum_fusion.4.refs_0_, bf16[1536,768]{1,0:T(8,128)(2,1)} %pad_maximum_fusion.1.refs_1_, bf16[1536,768]{1,0:T(8,128)(2,1)} %convolution_convert_fusion.1.refs_2_, ...), custom_call_target="tpu_custom_call" | custom-call | tf_op jit(solution)/shard_map/pallas_call | solution.py:216
  527.7 6.1 %psum.23 = f32[512]{0:T(512)S(1)} all-reduce(f32[512]{0:T(512)S(1)} %get-tuple-element.414), channel_id=1, replica_groups=mesh['seq'=8,'head'=4] {'head'}, use_global_device_ids=true, to_apply=%region_32.33 | all-reduce | flops 512 | bytes 4096 | tf_op jit(solution)/shard_map/psum | solution.py:504
  533.8 4.4 convert_element_type.156
  540.8 5.7 convert_element_type.158
  548.5 8.0 %all_gather.15 = bf16[1536,256]{1,0:T(8,128)(2,1)S(1)} all-gather(bf16[384,256]{1,0:T(8,128)(2,1)S(1)} %reshape.384), channel_id=1, replica_groups=mesh['seq'=8,'head'=4] {'head'}, dimensions={0}, use_global_device_ids=true | all-gather | bytes 983040 | tf_op jit(solution)/shard_map/all_gather | solution.py:530
  559.6 2.9 maximum_convert_fusion
  (410 shorter events, 116.4 us)
Async XLA Ops:
  7.2 111.3 %copy-start = (bf16[768,1536]{1,0:T(8,128)(2,1)S(1)}, bf16[768,1536]{1,0:T(8,128)(2,1)}, u32[]{:S(2)}) copy-start(bf16[768,1536]{1,0:T(8,128)(2,1)} %param.35) | copy-start | bytes 7077892
  7.2 24.7 %all-gather.4.cloned.1.call-start = ((), (), s32[]{:S(2)}) async-start(), calls=%async_computation.2 | async-start | bytes 1966080 | tf_op jit(solution)/shard_map/all_gather | solution.py:361
  7.9 110.5 %all-gather.6.cloned.1.call-start = ((), (), s32[]{:S(2)}) async-start(), calls=%async_computation.3 | async-start | bytes 1966080 | tf_op jit(solution)/shard_map/all_gather | solution.py:426
  8.7 266.5 %all-reduce.14.cloned.1.call-start = ((), (), s32[]{:S(2)}) async-start(), calls=%async_computation.4 | async-start | bytes 1048576 | tf_op jit(solution)/shard_map/psum | solution.py:469
  11.3 34.5 %copy-start.96 = (f32[2]{0:T(128)}, f32[2]{0:T(128)S(1)}, u32[]{:S(2)}) copy-start(f32[2]{0:T(128)S(1)} %fusion.107) | copy-start | bytes 28
  18.7 29.6 %copy-start.79 = (f32[512]{0:T(512)}, f32[512]{0:T(512)S(1)}, u32[]{:S(2)}) copy-start(f32[512]{0:T(512)S(1)} %get-tuple-element.507) | copy-start | bytes 6148
  18.7 29.6 %copy-start.81 = (f32[512]{0:T(512)}, f32[512]{0:T(512)S(1)}, u32[]{:S(2)}) copy-start(f32[512]{0:T(512)S(1)} %get-tuple-element.508) | copy-start | bytes 6148
  18.7 29.6 %copy-start.83 = (f32[512]{0:T(512)}, f32[512]{0:T(512)S(1)}, u32[]{:S(2)}) copy-start(f32[512]{0:T(512)S(1)} %get-tuple-element.509) | copy-start | bytes 6148
  20.1 28.2 %copy-start.65 = (f32[1,1024]{1,0:T(1,128)}, f32[1,1024]{1,0:T(1,128)S(1)}, u32[]{:S(2)}) copy-start(f32[1,1024]{1,0:T(1,128)S(1)} %get-tuple-element.505) | copy-start | bytes 12292
  20.2 28.2 %copy-start.67 = (f32[1,1024]{1,0:T(1,128)}, f32[1,1024]{1,0:T(1,128)S(1)}, u32[]{:S(2)}) copy-start(f32[1,1024]{1,0:T(1,128)S(1)} %get-tuple-element.506) | copy-start | bytes 12292
  20.8 21.3 %copy-start.99 = (f32[12]{0:T(128)}, f32[12]{0:T(128)S(1)}, u32[]{:S(2)}) copy-start(f32[12]{0:T(128)S(1)} %exponential_negate_fusion) | copy-start | bytes 148
  23.4 21.7 %copy-start.72 = (f32[2,256]{1,0:T(2,128)}, f32[2,256]{1,0:T(2,128)S(1)}, u32[]{:S(2)}) copy-start(f32[2,256]{1,0:T(2,128)S(1)} %get-tuple-element.515) | copy-start | bytes 6148
  23.4 21.7 %copy-start.87 = (f32[2,256]{1,0:T(2,128)}, f32[2,256]{1,0:T(2,128)S(1)}, u32[]{:S(2)}) copy-start(f32[2,256]{1,0:T(2,128)S(1)} %get-tuple-element.514) | copy-start | bytes 6148
  37.2 11.2 %copy-start.14 = (f32[512,256]{1,0:T(8,128)}, f32[512,256]{1,0:T(8,128)S(1)}, u32[]{:S(2)}) copy-start(f32[512,256]{1,0:T(8,128)S(1)} %fusion.129) | copy-start | bytes 1572868
  38.6 7.8 %collective-permute-start = (f32[3,1024]{1,0:T(4,128)S(1)}, f32[3,1024]{1,0:T(4,128)S(1)}, u32[]{:S(2)}, u32[]{:S(2)}) collective-permute-start(f32[3,1024]{1,0:T(4,128)S(1)} %fusion.98), channel_id=1, source_target_pairs={{0,4},{4,8},{8,12},{12,16},{16,20},{20,24},{24,28},{1,5},{5,9},{9,... | collective-permute-start | bytes 36872 | tf_op jit(solution)/shard_map/ppermute | solution.py:231
  45.8 14.3 %copy-start.56 = (f32[2,256,12]{1,2,0:T(8,128)}, f32[2,256,12]{1,2,0:T(8,128)S(1)}, u32[]{:S(2)}) copy-start(f32[2,256,12]{1,2,0:T(8,128)S(1)} %get-tuple-element.499) | copy-start | bytes 73732
  74.2 8.3 %copy-start.74 = (f32[12]{0:T(128)S(1)}, f32[12]{0:T(128)}, u32[]{:S(2)}) copy-start(f32[12]{0:T(128)} %get-tuple-element.287) | copy-start | bytes 148
  74.2 22.2 %copy-start.18 = (f32[512,128]{1,0:T(8,128)S(1)}, f32[512,128]{1,0:T(8,128)}, u32[]{:S(2)}) copy-start(f32[512,128]{1,0:T(8,128)} %copy-done.17) | copy-start | bytes 786436
  74.2 22.2 %copy-start.21 = (f32[512,128]{1,0:T(8,128)S(1)}, f32[512,128]{1,0:T(8,128)}, u32[]{:S(2)}) copy-start(f32[512,128]{1,0:T(8,128)} %get-tuple-element.481) | copy-start | bytes 786436
  74.2 14.3 %collective-permute-start.1 = (f32[12,64,128]{2,1,0:T(8,128)S(1)}, f32[12,64,128]{2,1,0:T(8,128)S(1)}, u32[]{:S(2)}, u32[]{:S(2)}) collective-permute-start(f32[12,64,128]{2,1,0:T(8,128)S(1)} %get-tuple-element.286), channel_id=1, source_target_pairs={{0,4},{4,8},{8,12},{12,16},{16,20},{20,24},{24,28},{1,5},{5,9},{9,... | collective-permute-start | bytes 1179656 | tf_op jit(solution)/shard_map/ppermute | solution.py:231
  82.5 21.3 %copy-start.85 = (f32[2,12]{1,0:T(2,128)S(1)}, f32[2,12]{1,0:T(2,128)}, u32[]{:S(2)}) copy-start(f32[2,12]{1,0:T(2,128)} %get-tuple-element.696) | copy-start | bytes 292
  82.5 14.5 %collective-permute-start.8 = (f32[12]{0:T(128)S(1)}, f32[12]{0:T(128)S(1)}, u32[]{:S(2)}, u32[]{:S(2)}) collective-permute-start(f32[12]{0:T(128)S(1)} %copy-done.74), channel_id=1, source_target_pairs={{4,0},{8,4},{12,8},{16,12},{20,16},{24,20},{28,24},{5,1},{9,5},{13... | collective-permute-start | bytes 152 | tf_op jit(solution)/shard_map/ppermute | solution.py:231
  83.9 13.1 %collective-permute-start.3 = (f32[12]{0:T(128)S(1)}, f32[12]{0:T(128)S(1)}, u32[]{:S(2)}, u32[]{:S(2)}) collective-permute-start(f32[12]{0:T(128)S(1)} %copy-done.74), channel_id=1, source_target_pairs={{0,4},{4,8},{8,12},{12,16},{16,20},{20,24},{24,28},{1,5},{5,9},{9,... | collective-permute-start | bytes 152 | tf_op jit(solution)/shard_map/ppermute | solution.py:231
  88.6 14.9 %collective-permute-start.2 = (f32[12,64,128]{2,1,0:T(8,128)S(1)}, f32[12,64,128]{2,1,0:T(8,128)S(1)}, u32[]{:S(2)}, u32[]{:S(2)}) collective-permute-start(f32[12,64,128]{2,1,0:T(8,128)S(1)} %multiply_add_fusion.9), channel_id=1, source_target_pairs={{0,4},{4,8},{8,12},{12,16},{16,20},{20,24},{24,28},{1,5},{5,9},{9,... | collective-permute-start | bytes 1179656 | tf_op jit(solution)/shard_map/ppermute | solution.py:231
  92.9 10.8 %collective-permute-start.5 = (f32[12,64,128]{2,1,0:T(8,128)S(1)}, f32[12,64,128]{2,1,0:T(8,128)S(1)}, u32[]{:S(2)}, u32[]{:S(2)}) collective-permute-start(f32[12,64,128]{2,1,0:T(8,128)S(1)} %multiply_add_fusion.9), channel_id=1, source_target_pairs={{0,12},{4,16},{8,20},{12,24},{16,28},{1,13},{5,17},{9,21},{13,25},... | collective-permute-start | bytes 1179656 | tf_op jit(solution)/shard_map/ppermute | solution.py:231
  97.0 8.3 %copy-start.49 = (f32[2,256,256]{2,1,0:T(8,128)}, f32[2,256,256]{2,1,0:T(8,128)S(1)}, u32[]{:S(2)}) copy-start(f32[2,256,256]{2,1,0:T(8,128)S(1)} %fusion.130) | copy-start | bytes 1572868
  97.6 5.9 %collective-permute-start.4 = (f32[12]{0:T(128)S(1)}, f32[12]{0:T(128)S(1)}, u32[]{:S(2)}, u32[]{:S(2)}) collective-permute-start(f32[12]{0:T(128)S(1)} %get-tuple-element.517), channel_id=1, source_target_pairs={{0,4},{4,8},{8,12},{12,16},{16,20},{20,24},{24,28},{1,5},{5,9},{9,... | collective-permute-start | bytes 152 | tf_op jit(solution)/shard_map/ppermute | solution.py:231
  101.9 90.9 %collective-permute-start.9 = (f32[12]{0:T(128)}, f32[12]{0:T(128)}, u32[]{:S(2)}, u32[]{:S(2)}) collective-permute-start(f32[12]{0:T(128)} %get-tuple-element.516), channel_id=1, source_target_pairs={{4,0},{8,4},{12,8},{16,12},{20,16},{24,20},{28,24},{5,1},{9,5},{13... | collective-permute-start | bytes 152 | tf_op jit(solution)/shard_map/ppermute | solution.py:231
  105.3 7.6 %copy-start.24 = (f32[2,256,12,64]{1,3,2,0:T(8,128)}, f32[2,256,12,64]{1,3,2,0:T(8,128)S(1)}, u32[]{:S(2)}) copy-start(f32[2,256,12,64]{1,3,2,0:T(8,128)S(1)} %fusion.80) | copy-start | bytes 4718596
  151.3 12.6 %copy-start.88 = (f32[2,256]{1,0:T(2,128)S(1)}, f32[2,256]{1,0:T(2,128)}, u32[]{:S(2)}) copy-start(f32[2,256]{1,0:T(2,128)} %copy-done.87) | copy-start | bytes 6148
  162.6 21.3 %collective-permute-start.6 = (f32[12,64,128]{2,1,0:T(8,128)}, f32[12,64,128]{2,1,0:T(8,128)}, u32[]{:S(2)}, u32[]{:S(2)}) collective-permute-start(f32[12,64,128]{2,1,0:T(8,128)} %get-tuple-element.416), channel_id=1, source_target_pairs={{4,0},{8,4},{12,8},{16,12},{20,16},{24,20},{28,24},{5,1},{9,5},{13... | collective-permute-start | bytes 1179656 | tf_op jit(solution)/shard_map/ppermute | solution.py:231
  183.8 7.6 %copy-start.19 = (f32[512,128]{1,0:T(8,128)S(1)}, f32[512,128]{1,0:T(8,128)}, u32[]{:S(2)}) copy-start(f32[512,128]{1,0:T(8,128)} %copy-done.17) | copy-start | bytes 786436
  183.8 7.6 %copy-start.30 = (f32[2,256,256]{2,1,0:T(8,128)S(1)}, f32[2,256,256]{2,1,0:T(8,128)}, u32[]{:S(2)}) copy-start(f32[2,256,256]{2,1,0:T(8,128)} %get-tuple-element.405) | copy-start | bytes 1572868
  185.1 17.3 %collective-permute-start.7 = (f32[12,64,128]{2,1,0:T(8,128)S(1)}, f32[12,64,128]{2,1,0:T(8,128)S(1)}, u32[]{:S(2)}, u32[]{:S(2)}) collective-permute-start(f32[12,64,128]{2,1,0:T(8,128)S(1)} %multiply_add_fusion.7), channel_id=1, source_target_pairs={{4,0},{8,4},{12,8},{16,12},{20,16},{24,20},{28,24},{5,1},{9,5},{13... | collective-permute-start | bytes 1179656 | tf_op jit(solution)/shard_map/ppermute | solution.py:231
  186.4 27.3 %collective-permute-start.10 = (f32[12,64,128]{2,1,0:T(8,128)S(1)}, f32[12,64,128]{2,1,0:T(8,128)S(1)}, u32[]{:S(2)}, u32[]{:S(2)}) collective-permute-start(f32[12,64,128]{2,1,0:T(8,128)S(1)} %multiply_add_fusion.7), channel_id=1, source_target_pairs={{12,0},{16,4},{20,8},{24,12},{28,16},{13,1},{17,5},{21,9},{25,13},... | collective-permute-start | bytes 1179656 | tf_op jit(solution)/shard_map/ppermute | solution.py:231
  191.4 24.2 %copy-start.71 = (f32[2,12]{1,0:T(2,128)S(1)}, f32[2,12]{1,0:T(2,128)}, u32[]{:S(2)}) copy-start(f32[2,12]{1,0:T(2,128)} %get-tuple-element.755) | copy-start | bytes 292
  227.5 78.2 %reduce-scatter.7.cloned.1.call-start = ((), (), s32[]{:S(2)}) async-start(), calls=%async_computation.5 | async-start | bytes 1966080
  232.4 104.3 %reduce-scatter.9.cloned.1.call-start = ((), (), s32[]{:S(2)}) async-start(), calls=%async_computation.6 | async-start | bytes 1966080
  241.8 7.5 %copy-start.61 = (f32[512,12]{0,1:T(8,128)S(1)}, f32[512,12]{0,1:T(8,128)}, u32[]{:S(2)}) copy-start(f32[512,12]{0,1:T(8,128)} %get-tuple-element.518) | copy-start | bytes 73732
  256.5 18.7 %copy-start.3 = (f32[515,1024]{1,0:T(8,128)S(1)}, f32[515,1024]{1,0:T(8,128)}, u32[]{:S(2)}) copy-start(f32[515,1024]{1,0:T(8,128)} %copy-done.2) | copy-start | bytes 6328324
  256.5 18.7 %copy-start.15 = (f32[512,256]{1,0:T(8,128)S(1)}, f32[512,256]{1,0:T(8,128)}, u32[]{:S(2)}) copy-start(f32[512,256]{1,0:T(8,128)} %copy-done.14) | copy-start | bytes 1572868
  256.5 18.7 %copy-start.80 = (f32[512]{0:T(512)S(1)}, f32[512]{0:T(512)}, u32[]{:S(2)}) copy-start(f32[512]{0:T(512)} %copy-done.79) | copy-start | bytes 6148
  256.5 18.7 %copy-start.82 = (f32[512]{0:T(512)S(1)}, f32[512]{0:T(512)}, u32[]{:S(2)}) copy-start(f32[512]{0:T(512)} %copy-done.81) | copy-start | bytes 6148
  256.5 18.7 %copy-start.84 = (f32[512]{0:T(512)S(1)}, f32[512]{0:T(512)}, u32[]{:S(2)}) copy-start(f32[512]{0:T(512)} %copy-done.83) | copy-start | bytes 6148
  279.9 6.7 %collective-permute-start.11 = (f32[3,1024]{1,0:T(4,128)S(1)}, f32[3,1024]{1,0:T(4,128)S(1)}, u32[]{:S(2)}, u32[]{:S(2)}) collective-permute-start(f32[3,1024]{1,0:T(4,128)S(1)} %pad_add_fusion.1), channel_id=1, source_target_pairs={{4,0},{8,4},{12,8},{16,12},{20,16},{24,20},{28,24},{5,1},{9,5},{13... | collective-permute-start | bytes 36872 | tf_op jit(solution)/shard_map/ppermute | solution.py:231
  301.7 36.2 %copy-start.32 = (bf16[512,384]{1,0:T(8,128)(2,1)S(1)}, bf16[512,384]{1,0:T(8,128)(2,1)}, u32[]{:S(2)}) copy-start(bf16[512,384]{1,0:T(8,128)(2,1)} %param.21) | copy-start | bytes 1179652
  301.7 36.2 %copy-start.90 = (f32[512]{0:T(512)S(1)}, f32[512]{0:T(512)}, u32[]{:S(2)}) copy-start(f32[512]{0:T(512)} %copy-done.89) | copy-start | bytes 6148
  304.6 35.6 %copy-start.94 = (bf16[768]{0:T(1024)(128)(2,1)S(1)}, bf16[768]{0:T(1024)(128)(2,1)}, u32[]{:S(2)}) copy-start(bf16[768]{0:T(1024)(128)(2,1)} %get-tuple-element.473) | copy-start | bytes 4612
  (76 other events, 250.5 us)
Sparse Core Ops, SparseCore 0:
  9.6 22.3 all-gather.3
  33.5 19.6 all-gather.5
  227.6 47.4 all-reduce.13
  277.6 28.1 reduce-scatter.6
  308.7 27.9 reduce-scatter.8

commit v2 on v1

v2 whole, which is shorter than its diff:
```python
import functools

import jax
import jax.numpy as jnp
from jax import lax
from jax.experimental import pallas as pl
from jax.experimental.pallas import tpu as pltpu
from jax.sharding import PartitionSpec as P

MESH = pl.DeviceIdType.MESH
F32, BF16 = jnp.float32, jnp.bfloat16
HIGH = lax.Precision.HIGHEST
EPS = 1e-05
Q = 128
LANES = 128
HEAD = 64
SUB = 8
FAR = -1e30
LINE = 4


def gather_kernel(peers_head, flat, count_in, *refs):
    ins, outs = refs[:count_in], refs[count_in : 2 * count_in]
    local_sem, send, recv = refs[2 * count_in :]
    head = lax.axis_index("head")
    chips = peers_head // 2
    x, core = head // 2, lax.rem(head, 2)
    partner = {"head": x * 2 + (1 - core)}
    across = [{"head": lax.rem(x + d, chips) * 2 + core} for d in range(1, chips)]
    barrier = pltpu.get_barrier_semaphore()
    for peer in [partner] + across:
        pl.semaphore_signal(barrier, inc=1, device_id=peer, device_id_type=MESH)
    pl.semaphore_wait(barrier, chips)

    def place(k, who):
        if flat[k]:
            width = ins[k].shape[1]
            return outs[k].at[:, pl.ds(pl.multiple_of(who * width, width), width)]
        return outs[k].at[who]

    def remote(src, dst, k, slot, peer):
        return pltpu.make_async_remote_copy(
            src_ref=src, dst_ref=dst, send_sem=send.at[k, slot], recv_sem=recv.at[k, slot],
            device_id=peer, device_id_type=MESH,
        )

    def first(k):
        copies = [remote(ins[k], place(k, head), k, d, across[d - 1]) for d in range(1, chips)]
        return copies + [remote(ins[k], place(k, head), k, 0, partner)]

    def second(k, d):
        source = lax.rem(x + chips - d, chips) * 2 + core
        return remote(place(k, source), place(k, source), k, chips - 1 + d, partner)

    own = [pltpu.make_async_copy(ins[k], place(k, head), local_sem.at[k]) for k in range(count_in)]
    for k in range(count_in):
        for copy in first(k):
            copy.start()
        own[k].start()
    for k in range(count_in):
        for d in range(1, chips):
            first(k)[d - 1].wait_recv()
            second(k, d).start()
    for k in range(count_in):
        own[k].wait()
        for copy in first(k):
            copy.wait_send()
        first(k)[-1].wait_recv()
        for d in range(1, chips):
            second(k, d).wait()


def gather_heads(arrays, peers_head, collective_id):
    flat = [array.ndim == 2 and array.shape[1] % 128 == 0 for array in arrays]
    shapes = [
        (a.shape[0], a.shape[1] * peers_head) if f else (peers_head,) + a.shape
        for a, f in zip(arrays, flat)
    ]
    count, chips = len(arrays), peers_head // 2
    dma = pltpu.SemaphoreType.DMA
    anywhere = pl.BlockSpec(memory_space=pl.ANY)
    gathered = pl.pallas_call(
        functools.partial(gather_kernel, peers_head, flat, count),
        out_shape=[jax.ShapeDtypeStruct(s, a.dtype) for s, a in zip(shapes, arrays)],
        in_specs=[anywhere] * count,
        out_specs=[anywhere] * count,
        scratch_shapes=[dma((count,)), dma((count, 2 * chips - 1)), dma((count, 2 * chips - 1))],
        compiler_params=pltpu.CompilerParams(collective_id=collective_id, has_side_effects=True),
    )(*arrays)
    return [
        g if f else jnp.moveaxis(g, 0, 1).reshape(a.shape[0], -1)
        for g, a, f in zip(gathered, arrays, flat)
    ]


def mm(left, right, contract=((1,), (0,)), precision=None):
    return lax.dot_general(
        left, right, (contract, ((), ())), precision=precision, preferred_element_type=F32
    )


def split(value):
    high = value.astype(BF16)
    return high, (value - high.astype(F32)).astype(BF16)


def twice(value, axis):
    return jnp.concatenate([value, value], axis=axis)


def sigmoid(v):
    return 1.0 / (1.0 + jnp.exp(-v))


def mixer_kernel(
    count, peers_head, inner,
    lengths, v_in, s_in, g_in, t_in, d_mix, taps_v, taps_s, off_v, off_s, bias, rate, skip, gain,
    mix_out, d_gate, d_value, d_state, d_step, grads_v, grads_s, grads_h,
    edge_v, edge_s, first_v, first_s, val, inf, inf_low, rea, rea_low, slope_v, slope_s, segs, mask_f, mask_b,
    step, sig, logs, run, run_t, tail, into, passing, pair, scaled, scaled_low, out, inter, d_u,
    states, starts, starts_low, before, total, factors, push, got, kept, prefix, spread_sum,
    rows_out, rows_in, pre_v, pre_s, back_v, back_s, back_in_v, back_in_s,
    edge_sems, p_send, p_recv, carry_send, carry_recv, row_send, row_recv, back_sems,
):
    tokens, channels = v_in.shape
    chunks, pairs, heads = tokens // Q, channels // LANES, channels // HEAD
    seq, head = lax.axis_index("seq"), lax.axis_index("head")
    window = count // 2
    steps = []
    width = window // 2
    while width >= 2:
        steps.append(width)
        width //= 2

    def remote(src, dst, send, recv, device):
        return pltpu.make_async_remote_copy(
            src_ref=src, dst_ref=dst, send_sem=send, recv_sem=recv, device_id=device, device_id_type=MESH
        )

    barrier = pltpu.get_barrier_semaphore()
    others = [{"seq": lax.rem(seq + d, count)} for d in range(1, count)]
    others += [{"head": lax.rem(head + d, peers_head)} for d in range(1, peers_head)]
    for other in others:
        pl.semaphore_signal(barrier, inc=1, device_id=other, device_id_type=MESH)
    pl.semaphore_wait(barrier, len(others))

    def edge_copies():
        there = {"seq": lax.rem(seq + 1, count)}
        return [
            remote(v_in.at[pl.ds(tokens - SUB, SUB)], edge_v, edge_sems.at[0], edge_sems.at[1], there),
            remote(s_in.at[pl.ds(tokens - SUB, SUB)], edge_s, edge_sems.at[2], edge_sems.at[3], there),
        ]

    @pl.when(seq < count - 1)
    def _():
        for copy in edge_copies():
            copy.start()

    lane = lax.broadcasted_iota(jnp.int32, (Q, LANES), 1)
    row = lax.broadcasted_iota(jnp.int32, (Q, LANES), 0)
    left = lane < HEAD

    anchor = seq * tokens
    bounds, bound = [], 0
    for k in range(lengths.shape[0]):
        bound = bound + lengths[k]
        bounds.append(bound)

    def sequence(places):
        number = jnp.zeros(places.shape, F32)
        for bound in bounds:
            number = number + jnp.where(places >= bound, 1.0, 0.0)
        return number

    places = lax.broadcasted_iota(jnp.int32, (tokens + 2 * SUB, LANES), 0) + (anchor - SUB)
    segs[...] = sequence(places)
    for k in range(3):
        same = segs[pl.ds(SUB, tokens)] == segs[pl.ds(SUB - 3 + k, tokens)]
        mask_f[k] = jnp.where(same, 1.0, 0.0)
        same = segs[pl.ds(0, tokens + SUB)] == segs[pl.ds(3 - k, tokens + SUB)]
        mask_b[k] = jnp.where(same, 1.0, 0.0)
    head_of = lax.broadcasted_iota(jnp.int32, (channels, LANES), 0) // HEAD
    column = lax.broadcasted_iota(jnp.int32, (channels, LANES), 1)
    spread_sum[...] = jnp.where(head_of == column, 1.0, 0.0).astype(BF16)
    grads_v[...] = jnp.zeros_like(grads_v)
    grads_s[...] = jnp.zeros_like(grads_s)

    raw = t_in[...] + bias[...]
    step[...] = jnp.maximum(raw, 0.0) + jnp.log1p(jnp.exp(-jnp.abs(raw)))
    sig[...] = sigmoid(raw)
    logs[...] = -jnp.exp(rate[...]) * step[...]
    lower = jnp.where(row >= lane, 1.0, 0.0)

    @pl.loop(0, chunks)
    def _(c):
        here = pl.ds(pl.multiple_of(c * Q, Q), Q)
        run[here] = mm(lower, logs[here], precision=HIGH)
        summed = run[here]
        run_t[c] = summed.T[:16]
        last = run[pl.ds(c * Q + Q - 1, 1)]
        mine = segs[pl.ds(pl.multiple_of(c * Q + SUB, SUB), Q)]
        at_end = segs[pl.ds(c * Q + SUB + Q - 1, 1)]
        entering = segs[pl.ds(c * Q + SUB - 1, 1)]
        tail[here] = jnp.exp(last - summed) * jnp.where(mine == at_end, 1.0, 0.0)
        into[here] = jnp.exp(summed) * jnp.where(mine == entering, 1.0, 0.0)
        through = jnp.exp(last) * jnp.where(at_end == entering, 1.0, 0.0)
        passing[c] = jnp.broadcast_to(through, (Q, LANES)).T[:16]

    product = jnp.ones((16, LANES), F32)
    for c in range(chunks):
        before[c] = product
        product = product * passing[c]
    factors[seq] = product

    def factor_copies():
        return [
            remote(
                factors.at[seq], factors.at[seq], p_send.at[d - 1], p_recv.at[d - 1],
                {"seq": lax.rem(seq + d, count)},
            )
            for d in range(1, count)
        ]

    for copy in factor_copies():
        copy.start()

    def convolve(source, base, rows, lanes, taps, offset):
        begin, size = rows
        summed = offset[:, lanes] + taps[3:4, lanes] * source[pl.ds(base, size), lanes]
        for k in range(3):
            term = taps[k : k + 1, lanes] * source[pl.ds(base - 3 + k, size), lanes]
            summed = summed + term * mask_f[k, pl.ds(begin, size)]
        s = sigmoid(summed)
        return summed * s, s * (1.0 + summed * (1.0 - s))

    def convolve_rows(c):
        rows = (c * Q, Q)
        span = pl.ds(c * Q, Q)

        @pl.loop(0, pairs)
        def _(b):
            lanes = pl.ds(pl.multiple_of(b * LANES, LANES), LANES)
            source, base = (v_in, c * Q) if c else (first_v, SUB)
            val[span, lanes], slope_v[span, lanes] = convolve(source, base, rows, lanes, taps_v, off_v)

        for b, (target, low) in enumerate(((inf, inf_low), (rea, rea_low))):
            lanes = pl.ds(b * LANES, LANES)
            source, base = (s_in, c * Q) if c else (first_s, SUB)
            active, slope_s[span, lanes] = convolve(source, base, rows, lanes, taps_s, off_s)
            target[span], low[span] = split(active)

    for c in range(1, chunks):
        convolve_rows(c)

    @pl.when(seq > 0)
    def _():
        for copy in edge_copies():
            copy.wait_recv()

    @pl.when(seq == 0)
    def _():
        edge_v[...] = jnp.zeros_like(edge_v)
        edge_s[...] = jnp.zeros_like(edge_s)

    first_v[pl.ds(0, SUB)] = edge_v[...]
    first_s[pl.ds(0, SUB)] = edge_s[...]
    first_v[pl.ds(SUB, Q)] = v_in[pl.ds(0, Q)]
    first_s[pl.ds(SUB, Q)] = s_in[pl.ds(0, Q)]
    convolve_rows(0)

    def both(ref, here, p):
        return jnp.where(left, ref[here, 2 * p : 2 * p + 1], ref[here, 2 * p + 1 : 2 * p + 2])

    def halves(value):
        return jnp.concatenate(
            [jnp.where(left, value, 0.0), jnp.where(left, 0.0, value)], axis=0
        ).astype(BF16)

    @pl.loop(0, chunks)
    def _(c):
        here = pl.ds(pl.multiple_of(c * Q, Q), Q)
        for p in range(pairs):
            lanes = pl.ds(p * LANES, LANES)
            weighted = both(step, here, p) * val[here, lanes]
            scaled[here, lanes], scaled_low[here, lanes] = split(both(tail, here, p) * weighted)
        states[c] = mm(
            twice(scaled[here], 0), jnp.concatenate([inf[here], inf_low[here]], axis=0), ((0,), (0,))
        )

    for h in range(heads):
        rows = pl.ds(h * HEAD, HEAD)
        held = jnp.zeros((HEAD, LANES), F32)
        for c in range(chunks):
            added = states[c, rows]
            states[c, rows] = held
            held = passing[c, h : h + 1] * held + added
        total[rows] = held

    def carry(direction):
        bank = 0 if direction == 1 else 1

        def reach(d):
            there = seq + direction * d
            return jnp.logical_and(there >= 0, there < count)

        def heard(d):
            there = seq - direction * d
            return jnp.logical_and(there >= 0, there < count)

        def copy(slot, d):
            source = min(slot, len(steps))
            return remote(
                push.at[bank, source], got.at[bank, slot],
                carry_send.at[bank, slot], carry_recv.at[bank, slot],
                {"seq": lax.rem(seq + direction * d + count, count)},
            )

        plan = [(k, d) for k, d in enumerate(steps)]
        ends = [(len(steps), 1), (len(steps) + 1, 2)]

        def send(slot, d):
            @pl.when(reach(d))
            def _():
                copy(slot, d).start()

        def factor(first, many, h):
            product = factors[first, h : h + 1]
            for i in range(1, many):
                product = product * factors[first - direction * i, h : h + 1]
            return product

        def launch(slot):
            push[bank, slot] = total[...].astype(BF16)
            if slot < len(steps):
                send(*plan[slot])
            else:
                for end in ends:
                    send(*end)

        def join(slot):
            d = plan[slot][1]

            @pl.when(heard(d))
            def _():
                copy(slot, d).wait_recv()
                for h in range(heads):
                    rows = pl.ds(h * HEAD, HEAD)
                    total[rows] = total[rows] + factor(seq, d, h) * got[bank, slot, rows].astype(F32)

            launch(slot + 1)

        def finish():
            total[...] = jnp.zeros_like(total)

            @pl.when(heard(1))
            def _():
                copy(*ends[0]).wait_recv()
                total[...] = got[bank, ends[0][0]].astype(F32)

            @pl.when(heard(2))
            def _():
                copy(*ends[1]).wait_recv()
                for h in range(heads):
                    rows = pl.ds(h * HEAD, HEAD)
                    far = got[bank, ends[1][0], rows].astype(F32)
                    total[rows] = total[rows] + factor(seq - direction, 1, h) * far

        def close():
            for slot, d in plan + ends:
                @pl.when(reach(d))
                def _(slot=slot, d=d):
                    copy(slot, d).wait_send()

        return launch, join, finish, close

    launch, join, finish, close_forward = carry(1)
    launch(0)

    def products(here):
        read = jnp.concatenate([rea[here], rea[here], rea_low[here]], axis=1)
        return mm(read, jnp.concatenate([inf[here], inf_low[here], inf[here]], axis=1), ((1,), (1,)))

    def from_state(high, low, c, lanes):
        state = jnp.concatenate([starts[c, lanes], starts_low[c, lanes], starts[c, lanes]], axis=1)
        return mm(jnp.concatenate([high, high, low], axis=1), state, ((1,), (1,)))

    def with_state(high, low, c, lanes):
        state = jnp.concatenate([starts[c, lanes], starts_low[c, lanes], starts[c, lanes]], axis=0)
        return mm(jnp.concatenate([high, high, low], axis=1), state)

    def within(c):
        here = pl.ds(pl.multiple_of(c * Q, Q), Q)
        mine = segs[pl.ds(pl.multiple_of(c * Q + SUB, SUB), Q)]
        across = sequence(lane + (anchor + c * Q))
        hidden = jnp.where(jnp.logical_and(mine == across, row >= lane), 0.0, FAR)
        cross = products(here)
        for p in range(pairs):
            lanes = pl.ds(p * LANES, LANES)
            mixing = []
            for h in (2 * p, 2 * p + 1):
                gap = (run[here, h : h + 1] - run_t[c, h : h + 1]) + hidden
                decay = jnp.exp(gap)
                pair[c * heads + h] = decay
                mixing.append((decay * cross).astype(BF16))
            weighted = both(step, here, p) * val[here, lanes]
            out[here, lanes] = mm(jnp.concatenate(mixing, axis=1), halves(weighted))

    @pl.loop(0, chunks // 2)
    def _(c):
        within(c)

    for copy in factor_copies():
        copy.wait_recv()
    for k in range(len(steps)):
        join(k)

    @pl.loop(chunks // 2, chunks)
    def _(c):
        within(c)

    finish()
    for h in range(heads):
        rows = pl.ds(h * HEAD, HEAD)
        incoming = total[rows]
        for c in range(chunks):
            starts[c, rows], starts_low[c, rows] = split(
                states[c, rows] + before[c, h : h + 1] * incoming
            )

    rows_out[...] = jnp.zeros_like(rows_out)

    @pl.loop(0, chunks)
    def _(c):
        here = pl.ds(pl.multiple_of(c * Q, Q), Q)
        squares, dots = jnp.zeros((Q, LANES), F32), jnp.zeros((Q, LANES), F32)
        for p in range(pairs):
            lanes = pl.ds(p * LANES, LANES)
            reached = from_state(rea[here], rea_low[here], c, lanes)
            reached = reached * both(into, here, p)
            inter[here, lanes] = reached
            mixed = out[here, lanes] + reached + skip[:, lanes] * val[here, lanes]
            out[here, lanes] = mixed
            gate = g_in[here, lanes]
            gated = mixed * (gate * sigmoid(gate))
            squares = squares + gated * gated
            dots = dots + d_mix[here, lanes] * gain[:, lanes] * gated
        rows_out[0:1, here] = jnp.sum(squares.T, axis=0, keepdims=True)
        rows_out[1:2, here] = jnp.sum(dots.T, axis=0, keepdims=True)

    row_copies = [
        remote(
            rows_out, rows_in.at[d - 1], row_send.at[d - 1], row_recv.at[d - 1],
            {"head": lax.rem(head + d, peers_head)},
        )
        for d in range(1, peers_head)
    ]
    for copy in row_copies:
        copy.start()
    summed = rows_out[...]
    for d, copy in enumerate(row_copies):
        copy.wait_recv()
        summed = summed + rows_in[d]
    for copy in row_copies:
        copy.wait_send()
    rows_out[0:1] = lax.rsqrt(summed[0:1] / inner + EPS)
    rows_out[1:2] = summed[1:2] / inner

    @pl.loop(0, chunks)
    def _(c):
        here = pl.ds(pl.multiple_of(c * Q, Q), Q)
        scale = jnp.broadcast_to(rows_out[0:1, here], (Q, LANES)).T
        dot = jnp.broadcast_to(rows_out[1:2, here], (Q, LANES)).T
        cubed = scale * scale * scale * dot
        for p in range(pairs):
            lanes = pl.ds(p * LANES, LANES)
            gate, mixed, slope = g_in[here, lanes], out[here, lanes], d_mix[here, lanes]
            s = sigmoid(gate)
            opened = gate * s
            gated = mixed * opened
            normed = gated * scale
            mix_out[here, lanes] = (normed * gain[:, lanes]).astype(BF16)
            d_gated = scale * (slope * gain[:, lanes]) - gated * cubed
            d_mixer = d_gated * opened
            d_gate[here, lanes] = (d_gated * mixed * (s * (1.0 + gate * (1.0 - s)))).astype(BF16)
            out[here, lanes] = d_mixer
            d_u[here, lanes] = both(into, here, p) * d_mixer
            grads_v[5:6, lanes] = grads_v[5:6, lanes] + jnp.sum(slope * normed, axis=0, keepdims=True)
            grads_v[6:7, lanes] = grads_v[6:7, lanes] + jnp.sum(
                d_mixer * val[here, lanes], axis=0, keepdims=True
            )
        carried = d_u[here].astype(BF16)
        states[c] = mm(
            twice(carried, 0), jnp.concatenate([rea[here], rea_low[here]], axis=0), ((0,), (0,))
        )
        d_read = jnp.zeros((Q, LANES), F32)
        for p in range(pairs):
            lanes = pl.ds(p * LANES, LANES)
            d_read = d_read + with_state(*split(d_u[here, lanes]), c, lanes)
        pre_s[pl.ds(pl.multiple_of(c * Q + SUB, SUB), Q), pl.ds(LANES, LANES)] = d_read

    for h in range(heads):
        rows = pl.ds(h * HEAD, HEAD)
        held = jnp.zeros((HEAD, LANES), F32)
        for c in reversed(range(chunks)):
            held = states[c, rows] + passing[c, h : h + 1] * held
        total[rows] = held

    launch, join, finish, close_backward = carry(-1)
    launch(0)
    upper = jnp.where(row < lane, 1.0, 0.0).astype(BF16)

    def within_back(c):
        here = pl.ds(pl.multiple_of(c * Q, Q), Q)
        padded = pl.ds(pl.multiple_of(c * Q + SUB, SUB), Q)
        cross = products(here)
        d_cross = jnp.zeros((Q, LANES), F32)
        from_inter = jnp.zeros((Q, LANES), F32)
        for p in range(pairs):
            lanes = pl.ds(p * LANES, LANES)
            weighted = (both(step, here, p) * val[here, lanes]).astype(BF16)
            d_out = out[here, lanes]
            d_halves = halves(d_out)
            d_pair = mm(d_halves, weighted, ((1,), (1,)))
            mixing, terms = [], []
            for i, h in enumerate((2 * p, 2 * p + 1)):
                decay = pair[c * heads + h]
                shared = d_pair[i * Q : (i + 1) * Q] * decay
                d_cross = d_cross + shared
                terms.append((shared * cross).astype(BF16))
                mixing.append((decay * cross).astype(BF16))
            d_u[here, lanes] = mm(jnp.concatenate(mixing, axis=0), d_halves, ((0,), (0,)))
            ahead = mm(jnp.concatenate(terms, axis=0), upper)
            for i, h in enumerate((2 * p, 2 * p + 1)):
                crossing = jnp.where(row >= lane, ahead[i * Q : (i + 1) * Q], 0.0)
                prefix[c, h : h + 1] = jnp.sum(crossing, axis=0, keepdims=True)
            from_inter = from_inter + mm(
                (d_out * inter[here, lanes]).astype(BF16), spread_sum[lanes]
            )
        kept[0, here] = from_inter
        d_cross = d_cross.astype(BF16)
        pre_s[padded, pl.ds(LANES, LANES)] = pre_s[padded, pl.ds(LANES, LANES)] + mm(
            d_cross, inf[here]
        )
        pre_s[padded, pl.ds(0, LANES)] = mm(d_cross, rea[here], ((0,), (0,)))

    prefix[...] = jnp.zeros_like(prefix)

    @pl.loop(0, chunks // 2)
    def _(c):
        within_back(c)

    for k in range(len(steps)):
        join(k)

    @pl.loop(chunks // 2, chunks)
    def _(c):
        within_back(c)

    finish()
    for h in range(heads):
        rows = pl.ds(h * HEAD, HEAD)
        held = total[rows]
        for c in reversed(range(chunks)):
            start = starts[c, rows].astype(F32) + starts_low[c, rows].astype(F32)
            met = jnp.sum(held * start, axis=0, keepdims=True)
            met = jnp.sum(met, axis=1, keepdims=True) * passing[c, h : h + 1]
            prefix[c, h : h + 1] = prefix[c, h : h + 1] + met
            added = states[c, rows]
            starts[c, rows], starts_low[c, rows] = split(held)
            held = added + passing[c, h : h + 1] * held

    from_here = jnp.where(row <= lane, 1.0, 0.0)
    under = jnp.where(row > lane, 1.0, 0.0)
    rates = -jnp.exp(rate[...])
    grads_h[...] = jnp.zeros_like(grads_h)
    pre_v[pl.ds(0, SUB)] = jnp.zeros((SUB, channels), F32)
    pre_v[pl.ds(tokens + SUB, SUB)] = jnp.zeros((SUB, channels), F32)
    pre_s[pl.ds(0, SUB)] = jnp.zeros((SUB, 2 * LANES), F32)
    pre_s[pl.ds(tokens + SUB, SUB)] = jnp.zeros((SUB, 2 * LANES), F32)

    @pl.loop(0, chunks)
    def _(c):
        here = pl.ds(pl.multiple_of(c * Q, Q), Q)
        padded = pl.ds(pl.multiple_of(c * Q + SUB, SUB), Q)
        from_tail, from_step = jnp.zeros((Q, LANES), F32), jnp.zeros((Q, LANES), F32)
        d_in = jnp.zeros((Q, LANES), F32)
        for p in range(pairs):
            lanes = pl.ds(p * LANES, LANES)
            sizes = both(step, here, p)
            value = val[here, lanes]
            d_tail = from_state(inf[here], inf_low[here], c, lanes)
            d_tail = d_tail * both(tail, here, p)
            d_weighted = d_u[here, lanes] + d_tail
            from_tail = from_tail + mm((sizes * value * d_tail).astype(BF16), spread_sum[lanes])
            from_step = from_step + mm((value * d_weighted).astype(BF16), spread_sum[lanes])
            d_val = sizes * d_weighted + skip[:, lanes] * out[here, lanes]
            pre_v[padded, lanes] = d_val * slope_v[here, lanes]
            d_in = d_in + with_state(scaled[here, lanes], scaled_low[here, lanes], c, lanes)
        inflow, readout = pl.ds(0, LANES), pl.ds(LANES, LANES)
        pre_s[padded, inflow] = (pre_s[padded, inflow] + d_in) * slope_s[here, inflow]
        pre_s[padded, readout] = pre_s[padded, readout] * slope_s[here, readout]
        d_log = mm(from_here, kept[0, here], precision=HIGH) + mm(under, from_tail, precision=HIGH)
        filled = jnp.concatenate([prefix[c], jnp.zeros((Q - 16, LANES), F32)], axis=0)
        d_log = d_log + filled.T
        d_size = (from_step + rates * d_log) * sig[here]
        d_step[here] = d_size.astype(BF16)
        grads_h[0:1] = grads_h[0:1] + jnp.sum(d_size, axis=0, keepdims=True)
        grads_h[1:2] = grads_h[1:2] + jnp.sum(d_log * logs[here], axis=0, keepdims=True)

    def back(source, base, size, lanes, taps):
        summed = taps[3:4, lanes] * source[pl.ds(base, size), lanes]
        for k in range(3):
            term = taps[k : k + 1, lanes] * source[pl.ds(base + 3 - k, size), lanes]
            summed = summed + term * mask_b[k, pl.ds(base, size)]
        return summed

    def back_copies():
        there = {"seq": lax.rem(seq + count - 1, count)}
        return [
            remote(back_v, back_in_v, back_sems.at[0], back_sems.at[1], there),
            remote(back_s, back_in_s, back_sems.at[2], back_sems.at[3], there),
        ]

    for b in range(pairs):
        lanes = pl.ds(b * LANES, LANES)
        back_v[:, lanes] = back(pre_v, 0, SUB, lanes, taps_v)
    for b in range(2):
        lanes = pl.ds(b * LANES, LANES)
        back_s[:, lanes] = back(pre_s, 0, SUB, lanes, taps_s)

    @pl.when(seq > 0)
    def _():
        for copy in back_copies():
            copy.start()

    def filter_grads(pre, source, base, c, lanes, grads):
        rows = pl.ds(c * Q + SUB, Q)
        slope = pre[rows, lanes]
        for k in range(3):
            term = slope * mask_f[k, pl.ds(c * Q, Q)] * source[pl.ds(base - 3 + k, Q), lanes]
            grads[k : k + 1, lanes] = grads[k : k + 1, lanes] + jnp.sum(term, axis=0, keepdims=True)
        term = slope * source[pl.ds(base, Q), lanes]
        grads[3:4, lanes] = grads[3:4, lanes] + jnp.sum(term, axis=0, keepdims=True)
        grads[4:5, lanes] = grads[4:5, lanes] + jnp.sum(slope, axis=0, keepdims=True)

    for c in range(chunks):
        if c == chunks - 1:
            @pl.when(seq < count - 1)
            def _():
                for copy in back_copies():
                    copy.wait_recv()

            @pl.when(seq == count - 1)
            def _():
                back_in_v[...] = jnp.zeros_like(back_in_v)
                back_in_s[...] = jnp.zeros_like(back_in_s)

        def one(pre, source, base, c, lanes, taps, grads, target, received):
            result = back(pre, c * Q + SUB, Q, lanes, taps)
            if c == chunks - 1:
                result = jnp.concatenate(
                    [result[: Q - SUB], result[Q - SUB :] + received[:, lanes]], axis=0
                )
            target[pl.ds(c * Q, Q), lanes] = result.astype(BF16)
            filter_grads(pre, source, base, c, lanes, grads)

        @pl.loop(0, pairs)
        def _(b, c=c):
            lanes = pl.ds(pl.multiple_of(b * LANES, LANES), LANES)
            source, base = (v_in, c * Q) if c else (first_v, SUB)
            one(pre_v, source, base, c, lanes, taps_v, grads_v, d_value, back_in_v)

        for b in range(2):
            lanes = pl.ds(b * LANES, LANES)
            source, base = (s_in, c * Q) if c else (first_s, SUB)
            one(pre_s, source, base, c, lanes, taps_s, grads_s, d_state, back_in_s)

    @pl.when(seq < count - 1)
    def _():
        for copy in edge_copies():
            copy.wait_send()

    @pl.when(seq > 0)
    def _():
        for copy in back_copies():
            copy.wait_send()

    for copy in factor_copies():
        copy.wait_send()
    close_forward()
    close_backward()


def mix(count, peers_head, inner, lengths, v_in, s_in, g_in, t_in, d_mix, *params, collective_id):
    tokens, channels = v_in.shape
    chunks, heads = tokens // Q, channels // HEAD
    slots = 1
    width = count // 4
    while width >= 2:
        slots += 1
        width //= 2
    vmem, dma = pltpu.VMEM, pltpu.SemaphoreType.DMA
    shape = jax.ShapeDtypeStruct
    outs = [
        shape((tokens, channels), BF16), shape((tokens, channels), BF16),
        shape((tokens, channels), BF16), shape((tokens, 2 * LANES), BF16),
        shape((tokens, LANES), BF16),
        shape((8, channels), F32), shape((8, 2 * LANES), F32), shape((8, LANES), F32),
    ]
    wide, narrow = (tokens, channels), (tokens, LANES)
    scratch = [
        vmem((SUB, channels), F32), vmem((SUB, 2 * LANES), F32),
        vmem((Q + SUB, channels), F32), vmem((Q + SUB, 2 * LANES), F32),
        vmem(wide, F32), vmem(narrow, BF16), vmem(narrow, BF16), vmem(narrow, BF16), vmem(narrow, BF16),
        vmem(wide, F32), vmem((tokens, 2 * LANES), F32),
        vmem((tokens + 2 * SUB, LANES), F32),
        vmem((3, tokens, LANES), F32), vmem((3, tokens + SUB, LANES), F32),
        vmem(narrow, F32), vmem(narrow, F32), vmem(narrow, F32), vmem(narrow, F32),
        vmem((chunks, 16, LANES), F32), vmem(narrow, F32), vmem(narrow, F32),
        vmem((chunks, 16, LANES), F32),
        vmem((chunks * heads, Q, LANES), F32), vmem(wide, BF16), vmem(wide, BF16),
        vmem(wide, F32), vmem(wide, F32), vmem(wide, F32),
        vmem((chunks, channels, LANES), F32),
        vmem((chunks, channels, LANES), BF16), vmem((chunks, channels, LANES), BF16),
        vmem((chunks, 16, LANES), F32), vmem((channels, LANES), F32),
        vmem((count, 16, LANES), F32),
        vmem((2, slots, channels, LANES), BF16), vmem((2, slots + 1, channels, LANES), BF16),
        vmem((1, tokens, LANES), F32), vmem((chunks, 16, LANES), F32),
        vmem((channels, LANES), BF16),
        vmem((8, tokens), F32), vmem((peers_head - 1, 8, tokens), F32),
        vmem((tokens + 2 * SUB, channels), F32), vmem((tokens + 2 * SUB, 2 * LANES), F32),
        vmem((SUB, channels), F32), vmem((SUB, 2 * LANES), F32),
        vmem((SUB, channels), F32), vmem((SUB, 2 * LANES), F32),
        dma((4,)), dma((count - 1,)), dma((count - 1,)),
        dma((2, slots + 1)), dma((2, slots + 1)),
        dma((peers_head - 1,)), dma((peers_head - 1,)), dma((4,)),
    ]
    inside = pl.BlockSpec(memory_space=pltpu.VMEM)
    return pl.pallas_call(
        functools.partial(mixer_kernel, count, peers_head, inner),
        out_shape=outs,
        in_specs=[pl.BlockSpec(memory_space=pltpu.SMEM)] + [inside] * (5 + len(params)),
        out_specs=[inside] * len(outs),
        scratch_shapes=scratch,
        compiler_params=pltpu.CompilerParams(
            collective_id=collective_id, has_side_effects=True, vmem_limit_bytes=60 * 1024 * 1024
        ),
    )(lengths, v_in, s_in, g_in, t_in, d_mix, *params)


def sum_rows(jobs, lines, peers_head, count_in, *refs):
    ins, rest = list(refs[:count_in]), refs[count_in:]
    blocks, tail, normed, mixed, dots = rest[:5]
    outs, rest = rest[5 : 5 + count_in + 1], rest[6 + count_in :]
    every, normed_sum, mixed_sum, dots_sum = rest[:4]
    scratch = rest[4:]
    count = len(jobs)
    own, y_in, z_in, final = (scratch[k * count : (k + 1) * count] for k in range(4))
    (own_sem, ys, yr, zs, zr, gzs, gzr, gys, gyr, keep_sem) = scratch[4 * count : 4 * count + 10]
    (packed, block_own, block_in, normed_own, normed_in, mixed_own, mixed_in, dots_in,
     local_sem, hs, hr) = scratch[4 * count + 10 :]
    ins = [packed] + ins
    seq, head = lax.axis_index("seq"), lax.axis_index("head")
    z, y = seq // lines, seq % lines
    barrier = pltpu.get_barrier_semaphore()

    def at(zz, yy):
        return {"seq": zz * lines + yy}

    def remote(src, dst, send, recv, peer):
        return pltpu.make_async_remote_copy(
            src_ref=src, dst_ref=dst, send_sem=send, recv_sem=recv, device_id=peer, device_id_type=MESH
        )

    peers = [at(z, lax.rem(y + d, lines)) for d in range(1, lines)]
    peers += [at(lax.rem(z + d, LINE), y) for d in range(1, LINE)]
    peers += [{"head": lax.rem(head + d, peers_head)} for d in range(1, peers_head)]
    for peer in peers:
        pl.semaphore_signal(barrier, inc=1, device_id=peer, device_id_type=MESH)
    pl.semaphore_wait(barrier, len(peers))

    width = normed_sum.shape[0]
    block = blocks.shape[1]

    def head_copies(kind):
        copies = []
        for d in range(1, peers_head):
            to = lax.rem(head + d, peers_head)
            rows = pl.ds(to * width, width)
            src, dst = (
                (blocks.at[to], block_in.at[d - 1]),
                (dots, dots_in.at[d - 1]),
                (normed.at[rows], normed_in.at[d - 1]),
                (mixed.at[rows], mixed_in.at[d - 1]),
                (outs[0].at[pl.ds(0, width)], every.at[head]),
            )[kind]
            copies.append(remote(src, dst, hs.at[kind, d - 1], hr.at[kind, d - 1], {"head": to}))
        return copies

    rows = pl.ds(head * width, width)
    local_copies = [
        pltpu.make_async_copy(blocks.at[head], block_own, local_sem.at[0]),
        pltpu.make_async_copy(tail, packed.at[pl.ds(block, tail.shape[0])], local_sem.at[1]),
        pltpu.make_async_copy(normed.at[rows], normed_own, local_sem.at[2]),
        pltpu.make_async_copy(mixed.at[rows], mixed_own, local_sem.at[3]),
    ]

    sizes = []
    for which, start, rows in jobs:
        sizes.append((which, start, rows, rows // lines, rows // lines // LINE))

    def y_copies(j):
        which, start, rows, part, piece = sizes[j]
        copies = []
        for d in range(1, lines):
            to = lax.rem(y + d, lines)
            copies.append(
                remote(
                    ins[which].at[pl.ds(start + to * part, part)],
                    y_in[j].at[d - 1],
                    ys.at[j, d - 1],
                    yr.at[j, d - 1],
                    at(z, to),
                )
            )
        return copies

    def own_copy(j):
        which, start, rows, part, piece = sizes[j]
        return pltpu.make_async_copy(
            ins[which].at[pl.ds(start + y * part, part)], own[j], own_sem.at[j]
        )

    def z_copies(j):
        piece = sizes[j][4]
        copies = []
        for d in (1, LINE - 1, 2):
            to = lax.rem(z + d, LINE)
            copies.append(
                remote(
                    own[j].at[pl.ds(to * piece, piece)],
                    z_in[j].at[d - 1],
                    zs.at[j, d - 1],
                    zr.at[j, d - 1],
                    at(to, y),
                )
            )
        return copies

    def place(j, zz, yy):
        which, start, rows, part, piece = sizes[j]
        return outs[which].at[pl.ds(start + yy * part + zz * piece, piece)]

    def gather_z(j):
        return [
            remote(final[j], place(j, z, y), gzs.at[j, d - 1], gzr.at[j, d - 1], at(lax.rem(z + d, LINE), y))
            for d in (1, LINE - 1, 2)
        ]

    def gather_y(j, d):
        source = lax.rem(z + LINE - d, LINE)
        src = final[j] if d == 0 else place(j, source, y)
        return [
            remote(
                src,
                place(j, source, y),
                gys.at[j, d, e - 1],
                gyr.at[j, d, e - 1],
                at(z, lax.rem(y + e, lines)),
            )
            for e in range(1, lines)
        ]

    def keep(j):
        return pltpu.make_async_copy(final[j], place(j, z, y), keep_sem.at[j])

    for copy in local_copies + head_copies(0):
        copy.start()
    for j in range(count):
        if jobs[j][0]:
            own_copy(j).start()
            for copy in y_copies(j):
                copy.start()
    for kind in (1, 2, 3):
        for copy in head_copies(kind):
            copy.start()

    def pack():
        local_copies[0].wait()
        local_copies[1].wait()
        for copy in head_copies(0):
            copy.wait_recv()

        def step(i, carry):
            rows = pl.ds(pl.multiple_of(i * 16, 16), 16)
            total = block_own[rows].astype(jnp.float32)
            for d in range(peers_head - 1):
                total = total + block_in[d, rows].astype(jnp.float32)
            packed[rows] = total.astype(jnp.bfloat16)
            return carry

        lax.fori_loop(0, block // 16, step, 0)

    def sum_heads(kind, mine, received, target, k):
        local_copies[k].wait()
        for copy in head_copies(kind):
            copy.wait_recv()

        def step(i, carry):
            rows = pl.ds(pl.multiple_of(i * 16, 16), 16)
            total = mine[rows].astype(jnp.float32)
            for d in range(peers_head - 1):
                total = total + received[d, rows].astype(jnp.float32)
            target[rows] = total
            return carry

        lax.fori_loop(0, width // 16, step, 0)

    def reduce_y(j):
        if not jobs[j][0]:
            pack()
            own_copy(j).start()
            for copy in y_copies(j):
                copy.start()
        own_copy(j).wait()
        for copy in y_copies(j):
            copy.wait_recv()
        part = sizes[j][3]
        tile = 16 if part % 16 == 0 else 8

        def step(i, carry):
            rows = pl.ds(pl.multiple_of(i * tile, tile), tile)
            total = own[j][rows].astype(jnp.float32)
            for d in range(lines - 1):
                total = total + y_in[j][d, rows].astype(jnp.float32)
            own[j][rows] = total.astype(jnp.bfloat16)
            return carry

        lax.fori_loop(0, part // tile, step, 0)
        for copy in z_copies(j):
            copy.start()

    def reduce_z(j):
        for copy in z_copies(j):
            copy.wait_recv()
        piece = sizes[j][4]
        tile = 16 if piece % 16 == 0 else 8
        base = z * piece

        def step(i, carry):
            rows = pl.ds(pl.multiple_of(i * tile, tile), tile)
            mine = pl.ds(pl.multiple_of(base + i * tile, tile), tile)
            total = own[j][mine].astype(jnp.float32)
            for d in range(LINE - 1):
                total = total + z_in[j][d, rows].astype(jnp.float32)
            final[j][rows] = total.astype(jnp.bfloat16)
            return carry

        lax.fori_loop(0, piece // tile, step, 0)
        keep(j).start()
        for copy in gather_z(j):
            copy.start()
        for copy in gather_y(j, 0):
            copy.start()

    def forward(j):
        copies = dict(zip((1, LINE - 1, 2), gather_z(j)))
        for d in (1, LINE - 1, 2):
            copies[d].wait_recv()
            for copy in gather_y(j, d):
                copy.start()

    for i in range(count + 2):
        if i < count:
            reduce_y(i)
        if 0 <= i - 1 < count:
            reduce_z(i - 1)
        if 0 <= i - 2 < count:
            forward(i - 2)
    total = dots[...]
    for d, copy in enumerate(head_copies(1)):
        copy.wait_recv()
        total = total + dots_in[d]
    dots_sum[...] = total
    sum_heads(2, normed_own, normed_in, normed_sum, 2)
    sum_heads(3, mixed_own, mixed_in, mixed_sum, 3)
    for j in sorted(range(count), key=lambda j: jobs[j][0]):
        keep(j).wait()
        for copy in y_copies(j) + z_copies(j) + gather_z(j):
            copy.wait_send()
        for d in range(LINE):
            for copy in gather_y(j, d):
                copy.wait_recv()
                copy.wait_send()
        if not jobs[j][0]:
            mine = pltpu.make_async_copy(outs[0].at[pl.ds(0, width)], every.at[head], local_sem.at[4])
            mine.start()
            for copy in head_copies(4):
                copy.start()
            mine.wait()
    for copy in head_copies(4):
        copy.wait_recv()
    for kind in range(5):
        for copy in head_copies(kind):
            copy.wait_send()


def sum_over_seq(arrays, split, blocks, tail, normed, mixed, dots, lines, peers_head, collective_id):
    bf16, f32 = jnp.bfloat16, jnp.float32
    width, tokens = normed.shape[0] // peers_head, normed.shape[1]
    packed = jax.ShapeDtypeStruct((blocks.shape[1] + tail.shape[0], tail.shape[1]), bf16)
    jobs = []
    for which, (array, parts) in enumerate(zip([packed] + arrays, (1,) + split)):
        rows = array.shape[0] // parts
        jobs += [(which, k * rows, rows) for k in range(parts)]
    jobs = jobs[1:3] + jobs[:1] + jobs[3:]
    count = len(jobs)
    widths = [([packed] + arrays)[job[0]].shape[1] for job in jobs]
    scratch = [pltpu.VMEM((job[2] // lines, w), bf16) for job, w in zip(jobs, widths)]
    scratch += [pltpu.VMEM((lines - 1, job[2] // lines, w), bf16) for job, w in zip(jobs, widths)]
    scratch += [
        pltpu.VMEM((LINE - 1, job[2] // lines // LINE, w), bf16) for job, w in zip(jobs, widths)
    ]
    scratch += [pltpu.VMEM((job[2] // lines // LINE, w), bf16) for job, w in zip(jobs, widths)]
    dma = pltpu.SemaphoreType.DMA
    scratch += [
        dma((count,)),
        dma((count, lines - 1)),
        dma((count, lines - 1)),
        dma((count, LINE - 1)),
        dma((count, LINE - 1)),
        dma((count, LINE - 1)),
        dma((count, LINE - 1)),
        dma((count, LINE, lines - 1)),
        dma((count, LINE, lines - 1)),
        dma((count,)),
        pltpu.VMEM(packed.shape, bf16),
        pltpu.VMEM(blocks.shape[1:], bf16),
        pltpu.VMEM((peers_head - 1,) + blocks.shape[1:], bf16),
        pltpu.VMEM((width, tokens), bf16),
        pltpu.VMEM((peers_head - 1, width, tokens), bf16),
        pltpu.VMEM((width, tokens), bf16),
        pltpu.VMEM((peers_head - 1, width, tokens), bf16),
        pltpu.VMEM((peers_head - 1,) + dots.shape, f32),
        dma((5,)),
        dma((5, peers_head - 1)),
        dma((5, peers_head - 1)),
    ]
    anywhere, inside = pl.BlockSpec(memory_space=pl.ANY), pl.BlockSpec(memory_space=pltpu.VMEM)
    shape = jax.ShapeDtypeStruct
    return pl.pallas_call(
        functools.partial(sum_rows, jobs, lines, peers_head, len(arrays)),
        out_shape=[packed]
        + [shape(array.shape, bf16) for array in arrays]
        + [shape((peers_head, width, tail.shape[1]), bf16)]
        + [shape((width, tokens), f32)] * 2
        + [shape(dots.shape, f32)],
        in_specs=[anywhere] * (len(arrays) + 4) + [inside],
        out_specs=[anywhere] * (len(arrays) + 2) + [inside] * 3,
        scratch_shapes=scratch,
        compiler_params=pltpu.CompilerParams(
            collective_id=collective_id, has_side_effects=True, vmem_limit_bytes=60 * 1024 * 1024
        ),
    )(*arrays, blocks, tail, normed, mixed, dots)


def contract_rows(left, right):
    return lax.dot_general(
        left, right, (((0,), (0,)), ((), ())), preferred_element_type=jnp.float32
    )


def contract_cols(left, right):
    return lax.dot_general(
        left, right, (((1,), (1,)), ((), ())), preferred_element_type=jnp.float32
    )


def local(
    hidden_in,
    norm_gain,
    gate_weight,
    value_weight,
    step_weight,
    state_weight,
    value_filter,
    value_offset,
    state_filter,
    state_offset,
    step_bias,
    decay_log,
    skip_gain,
    mix_gain,
    out_weight,
    lengths,
    cotangent,
):
    tokens, width = hidden_in.shape
    heads, channels = step_weight.shape[1], value_weight.shape[1]
    count, peers_head = lax.axis_size("seq"), lax.axis_size("head")
    features = width * peers_head
    gain_block = jnp.broadcast_to(norm_gain.astype(F32)[None, :], (8, width))
    hidden_full, cot_full, gain_full = gather_heads([hidden_in, cotangent, gain_block], peers_head, 1)
    gain_full = gain_full[:1]
    rows_full = hidden_full.astype(F32)
    scale_in = lax.rsqrt(jnp.mean(rows_full * rows_full, axis=1, keepdims=True) + EPS)
    normed = (rows_full * scale_in * gain_full).astype(BF16)

    def project(weight):
        return jnp.dot(normed, weight, preferred_element_type=F32)

    def lanes(vector):
        return jnp.pad(vector, (0, LANES - heads))[None, :]

    step_wide = jnp.pad(step_weight, ((0, 0), (0, LANES - heads)))
    d_mix = contract_cols(cot_full, out_weight)
    mix_out, d_gate, d_value, d_state, d_step, grads_v, grads_s, grads_h = mix(
        count,
        peers_head,
        channels * peers_head,
        lengths,
        project(value_weight),
        project(state_weight),
        project(gate_weight),
        project(step_wide),
        d_mix,
        value_filter,
        state_filter,
        value_offset[None, :],
        state_offset[None, :],
        lanes(step_bias),
        lanes(decay_log),
        jnp.repeat(skip_gain, HEAD)[None, :],
        mix_gain[None, :],
        collective_id=2,
    )
    half = features // 2
    out_part = jnp.concatenate(
        [contract_rows(mix_out, cot_full[:, :half]), contract_rows(mix_out, cot_full[:, half:])]
    ).astype(BF16)
    gate_part = contract_rows(normed, d_gate).astype(BF16)
    value_part = contract_rows(normed, d_value).astype(BF16)
    state_part = contract_rows(normed, d_state)
    step_part = contract_rows(normed, d_step)[:, :heads]
    normed_part = (
        contract_cols(gate_weight, d_gate)
        + contract_cols(value_weight, d_value)
        + contract_cols(state_weight, d_state)
        + contract_cols(step_wide, d_step)
    )
    mixed_part = lax.dot_general(
        out_weight, mix_out, (((0,), (1,)), ((), ())), preferred_element_type=F32
    )
    rows_t = rows_full.T
    weighted = normed_part * rows_t
    dots = jnp.sum(weighted * gain_full.T, axis=0)
    gain_part = jnp.sum(weighted * scale_in.T, axis=1)
    dots = jnp.broadcast_to(dots[None, :], (8, tokens))
    state_size = d_state.shape[1]
    shared = jnp.concatenate([grads_s[:5], gain_part.reshape(-1, state_size)])
    shared = jnp.pad(shared, ((0, 16 - shared.shape[0]), (0, 0)))
    blocks = jnp.concatenate(
        [
            state_part.reshape(peers_head, width, state_size),
            jnp.broadcast_to(shared[None], (peers_head, 16, state_size)),
        ],
        axis=1,
    ).astype(BF16)
    own = (
        step_part,
        grads_v[:4],
        grads_v[4],
        grads_h[0, :heads],
        grads_h[1, :heads],
        jnp.sum(grads_v[6].reshape(heads, HEAD), axis=1),
        grads_v[5],
    )
    packed = jnp.concatenate([jnp.reshape(part, (-1,)) for part in own])
    tail_rows = width // 3 - 16
    packed = jnp.pad(packed, (0, tail_rows * state_size - packed.size))
    packed = packed.reshape(tail_rows, state_size).astype(BF16)
    extra, out_sum, gate_sum, value_sum, state_sum, normed_sum, mixed_sum, dot_sum = sum_over_seq(
        [out_part, gate_part, value_part],
        (3, 3, 3),
        blocks,
        packed,
        normed_part.astype(BF16),
        mixed_part.astype(BF16),
        dots,
        count // LINE,
        peers_head,
        3,
    )
    own_rows = hidden_in.astype(F32)
    block_out = (own_rows + mixed_sum.T).astype(BF16)
    delta_hidden = (
        cotangent.astype(F32)
        + scale_in * (normed_sum.T * norm_gain.astype(F32)[None, :])
        - own_rows * scale_in**3 * (dot_sum[0] / features)[:, None]
    )
    extra = extra[width:].astype(F32)
    norm_sum = lax.dynamic_slice_in_dim(
        extra[5 : 5 + features // state_size].reshape(-1), lax.axis_index("head") * width, width, 0
    )
    packed = extra[16:].reshape(-1)
    pieces, start = [], 0
    for part in own:
        pieces.append(jnp.reshape(packed[start : start + part.size], part.shape))
        start += part.size
    step_sum, filter_sum, offset_sum, bias_sum, decay_sum, skip_sum, gain_sum = pieces
    return (
        block_out,
        delta_hidden,
        norm_sum,
        gate_sum.astype(F32),
        value_sum.astype(F32),
        step_sum,
        state_sum.reshape(features, state_size).astype(F32),
        filter_sum,
        offset_sum,
        extra[:4],
        extra[4],
        bias_sum,
        decay_sum,
        skip_sum,
        gain_sum,
        jnp.concatenate(jnp.split(out_sum, 2, axis=0), axis=1).astype(F32),
    )


def solution(mesh):
    in_specs = (
        P("seq", "head"),
        P("head"),
        P(None, "head"),
        P(None, "head"),
        P(None, "head"),
        P(),
        P(None, "head"),
        P("head"),
        P(),
        P(),
        P("head"),
        P("head"),
        P("head"),
        P("head"),
        P("head", None),
        P(),
        P("seq", "head"),
    )
    out_specs = (
        P("seq", "head"),
        P("seq", "head"),
        P("head"),
        P(None, "head"),
        P(None, "head"),
        P(None, "head"),
        P(),
        P(None, "head"),
        P("head"),
        P(),
        P(),
        P("head"),
        P("head"),
        P("head"),
        P("head"),
        P("head", None),
    )
    return jax.shard_map(local, mesh=mesh, in_specs=in_specs, out_specs=out_specs, check_vma=False)
```

time: 581 us -> 397 us (0.68); the launches traced: 571 us -> 396 us
  Pallas kernels: 182 us -> 324 us
  waiting for transfers between devices: 80.6 us -> 0 us
  other arithmetic: 75.4 us -> 16.8 us
  matrix products: 84.5 us -> 32.4 us
  local copies, waits for them, and re-layouts: 72.8 us -> 22.1 us
  starting transfers between devices: 32.6 us -> 0 us
  blocking collectives: 27.3 us -> 0 us
  between operations: 16 us -> 1.12 us
    pallas_call x1 -> x3, Pallas kernels: 182 us -> 324 us  [the longest x1 230 us: sum_over_seq(): pl.pallas_call(functools.partial(sum_rows, jobs, lines, peers_head, len(a...]
    dot_general x17 -> x5, matrix products: 59.2 us -> 13.1 us  [the longest x4 10.4 us: project(): return jnp.dot(normed, weight, preferred_element_type=F32)]
    ppermute x12 -> x0, starting transfers between devices: 32.2 us -> none  [shifted(): lax.ppermute(value, axis, [(source, source + steps) for source in range(l...]
    unnamed x7 -> x0, waiting for transfers between devices: 31.7 us -> none
    ppermute x12 -> x0, waiting for transfers between devices: 25.2 us -> none  [shifted(): lax.ppermute(value, axis, [(source, source + steps) for source in range(l...]
    another operation x13 -> x3, other arithmetic: 15.6 us -> 0.02 us
    psum x1 -> x0, waiting for transfers between devices: 15.2 us -> none  [local(): d_shared = lax.psum(d_shared, 'head')]
    reduce_sum x13 -> x2, other arithmetic: 16.6 us -> 2.05 us  [the longest x1 1.93 us: local(): jnp.mean(rows_full * rows_full, axis=1, keepdims=True) + EPS]
  transfers between devices with their start and end apart: 17 -> 0, of which waited for: 8 -> 0; matrix products, arithmetic and copies ran while one was open for 32% -> 0% of each run, Pallas kernels for 0% -> 0%
where the time goes in v2:
time: 397 us; the launch traced here: 396 us
  Pallas kernels  324 us (82%)
  matrix products  32.4 us (8%)
  local copies, waits for them, and re-layouts  22.1 us (6%)
  other arithmetic  16.8 us (4%)
    pallas_call x1, Pallas kernels, sum_over_seq(): pl.pallas_call(functools.partial(sum_rows, jobs, lines, peers_head, len(a...  230 us
    pallas_call x1, Pallas kernels, mix(): pl.pallas_call(functools.partial(mixer_kernel, count, peers_head, inner),...  65.7 us
    pallas_call x1, Pallas kernels, gather_heads(): pl.pallas_call(functools.partial(gather_kernel, peers_head, flat, count),...  28.5 us
    dot_general x4, matrix products, project(): return jnp.dot(normed, weight, preferred_element_type=F32)  10.4 us
    dot_general x5, matrix products, contract_cols(): lax.dot_general(left, right, (((1,), (1,)), ((), ())), preferred_element_...  9.66 us
    dot_general x6, matrix products, contract_rows(): lax.dot_general(left, right, (((0,), (0,)), ((), ())), preferred_element_...  9.62 us

profile of v2, /device:TPU:0, one launch (start us, length us, event | category | flops | bytes accessed | tf_op | source)
XLA Modules:
  0.0 396.2 jit_solution(16129686191289090162)
XLA Ops:
  0.7 1.4 broadcast_in_dim.18.refs_2_
  2.1 28.5 %shard_map.288 = (bf16[512,1536]{1,0:T(8,128)(2,1)}, bf16[512,1536]{1,0:T(8,128)(2,1)}, f32[8,1536]{1,0:T(8,128)}) custom-call(bf16[512,384]{1,0:T(8,128)(2,1)} %refs_0_.1, bf16[512,384]{1,0:T(8,128)(2,1)} %refs_1_.1, f32[8,384]{1,0:T(8,128)} %broadcast_in_dim.18.refs_2_), custom_call_target="tpu_custom_call" | custom-call | tf_op jit(solution)/shard_map/pallas_call | solution.py:82
  30.6 2.6 copy.44
  33.2 1.9 fusion.1
  35.1 0.8 slice_reduce_fusion
  35.9 3.0 fusion.12.t_in
  39.0 2.8 fusion.23.g_in
  41.8 1.7 fusion.25.s_in
  43.5 2.8 fusion.27.v_in
  46.4 2.6 fusion.31.d_mix
  49.6 0.7 broadcast_in_dim_reshape.3.skip
  51.4 65.7 %shard_map.289 = (bf16[512,768]{1,0:T(8,128)(2,1)}, bf16[512,768]{1,0:T(8,128)(2,1)}, bf16[512,768]{1,0:T(8,128)(2,1)}, bf16[512,256]{1,0:T(8,128)(2,1)}, bf16[5...) custom-call(s32[4]{0:T(128)} %lengths.1, f32[512,768]{1,0:T(8,128)} %fusion.27.v_in, ...), custom_call_target="tpu_custom_call" | custom-call | tf_op jit(solution)/shard_map/pallas_call | solution.py:739
  117.2 1.7 fusion.17
  119.1 0.7 reshape.101
  120.5 0.6 convert_element_type.71.refs_4_
  121.1 2.8 fusion.32
  123.9 1.4 convolution_add_fusion.2
  125.4 0.6 fusion
  126.0 0.7 copy-done.4
  126.8 2.3 multiply_reduce_fusion
  129.1 0.6 convolution_convert_fusion.3
  129.8 1.0 pad_maximum_fusion.1.refs_3_
  130.8 0.6 broadcast_in_dim.47.refs_7_
  131.4 2.8 convolution_convert_fusion.refs_2_
  134.2 2.8 convolution_convert_fusion.1.refs_1_
  137.1 0.8 convolution_convert_fusion.5
  137.9 0.8 convolution_convert_fusion.4
  138.7 1.6 pad_maximum_fusion.refs_0_
  140.3 0.9 copy-done.29
  141.2 2.7 fusion.5.refs_6_
  143.9 229.6 %shard_map.290 = (bf16[512,256]{1,0:T(8,128)(2,1)}, bf16[1536,768]{1,0:T(8,128)(2,1)}, bf16[1536,768]{1,0:T(8,128)(2,1)}, bf16[1536,768]{1,0:T(8,128)(2,1)}, bf1...) custom-call(bf16[1536,768]{1,0:T(8,128)(2,1)} %pad_maximum_fusion.refs_0_, ...), custom_call_target="tpu_custom_call" | custom-call | tf_op jit(solution)/shard_map/pallas_call | solution.py:1051
  373.5 1.8 fusion.29
  375.3 2.8 maximum_convert_fusion
  378.2 2.5 convert_element_type.78
  380.7 2.5 convert_element_type.79
  383.3 0.7 slice_multiply_fusion
  384.4 1.4 fusion.8
  385.8 1.1 copy.52
  387.0 0.9 copy.51
  387.9 1.3 bitcast_convert_fusion
  389.2 0.8 slice_convert_fusion.1
  390.1 0.8 reshape.104
  390.9 0.9 copy.53
  391.9 0.7 slice.125
  393.2 0.6 reshape.105
  393.8 0.7 dynamic_slice.3
  394.5 0.6 slice.103
  395.1 0.6 slice.119
  (100 shorter events, 4.4 us)
Async XLA Ops:
  0.6 38.3 %copy-start = (bf16[1536,768]{1,0:T(8,128)(2,1)S(1)}, bf16[1536,768]{1,0:T(8,128)(2,1)}, u32[]{:S(2)}) copy-start(bf16[1536,768]{1,0:T(8,128)(2,1)} %param.19) | copy-start | bytes 7077892
  30.6 5.4 %copy-start.18 = (bf16[1536,12]{0,1:T(8,128)(2,1)S(1)}, bf16[1536,12]{0,1:T(8,128)(2,1)}, u32[]{:S(2)}) copy-start(bf16[1536,12]{0,1:T(8,128)(2,1)} %param.21) | copy-start | bytes 110596
  33.2 5.8 %copy-start.2 = (bf16[512,1536]{0,1:T(8,128)(2,1)S(1)}, bf16[512,1536]{0,1:T(8,128)(2,1)}, u32[]{:S(2)}) copy-start(bf16[512,1536]{0,1:T(8,128)(2,1)} %copy.44) | copy-start | bytes 4718596
  39.0 2.8 copy-start.14
  41.8 1.8 copy-start.7
  43.5 2.8 copy-start.28
  43.5 2.8 copy-start.30
  46.4 2.6 copy-start.26
  46.4 2.6 copy-start.27
  46.4 3.1 copy-start.25
  46.4 3.8 copy-start.20
  46.4 4.4 %copy-start.21 = (f32[768]{0:T(1024)S(1)}, f32[768]{0:T(1024)}, u32[]{:S(2)}) copy-start(f32[768]{0:T(1024)} %param.30) | copy-start | bytes 9220
  51.4 65.8 %copy-start.3 = (bf16[512,1536]{0,1:T(8,128)(2,1)S(1)}, bf16[512,1536]{0,1:T(8,128)(2,1)}, u32[]{:S(2)}) copy-start(bf16[512,1536]{0,1:T(8,128)(2,1)} %copy.44) | copy-start | bytes 4718596
  117.1 2.7 copy-start.19
  117.2 2.9 copy-start.22
  121.1 2.8 copy-start.8
  121.1 2.8 copy-start.11
  123.9 1.5 copy-start.15
  123.9 1.5 copy-start.16
  125.4 1.4 copy-start.4
  125.4 1.4 copy-start.17
  126.8 2.3 copy-start.24
  131.4 2.9 copy-start.33
  134.2 2.9 copy-start.31
  134.2 2.9 copy-start.32
  138.7 2.5 copy-start.29
  375.3 2.8 copy-start.6
  378.2 2.5 copy-start.5
  380.7 3.3 copy-start.9
  380.7 3.5 copy-start.10
  380.7 3.7 copy-start.23
  380.7 3.7 copy-start.12
  385.8 2.1 copy-start.13
  387.9 8.3 %copy-start.1 = (bf16[1536,768]{1,0:T(8,128)(2,1)S(1)}, bf16[1536,768]{1,0:T(8,128)(2,1)}, u32[]{:S(2)}) copy-start(bf16[1536,768]{1,0:T(8,128)(2,1)} %param.19) | copy-start | bytes 7077892

commit v3 on v2

--- a/solution.py
+++ b/solution.py
@@ -748,320 +748,520 @@
     )(lengths, v_in, s_in, g_in, t_in, d_mix, *params)
 
 
-def sum_rows(jobs, lines, peers_head, count_in, *refs):
-    ins, rest = list(refs[:count_in]), refs[count_in:]
-    blocks, tail, normed, mixed, dots = rest[:5]
-    outs, rest = rest[5 : 5 + count_in + 1], rest[6 + count_in :]
-    every, normed_sum, mixed_sum, dots_sum = rest[:4]
-    scratch = rest[4:]
+def add_rows(target, terms, rows, dtype=BF16):
+    tile = next(t for t in (32, 16, 8) if rows % t == 0)
+
+    @pl.loop(0, rows // tile)
+    def _(i):
+        def at(start):
+            return pl.ds(pl.multiple_of(start + i * tile, 8), tile)
+
+        total = terms[0][0][at(terms[0][1])].astype(F32)
+        for ref, start in terms[1:]:
+            total = total + ref[at(start)].astype(F32)
+        target[0][at(target[1])] = total.astype(dtype)
+
+
+class Job:
+    def __init__(self, index, y_first, src, dst, start, rows, lines, y_in, right, left, total, final, sems, where):
+        self.index, self.y_first, self.src, self.dst, self.start = index, y_first, src, dst, start
+        self.lines, self.y_in, self.right, self.left = lines, y_in, right, left
+        self.total, self.final = total, final
+        self.sems = sems
+        self.seq, self.z, self.y = where
+        self.part = rows // lines
+        self.chunk = rows // lines // LINE if y_first else rows // LINE
+        self.piece = rows // lines // LINE
+        self.rows = rows
+        self.base = start + self.y * self.part if y_first else start
+
+    def remote(self, src, dst, name, slot, device):
+        send, recv = self.sems[name]
+        return pltpu.make_async_remote_copy(
+            src_ref=src, dst_ref=dst, send_sem=send.at[(self.index,) + slot],
+            recv_sem=recv.at[(self.index,) + slot], device_id={"seq": device}, device_id_type=MESH,
+        )
+
+    def seat(self, z, y):
+        return z * self.lines + y
+
+    def peer_y(self, d):
+        return lax.rem(self.y + d, self.lines)
+
+    def swap(self, d):
+        to = self.peer_y(d)
+        if self.y_first:
+            src = self.src.at[pl.ds(self.start + to * self.part, self.part)]
+        else:
+            src = self.total.at[pl.ds(to * self.piece, self.piece)]
+        return self.remote(src, self.y_in.at[d - 1], "swap", (d - 1,), self.seat(self.z, to))
+
+    def swaps(self):
+        for d in range(1, self.lines):
+            self.swap(d).start()
+
+    def join_y(self):
+        for d in range(1, self.lines):
+            self.swap(d).wait_recv()
+        others = [(self.y_in.at[d], 0) for d in range(self.lines - 1)]
+        if self.y_first:
+            add_rows((self.src, self.base), [(self.src, self.base)] + others, self.part)
+        else:
+            mine = self.y * self.piece
+            add_rows((self.final, mine), [(self.total, mine)] + others, self.piece)
+
+    def pass_on(self, c, z, direction, first):
+        box = self.right if direction > 0 else self.left
+        src = self.src.at[pl.ds(self.base + c * self.chunk, self.chunk)] if first else box.at[c]
+        name = "right" if direction > 0 else "left"
+        return self.remote(src, box.at[c], name, (c,), self.seat(z + direction, self.y))
+
+    def come(self, c, direction):
+        box = self.right if direction > 0 else self.left
+        return self.remote(box.at[c], box.at[c], "right" if direction > 0 else "left", (c,), self.seq)
+
+    def chain_start(self):
+        @pl.when(self.z == 0)
+        def _():
+            for c in (3, 2, 1):
+                self.pass_on(c, 0, 1, True).start()
+
+        @pl.when(self.z == 3)
+        def _():
+            for c in (0, 1, 2):
+                self.pass_on(c, 3, -1, True).start()
+
+    def chain_hop(self, h):
+        for z, direction, last in ((h, 1, 3), (3 - h, -1, 0)):
+            box = self.right if direction > 0 else self.left
+
+            @pl.when(self.z == z)
+            def _(z=z, direction=direction, last=last, box=box):
+                for c in range(last, z - direction, -direction):
+                    self.come(c, direction).wait_recv()
+                    if c != z:
+                        add_rows((box.at[c], 0), [(box.at[c], 0), (self.src, self.base + c * self.chunk)], self.chunk)
+                        self.pass_on(c, z, direction, False).start()
+
+    def chain_end(self, seats):
+        for z in seats:
+            @pl.when(self.z == z)
+            def _(z=z):
+                terms = [(self.src, self.base + z * self.chunk)]
+                if z > 0:
+                    terms.append((self.right.at[z], 0))
+                if z < LINE - 1:
+                    terms.append((self.left.at[z], 0))
+                add_rows((self.final if self.y_first else self.total, 0), terms, self.chunk)
+                self.chain_done()
+
+    def chain_done(self):
+        if self.y_first:
+            self.keep().start()
+            self.spread_start()
+            for d in range(1, self.lines):
+                self.share(0, d).start()
+        else:
+            self.swaps()
+
+    def place(self, z):
+        first = self.y * self.part if self.y_first else 0
+        return self.dst.at[pl.ds(self.start + first + z * self.chunk, self.chunk)]
+
+    def keep(self):
+        return pltpu.make_async_copy(self.final, self.place(self.z), self.sems["keep"].at[self.index])
+
+    def spread(self, direction, h):
+        src = self.final if h == 1 else self.place(self.z - direction * (h - 1))
+        slot = h if direction > 0 else LINE - 1 + h
+        device = self.seat(self.z + direction, self.y)
+        return self.remote(src, self.place(self.z - direction * (h - 1)), "spread", (slot,), device)
+
+    def spread_from(self, direction, h):
+        slot = h if direction > 0 else LINE - 1 + h
+        there = self.place(self.z - direction * h)
+        return self.remote(there, there, "spread", (slot,), self.seq)
+
+    def goes(self, direction):
+        return self.z < LINE - 1 if direction > 0 else self.z > 0
+
+    def comes(self, direction, h):
+        return self.z >= h if direction > 0 else self.z < LINE - h
+
+    def spread_start(self):
+        for direction in (1, -1):
+            @pl.when(self.goes(direction))
+            def _(direction=direction):
+                self.spread(direction, 1).start()
+
+    def spread_hop(self, h):
+        for direction in (1, -1):
+            @pl.when(self.comes(direction, h))
+            def _(direction=direction):
+                self.spread_from(direction, h).wait_recv()
+                if h < LINE - 1:
+                    @pl.when(self.goes(direction))
+                    def _():
+                        self.spread(direction, h + 1).start()
+
+                if self.y_first:
+                    for d in range(1, self.lines):
+                        self.share(h if direction > 0 else LINE - 1 + h, d).start()
+
+    def share(self, slot, d):
+        to = self.seat(self.z, self.peer_y(d))
+        if self.y_first:
+            if slot == 0:
+                src, there = self.final, self.place(self.z)
+            else:
+                z = self.z - slot if slot < LINE else self.z + (slot - LINE + 1)
+                src = there = self.place(z)
+        else:
+            src = there = self.final.at[pl.ds(self.y * self.piece, self.piece)]
+        return self.remote(src, there, "share", (slot, d - 1), to)
+
+    def share_all(self):
+        for d in range(1, self.lines):
+            self.share(0, d).start()
+
+    def shared(self):
+        for d in range(1, self.lines):
+            self.share(0, d).wait_recv()
+        self.keep().start()
+        self.spread_start()
+
+    def stages(self, make):
+        def enter():
+            make()
+            if self.y_first:
+                self.swaps()
+            else:
+                self.chain_start()
+
+        def joined():
+            self.join_y()
+            self.chain_start()
+
+        def second():
+            self.chain_hop(2)
+            self.chain_end((1, 2))
+
+        def third():
+            self.chain_hop(3)
+            self.chain_end((0, 3))
+
+        def turn():
+            self.join_y()
+            self.share_all()
+
+        hops = [functools.partial(self.spread_hop, h) for h in range(1, LINE)]
+        chain = [functools.partial(self.chain_hop, 1), second, third]
+        if self.y_first:
+            return [enter, joined] + chain + hops
+        return [enter] + chain + [turn, self.shared] + hops
+
+    def close(self):
+        self.keep().wait()
+        for d in range(1, self.lines):
+            self.swap(d).wait_send()
+            self.share(0, d).wait_send()
+            if self.y_first:
+                self.share(0, d).wait_recv()
+        for h in range(1, LINE):
+            for direction in (1, -1):
+                @pl.when(self.z == (h - 1 if direction > 0 else LINE - h))
+                def _(h=h, direction=direction):
+                    z = h - 1 if direction > 0 else LINE - h
+                    last = LINE - 1 if direction > 0 else 0
+                    for c in range(last, z, -direction):
+                        self.pass_on(c, z, direction, h == 1).wait_send()
+
+                there = self.comes(direction, h - 1) if h > 1 else True
+
+                @pl.when(jnp.logical_and(there, self.goes(direction)))
+                def _(h=h, direction=direction):
+                    self.spread(direction, h).wait_send()
+
+                if self.y_first:
+                    @pl.when(self.comes(direction, h))
+                    def _(h=h, direction=direction):
+                        for d in range(1, self.lines):
+                            copy = self.share(h if direction > 0 else LINE - 1 + h, d)
+                            copy.wait_send()
+                            copy.wait_recv()
+
+
+def sum_rows(jobs, order, lines, peers_head, *refs):
+    (normed, cot, hidden, scale, gain, mix_out, d_gate, d_value, d_state, d_step, grads_v, grads_s, grads_h,
+     gate_w, value_w, out_w, state_w, step_w) = refs[:18]
+    outs, (every, normed_sum, mixed_sum, dots_sum) = refs[18:22], refs[22:26]
+    scratch = refs[26:]
     count = len(jobs)
-    own, y_in, z_in, final = (scratch[k * count : (k + 1) * count] for k in range(4))
-    (own_sem, ys, yr, zs, zr, gzs, gzr, gys, gyr, keep_sem) = scratch[4 * count : 4 * count + 10]
-    (packed, block_own, block_in, normed_own, normed_in, mixed_own, mixed_in, dots_in,
-     local_sem, hs, hr) = scratch[4 * count + 10 :]
-    ins = [packed] + ins
+    y_in, right, left, total, final = (scratch[k * count : (k + 1) * count] for k in range(5))
+    names = ("swap", "right", "left", "spread", "share")
+    pairs = scratch[5 * count : 5 * count + 10]
+    sems = {name: (pairs[2 * k], pairs[2 * k + 1]) for k, name in enumerate(names)}
+    (sems["keep"], packed, out_part, gate_part, value_part, gate_m, value_m, out_m, state_m, step_m,
+     blocks, block_in, normed_part, normed_in, mixed_part, mixed_in, dots, dots_in, gain_part, rest, product,
+     local_sem, hs, hr) = scratch[5 * count + 10 :]
+    parts = [packed, out_part, gate_part, value_part]
+    tokens, features = normed.shape
+    width, channels = features // peers_head, d_gate.shape[1]
+    heads = channels // HEAD
     seq, head = lax.axis_index("seq"), lax.axis_index("head")
-    z, y = seq // lines, seq % lines
+    z, y = seq // lines, lax.rem(seq, lines)
+    work = [
+        Job(j, y_first, parts[which], outs[which], start, rows, lines,
+            y_in[j], right[j], left[j], total[j], final[j], sems, (seq, z, y))
+        for j, (which, start, rows, y_first) in enumerate(jobs)
+    ]
+    shared = [j for j in range(count) if not jobs[j][0]][0]
+
+    loads = [
+        pltpu.make_async_copy(src, dst, local_sem.at[k])
+        for k, (src, dst) in enumerate(
+            ((gate_w, gate_m), (value_w, value_m), (out_w, out_m), (state_w, state_m), (step_w, step_m))
+        )
+    ]
+    for copy in loads:
+        copy.start()
+
     barrier = pltpu.get_barrier_semaphore()
-
-    def at(zz, yy):
-        return {"seq": zz * lines + yy}
-
-    def remote(src, dst, send, recv, peer):
-        return pltpu.make_async_remote_copy(
-            src_ref=src, dst_ref=dst, send_sem=send, recv_sem=recv, device_id=peer, device_id_type=MESH
-        )
-
-    peers = [at(z, lax.rem(y + d, lines)) for d in range(1, lines)]
-    peers += [at(lax.rem(z + d, LINE), y) for d in range(1, LINE)]
+    peers = [{"seq": z * lines + lax.rem(y + d, lines)} for d in range(1, lines)]
     peers += [{"head": lax.rem(head + d, peers_head)} for d in range(1, peers_head)]
     for peer in peers:
         pl.semaphore_signal(barrier, inc=1, device_id=peer, device_id_type=MESH)
-    pl.semaphore_wait(barrier, len(peers))
-
-    width = normed_sum.shape[0]
+    for direction in (1, -1):
+        @pl.when(z < LINE - 1 if direction > 0 else z > 0)
+        def _(direction=direction):
+            pl.semaphore_signal(
+                barrier, inc=1, device_id={"seq": (z + direction) * lines + y}, device_id_type=MESH
+            )
+
+    ends = jnp.logical_or(z == 0, z == LINE - 1)
+
+    @pl.when(ends)
+    def _():
+        pl.semaphore_wait(barrier, len(peers) + 1)
+
+    @pl.when(jnp.logical_not(ends))
+    def _():
+        pl.semaphore_wait(barrier, len(peers) + 2)
+
     block = blocks.shape[1]
 
     def head_copies(kind):
-        copies = []
         for d in range(1, peers_head):
             to = lax.rem(head + d, peers_head)
-            rows = pl.ds(to * width, width)
-            src, dst = (
-                (blocks.at[to], block_in.at[d - 1]),
-                (dots, dots_in.at[d - 1]),
-                (normed.at[rows], normed_in.at[d - 1]),
-                (mixed.at[rows], mixed_in.at[d - 1]),
-                (outs[0].at[pl.ds(0, width)], every.at[head]),
-            )[kind]
-            copies.append(remote(src, dst, hs.at[kind, d - 1], hr.at[kind, d - 1], {"head": to}))
-        return copies
-
-    rows = pl.ds(head * width, width)
-    local_copies = [
-        pltpu.make_async_copy(blocks.at[head], block_own, local_sem.at[0]),
-        pltpu.make_async_copy(tail, packed.at[pl.ds(block, tail.shape[0])], local_sem.at[1]),
-        pltpu.make_async_copy(normed.at[rows], normed_own, local_sem.at[2]),
-        pltpu.make_async_copy(mixed.at[rows], mixed_own, local_sem.at[3]),
-    ]
-
-    sizes = []
-    for which, start, rows in jobs:
-        sizes.append((which, start, rows, rows // lines, rows // lines // LINE))
-
-    def y_copies(j):
-        which, start, rows, part, piece = sizes[j]
-        copies = []
-        for d in range(1, lines):
-            to = lax.rem(y + d, lines)
-            copies.append(
-                remote(
-                    ins[which].at[pl.ds(start + to * part, part)],
-                    y_in[j].at[d - 1],
-                    ys.at[j, d - 1],
-                    yr.at[j, d - 1],
-                    at(z, to),
+            if kind < 4:
+                src = (blocks.at[to], dots, normed_part.at[to], mixed_part.at[to])[kind]
+                dst = (block_in, dots_in, normed_in, mixed_in)[kind].at[d - 1]
+            else:
+                src, dst = outs[0].at[pl.ds(0, width)], every.at[head]
+            yield pltpu.make_async_remote_copy(
+                src_ref=src, dst_ref=dst, send_sem=hs.at[kind, d - 1], recv_sem=hr.at[kind, d - 1],
+                device_id={"head": to}, device_id_type=MESH,
+            )
+
+    def start(copies):
+        for copy in copies:
+            copy.start()
+
+    def received(copies):
+        for copy in copies:
+            copy.wait_recv()
+
+    def outer(left_ref, right_ref, target, start, rows):
+        tall = 128 if rows % 128 == 0 else rows
+        for r in range(start, start + rows, tall):
+            turned = left_ref[:, pl.ds(r, tall)].T
+            target[pl.ds(r, tall)] = jnp.dot(
+                turned, right_ref[...], preferred_element_type=F32
+            ).astype(target.dtype)
+
+    def make(j):
+        which, begin, rows, y_first = jobs[j]
+        if not which:
+            return pack
+        operands = ((mix_out, cot), (normed, d_gate), (normed, d_value))[which - 1]
+        return lambda: outer(*operands, parts[which], begin, rows)
+
+    def over_head(quarter):
+        if quarter == 0:
+            for copy in loads:
+                copy.wait()
+            dots[...] = jnp.zeros_like(dots)
+            gain_part[...] = jnp.zeros_like(gain_part)
+
+        def by_head(h):
+            mine = pl.ds(h * width, width)
+            result = jnp.zeros((tokens, width), F32)
+            for left_ref, right_ref in (
+                (d_gate, gate_m), (d_value, value_m), (d_state, state_m), (d_step, step_m)
+            ):
+                result = result + lax.dot_general(
+                    left_ref[...], right_ref[mine], (((1,), (1,)), ((), ())),
+                    preferred_element_type=F32,
                 )
-            )
-        return copies
-
-    def own_copy(j):
-        which, start, rows, part, piece = sizes[j]
-        return pltpu.make_async_copy(
-            ins[which].at[pl.ds(start + y * part, part)], own[j], own_sem.at[j]
+            product[...] = result
+            mixed_part[h] = jnp.dot(
+                mix_out[...], out_m[:, mine], preferred_element_type=F32
+            ).astype(BF16)
+
+            @pl.loop(0, tokens // Q)
+            def _(c):
+                here = pl.ds(pl.multiple_of(c * Q, Q), Q)
+                result = product[here]
+                normed_part[h, here] = result.astype(BF16)
+                rows = result * hidden[here, mine].astype(F32)
+                gain_part[:, mine] = gain_part[:, mine] + jnp.sum(
+                    rows * scale[here], axis=0, keepdims=True
+                )
+                dot = jnp.sum(rows * gain[:, mine], axis=1, keepdims=True)
+                dot = jnp.broadcast_to(dot, (Q, LANES)).T
+                dots[:, here] = dots[:, here] + dot[:8]
+
+        for h in range(quarter * peers_head // 4, (quarter + 1) * peers_head // 4):
+            by_head(h)
+
+    def over_head_send():
+        states = blocks.shape[2]
+        rest[...] = jnp.zeros_like(rest)
+        rest[0:8] = grads_s[...]
+        for k in range(features // states):
+            rest[8 + k : 9 + k] = gain_part[:, pl.ds(k * states, states)]
+        for h in range(peers_head):
+            turned = normed[:, pl.ds(h * width, width)].T
+            blocks[h, pl.ds(0, width)] = jnp.dot(
+                turned, d_state[...], preferred_element_type=F32
+            ).astype(BF16)
+            blocks[h, pl.ds(width, 16)] = rest[0:16].astype(BF16)
+        for kind in range(4):
+            start(head_copies(kind))
+        steps = lax.dot_general(
+            d_step[...], normed[...], (((0,), (0,)), ((), ())), preferred_element_type=F32
         )
-
-    def z_copies(j):
-        piece = sizes[j][4]
-        copies = []
-        for d in (1, LINE - 1, 2):
-            to = lax.rem(z + d, LINE)
-            copies.append(
-                remote(
-                    own[j].at[pl.ds(to * piece, piece)],
-                    z_in[j].at[d - 1],
-                    zs.at[j, d - 1],
-                    zr.at[j, d - 1],
-                    at(to, y),
-                )
-            )
-        return copies
-
-    def place(j, zz, yy):
-        which, start, rows, part, piece = sizes[j]
-        return outs[which].at[pl.ds(start + yy * part + zz * piece, piece)]
-
-    def gather_z(j):
-        return [
-            remote(final[j], place(j, z, y), gzs.at[j, d - 1], gzr.at[j, d - 1], at(lax.rem(z + d, LINE), y))
-            for d in (1, LINE - 1, 2)
-        ]
-
-    def gather_y(j, d):
-        source = lax.rem(z + LINE - d, LINE)
-        src = final[j] if d == 0 else place(j, source, y)
-        return [
-            remote(
-                src,
-                place(j, source, y),
-                gys.at[j, d, e - 1],
-                gyr.at[j, d, e - 1],
-                at(z, lax.rem(y + e, lines)),
-            )
-            for e in range(1, lines)
-        ]
-
-    def keep(j):
-        return pltpu.make_async_copy(final[j], place(j, z, y), keep_sem.at[j])
-
-    for copy in local_copies + head_copies(0):
-        copy.start()
-    for j in range(count):
-        if jobs[j][0]:
-            own_copy(j).start()
-            for copy in y_copies(j):
-                copy.start()
-    for kind in (1, 2, 3):
-        for copy in head_copies(kind):
-            copy.start()
+        for k in range(features // states):
+            rest[16 + k * heads : 16 + (k + 1) * heads] = steps[:heads, k * states : (k + 1) * states]
+        at = 16 + heads * (features // states)
+        for k in range(0, channels, states):
+            lanes = min(states, channels - k)
+            rest[at : at + 8, 0:lanes] = grads_v[:, pl.ds(k, lanes)]
+            at += 8
+        rest[at : at + 2, 0:LANES] = grads_h[0:2]
+        packed[pl.ds(block, rest.shape[0] - 16)] = rest[16:].astype(BF16)
 
     def pack():
-        local_copies[0].wait()
-        local_copies[1].wait()
-        for copy in head_copies(0):
-            copy.wait_recv()
-
-        def step(i, carry):
-            rows = pl.ds(pl.multiple_of(i * 16, 16), 16)
-            total = block_own[rows].astype(jnp.float32)
-            for d in range(peers_head - 1):
-                total = total + block_in[d, rows].astype(jnp.float32)
-            packed[rows] = total.astype(jnp.bfloat16)
-            return carry
-
-        lax.fori_loop(0, block // 16, step, 0)
-
-    def sum_heads(kind, mine, received, target, k):
-        local_copies[k].wait()
-        for copy in head_copies(kind):
-            copy.wait_recv()
-
-        def step(i, carry):
-            rows = pl.ds(pl.multiple_of(i * 16, 16), 16)
-            total = mine[rows].astype(jnp.float32)
-            for d in range(peers_head - 1):
-                total = total + received[d, rows].astype(jnp.float32)
-            target[rows] = total
-            return carry
-
-        lax.fori_loop(0, width // 16, step, 0)
-
-    def reduce_y(j):
-        if not jobs[j][0]:
-            pack()
-            own_copy(j).start()
-            for copy in y_copies(j):
-                copy.start()
-        own_copy(j).wait()
-        for copy in y_copies(j):
-            copy.wait_recv()
-        part = sizes[j][3]
-        tile = 16 if part % 16 == 0 else 8
-
-        def step(i, carry):
-            rows = pl.ds(pl.multiple_of(i * tile, tile), tile)
-            total = own[j][rows].astype(jnp.float32)
-            for d in range(lines - 1):
-                total = total + y_in[j][d, rows].astype(jnp.float32)
-            own[j][rows] = total.astype(jnp.bfloat16)
-            return carry
-
-        lax.fori_loop(0, part // tile, step, 0)
-        for copy in z_copies(j):
-            copy.start()
-
-    def reduce_z(j):
-        for copy in z_copies(j):
-            copy.wait_recv()
-        piece = sizes[j][4]
-        tile = 16 if piece % 16 == 0 else 8
-        base = z * piece
-
-        def step(i, carry):
-            rows = pl.ds(pl.multiple_of(i * tile, tile), tile)
-            mine = pl.ds(pl.multiple_of(base + i * tile, tile), tile)
-            total = own[j][mine].astype(jnp.float32)
-            for d in range(LINE - 1):
-                total = total + z_in[j][d, rows].astype(jnp.float32)
-            final[j][rows] = total.astype(jnp.bfloat16)
-            return carry
-
-        lax.fori_loop(0, piece // tile, step, 0)
-        keep(j).start()
-        for copy in gather_z(j):
-            copy.start()
-        for copy in gather_y(j, 0):
-            copy.start()
-
-    def forward(j):
-        copies = dict(zip((1, LINE - 1, 2), gather_z(j)))
-        for d in (1, LINE - 1, 2):
-            copies[d].wait_recv()
-            for copy in gather_y(j, d):
-                copy.start()
-
-    for i in range(count + 2):
-        if i < count:
-            reduce_y(i)
-        if 0 <= i - 1 < count:
-            reduce_z(i - 1)
-        if 0 <= i - 2 < count:
-            forward(i - 2)
-    total = dots[...]
-    for d, copy in enumerate(head_copies(1)):
-        copy.wait_recv()
-        total = total + dots_in[d]
-    dots_sum[...] = total
-    sum_heads(2, normed_own, normed_in, normed_sum, 2)
-    sum_heads(3, mixed_own, mixed_in, mixed_sum, 3)
-    for j in sorted(range(count), key=lambda j: jobs[j][0]):
-        keep(j).wait()
-        for copy in y_copies(j) + z_copies(j) + gather_z(j):
-            copy.wait_send()
-        for d in range(LINE):
-            for copy in gather_y(j, d):
-                copy.wait_recv()
-                copy.wait_send()
-        if not jobs[j][0]:
-            mine = pltpu.make_async_copy(outs[0].at[pl.ds(0, width)], every.at[head], local_sem.at[4])
+        received(head_copies(0))
+        others = [(block_in.at[d], 0) for d in range(peers_head - 1)]
+        add_rows((packed, 0), [(blocks.at[head], 0)] + others, block)
+
+    def sum_heads():
+        received(head_copies(1))
+        summed = dots[...]
+        for d in range(peers_head - 1):
+            summed = summed + dots_in[d]
+        dots_sum[...] = summed
+        for kind, mine, boxes, target in (
+            (2, normed_part, normed_in, normed_sum), (3, mixed_part, mixed_in, mixed_sum)
+        ):
+            received(head_copies(kind))
+            others = [(boxes.at[d], 0) for d in range(peers_head - 1)]
+            add_rows((target, 0), [(mine.at[head], 0)] + others, tokens, F32)
+
+    plans = [job.stages(make(job.index)) for job in work]
+    plans.append([functools.partial(over_head, q) for q in range(4)] + [over_head_send, sum_heads])
+    for j, stage in order:
+        plans[j][stage]()
+    for job in sorted(work, key=lambda job: job.index != shared):
+        job.close()
+        if job.index == shared:
+            mine = pltpu.make_async_copy(outs[0].at[pl.ds(0, width)], every.at[head], local_sem.at[0])
             mine.start()
-            for copy in head_copies(4):
-                copy.start()
+            start(head_copies(4))
             mine.wait()
-    for copy in head_copies(4):
-        copy.wait_recv()
+    received(head_copies(4))
     for kind in range(5):
         for copy in head_copies(kind):
             copy.wait_send()
 
 
-def sum_over_seq(arrays, split, blocks, tail, normed, mixed, dots, lines, peers_head, collective_id):
-    bf16, f32 = jnp.bfloat16, jnp.float32
-    width, tokens = normed.shape[0] // peers_head, normed.shape[1]
-    packed = jax.ShapeDtypeStruct((blocks.shape[1] + tail.shape[0], tail.shape[1]), bf16)
+def sum_over_seq(plan, order, values, grads, weights, lines, peers_head, collective_id):
+    normed, d_gate, d_state = values[0], values[6], values[8]
+    tokens, features = normed.shape
+    channels, states, width = d_gate.shape[1], d_state.shape[1], normed.shape[1] // peers_head
+    heads = channels // HEAD
+    shape, dma, vmem = jax.ShapeDtypeStruct, pltpu.SemaphoreType.DMA, pltpu.VMEM
+    extra = heads * (features // states) + 8 * -(-channels // states) + 8
+    total = -(-(width + 16 + extra) // (8 * lines * LINE)) * 8 * lines * LINE
+    whole = [
+        shape((total, states), BF16), shape((channels, features), BF16),
+        shape((features, channels), BF16), shape((features, channels), BF16),
+    ]
     jobs = []
-    for which, (array, parts) in enumerate(zip([packed] + arrays, (1,) + split)):
-        rows = array.shape[0] // parts
-        jobs += [(which, k * rows, rows) for k in range(parts)]
-    jobs = jobs[1:3] + jobs[:1] + jobs[3:]
+    for which, number, parts, y_first in plan:
+        rows = whole[which].shape[0] // parts
+        jobs.append((which, number * rows, rows, y_first))
     count = len(jobs)
-    widths = [([packed] + arrays)[job[0]].shape[1] for job in jobs]
-    scratch = [pltpu.VMEM((job[2] // lines, w), bf16) for job, w in zip(jobs, widths)]
-    scratch += [pltpu.VMEM((lines - 1, job[2] // lines, w), bf16) for job, w in zip(jobs, widths)]
+    groups = [[] for _ in range(5)]
+    for which, start, rows, y_first in jobs:
+        columns = whole[which].shape[1]
+        part, piece = rows // lines, rows // lines // LINE
+        chunk = piece if y_first else rows // LINE
+        sizes = (
+            (lines - 1, part if y_first else piece), (LINE, chunk), (LINE, chunk),
+            (8 if y_first else chunk,), (chunk,),
+        )
+        for group, size in zip(groups, sizes):
+            group.append(vmem(size + (columns,), BF16))
+    scratch = [one for group in groups for one in group]
+    for slots in ((lines - 1,), (LINE,), (LINE,), (2 * LINE - 1,), (2 * LINE - 1, lines - 1)):
+        scratch += [dma((count,) + slots)] * 2
+    others = peers_head - 1
+    scratch += [dma((count,))]
+    scratch += [vmem(one.shape, BF16) for one in whole]
+    scratch += [vmem(one.shape, BF16) for one in weights]
     scratch += [
-        pltpu.VMEM((LINE - 1, job[2] // lines // LINE, w), bf16) for job, w in zip(jobs, widths)
-    ]
-    scratch += [pltpu.VMEM((job[2] // lines // LINE, w), bf16) for job, w in zip(jobs, widths)]
-    dma = pltpu.SemaphoreType.DMA
-    scratch += [
-        dma((count,)),
-        dma((count, lines - 1)),
-        dma((count, lines - 1)),
-        dma((count, LINE - 1)),
-        dma((count, LINE - 1)),
-        dma((count, LINE - 1)),
-        dma((count, LINE - 1)),
-        dma((count, LINE, lines - 1)),
-        dma((count, LINE, lines - 1)),
-        dma((count,)),
-        pltpu.VMEM(packed.shape, bf16),
-        pltpu.VMEM(blocks.shape[1:], bf16),
-        pltpu.VMEM((peers_head - 1,) + blocks.shape[1:], bf16),
-        pltpu.VMEM((width, tokens), bf16),
-        pltpu.VMEM((peers_head - 1, width, tokens), bf16),
-        pltpu.VMEM((width, tokens), bf16),
-        pltpu.VMEM((peers_head - 1, width, tokens), bf16),
-        pltpu.VMEM((peers_head - 1,) + dots.shape, f32),
-        dma((5,)),
-        dma((5, peers_head - 1)),
-        dma((5, peers_head - 1)),
+        vmem((peers_head, width + 16, states), BF16), vmem((others, width + 16, states), BF16),
+        vmem((peers_head, tokens, width), BF16), vmem((others, tokens, width), BF16),
+        vmem((peers_head, tokens, width), BF16), vmem((others, tokens, width), BF16),
+        vmem((8, tokens), F32), vmem((others, 8, tokens), F32), vmem((1, features), F32),
+        vmem((total - width, states), F32), vmem((tokens, width), F32),
+        dma((5,)), dma((5, others)), dma((5, others)),
     ]
     anywhere, inside = pl.BlockSpec(memory_space=pl.ANY), pl.BlockSpec(memory_space=pltpu.VMEM)
-    shape = jax.ShapeDtypeStruct
+    operands = list(values) + list(grads)
     return pl.pallas_call(
-        functools.partial(sum_rows, jobs, lines, peers_head, len(arrays)),
-        out_shape=[packed]
-        + [shape(array.shape, bf16) for array in arrays]
-        + [shape((peers_head, width, tail.shape[1]), bf16)]
-        + [shape((width, tokens), f32)] * 2
-        + [shape(dots.shape, f32)],
-        in_specs=[anywhere] * (len(arrays) + 4) + [inside],
-        out_specs=[anywhere] * (len(arrays) + 2) + [inside] * 3,
+        functools.partial(sum_rows, jobs, order, lines, peers_head),
+        out_shape=whole
+        + [shape((peers_head, width, states), BF16)]
+        + [shape((tokens, width), F32)] * 2
+        + [shape((8, tokens), F32)],
+        in_specs=[inside] * len(operands) + [anywhere] * len(weights),
+        out_specs=[anywhere] * 5 + [inside] * 3,
         scratch_shapes=scratch,
         compiler_params=pltpu.CompilerParams(
-            collective_id=collective_id, has_side_effects=True, vmem_limit_bytes=60 * 1024 * 1024
+            collective_id=collective_id, has_side_effects=True, vmem_limit_bytes=61 * 1024 * 1024
         ),
-    )(*arrays, blocks, tail, normed, mixed, dots)
+    )(*operands, *weights)
+
+
+PLAN = (
+    (1, 0, 3, True), (1, 1, 3, False), (1, 2, 3, True), (2, 0, 3, False),
+    (2, 1, 3, True), (2, 2, 3, True), (3, 0, 3, True), (0, 0, 1, False),
+    (3, 1, 3, True), (3, 2, 3, True),
+)
+ORDER = (
+    (2, 0), (1, 0), (4, 0), (1, 1), (2, 1), (1, 2), (5, 0), (4, 1), (2, 2), (10, 0),
+    (3, 0), (0, 0), (4, 2), (2, 3), (1, 3), (2, 4), (4, 3), (10, 1), (3, 1), (0, 1),
+    (1, 4), (2, 5), (3, 2), (4, 4), (1, 5), (10, 2), (6, 0), (5, 1), (2, 6), (9, 0),
+    (0, 2), (10, 3), (1, 6), (10, 4), (3, 3), (4, 5), (6, 1), (0, 3), (1, 7), (3, 4),
+    (6, 2), (2, 7), (0, 4), (4, 6), (1, 8), (5, 2), (8, 0), (9, 1), (6, 3), (0, 5),
+    (5, 3), (3, 5), (4, 7), (9, 2), (0, 6), (7, 0), (5, 4), (3, 6), (9, 3), (6, 4),
+    (8, 1), (0, 7), (6, 5), (7, 1), (8, 2), (9, 4), (7, 2), (5, 5), (7, 3), (6, 6),
+    (10, 5), (6, 7), (9, 5), (8, 3), (7, 4), (5, 6), (3, 7), (9, 6), (8, 4), (5, 7),
+    (8, 5), (9, 7), (7, 5), (8, 6), (3, 8), (7, 6), (8, 7), (7, 7), (7, 8),
+)
 
 
 def contract_rows(left, right):
@@ -1134,80 +1334,36 @@
         mix_gain[None, :],
         collective_id=2,
     )
-    half = features // 2
-    out_part = jnp.concatenate(
-        [contract_rows(mix_out, cot_full[:, :half]), contract_rows(mix_out, cot_full[:, half:])]
-    ).astype(BF16)
-    gate_part = contract_rows(normed, d_gate).astype(BF16)
-    value_part = contract_rows(normed, d_value).astype(BF16)
-    state_part = contract_rows(normed, d_state)
-    step_part = contract_rows(normed, d_step)[:, :heads]
-    normed_part = (
-        contract_cols(gate_weight, d_gate)
-        + contract_cols(value_weight, d_value)
-        + contract_cols(state_weight, d_state)
-        + contract_cols(step_wide, d_step)
-    )
-    mixed_part = lax.dot_general(
-        out_weight, mix_out, (((0,), (1,)), ((), ())), preferred_element_type=F32
-    )
-    rows_t = rows_full.T
-    weighted = normed_part * rows_t
-    dots = jnp.sum(weighted * gain_full.T, axis=0)
-    gain_part = jnp.sum(weighted * scale_in.T, axis=1)
-    dots = jnp.broadcast_to(dots[None, :], (8, tokens))
-    state_size = d_state.shape[1]
-    shared = jnp.concatenate([grads_s[:5], gain_part.reshape(-1, state_size)])
-    shared = jnp.pad(shared, ((0, 16 - shared.shape[0]), (0, 0)))
-    blocks = jnp.concatenate(
-        [
-            state_part.reshape(peers_head, width, state_size),
-            jnp.broadcast_to(shared[None], (peers_head, 16, state_size)),
-        ],
-        axis=1,
-    ).astype(BF16)
-    own = (
-        step_part,
-        grads_v[:4],
-        grads_v[4],
-        grads_h[0, :heads],
-        grads_h[1, :heads],
-        jnp.sum(grads_v[6].reshape(heads, HEAD), axis=1),
-        grads_v[5],
-    )
-    packed = jnp.concatenate([jnp.reshape(part, (-1,)) for part in own])
-    tail_rows = width // 3 - 16
-    packed = jnp.pad(packed, (0, tail_rows * state_size - packed.size))
-    packed = packed.reshape(tail_rows, state_size).astype(BF16)
     extra, out_sum, gate_sum, value_sum, state_sum, normed_sum, mixed_sum, dot_sum = sum_over_seq(
-        [out_part, gate_part, value_part],
-        (3, 3, 3),
-        blocks,
-        packed,
-        normed_part.astype(BF16),
-        mixed_part.astype(BF16),
-        dots,
+        PLAN,
+        ORDER,
+        (normed, cot_full, hidden_full, scale_in, gain_full, mix_out, d_gate, d_value, d_state, d_step),
+        (grads_v, grads_s, grads_h),
+        (gate_weight, value_weight, out_weight, state_weight, step_wide),
         count // LINE,
         peers_head,
         3,
     )
     own_rows = hidden_in.astype(F32)
-    block_out = (own_rows + mixed_sum.T).astype(BF16)
+    block_out = (own_rows + mixed_sum).astype(BF16)
     delta_hidden = (
         cotangent.astype(F32)
-        + scale_in * (normed_sum.T * norm_gain.astype(F32)[None, :])
+        + scale_in * (normed_sum * norm_gain.astype(F32)[None, :])
         - own_rows * scale_in**3 * (dot_sum[0] / features)[:, None]
     )
     extra = extra[width:].astype(F32)
+    states = extra.shape[1]
     norm_sum = lax.dynamic_slice_in_dim(
-        extra[5 : 5 + features // state_size].reshape(-1), lax.axis_index("head") * width, width, 0
+        extra[8 : 8 + features // states].reshape(-1), lax.axis_index("head") * width, width, 0
     )
-    packed = extra[16:].reshape(-1)
-    pieces, start = [], 0
-    for part in own:
-        pieces.append(jnp.reshape(packed[start : start + part.size], part.shape))
-        start += part.size
-    step_sum, filter_sum, offset_sum, bias_sum, decay_sum, skip_sum, gain_sum = pieces
+    tiles = features // states
+    step_sum = extra[16 : 16 + heads * tiles].reshape(tiles, heads, states)
+    step_sum = jnp.transpose(step_sum, (0, 2, 1)).reshape(features, heads)
+    at = 16 + heads * tiles
+    wide = -(-channels // states)
+    channel_sum = extra[at : at + 8 * wide].reshape(wide, 8, states)
+    channel_sum = jnp.transpose(channel_sum, (1, 0, 2)).reshape(8, wide * states)[:, :channels]
+    head_sum = extra[at + 8 * wide : at + 8 * wide + 2, :heads]
     return (
         block_out,
         delta_hidden,
@@ -1215,16 +1371,16 @@
         gate_sum.astype(F32),
         value_sum.astype(F32),
         step_sum,
-        state_sum.reshape(features, state_size).astype(F32),
-        filter_sum,
-        offset_sum,
+        state_sum.reshape(features, states).astype(F32),
+        channel_sum[:4],
+        channel_sum[4],
         extra[:4],
         extra[4],
-        bias_sum,
-        decay_sum,
-        skip_sum,
-        gain_sum,
-        jnp.concatenate(jnp.split(out_sum, 2, axis=0), axis=1).astype(F32),
+        head_sum[0],
+        head_sum[1],
+        jnp.sum(channel_sum[6].reshape(heads, HEAD), axis=1),
+        channel_sum[5],
+        out_sum.astype(F32),
     )
 
 

time: 397 us -> 288 us (0.73)
  Pallas kernels: 324 us -> 245 us
  matrix products: 32.4 us -> 12.1 us
  local copies, waits for them, and re-layouts: 22.1 us -> 13 us
    pallas_call x1, Pallas kernels: 230 us -> 151 us  [sum_over_seq(): pl.pallas_call(functools.partial(sum_rows, jobs, order, lines, peers_head...]
    dot_general x7 -> x0, matrix products: 12.3 us -> none  [the longest x6 9.62 us: contract_rows(): lax.dot_general(left, right, (((0,), (0,)), ((), ())), preferred_element_...]
    dot_general x5 -> x1, matrix products: 9.66 us -> 2.55 us  [contract_cols(): lax.dot_general(left, right, (((1,), (1,)), ((), ())), preferred_element_...]
where the time goes in v3:
time: 288 us
  Pallas kernels  245 us (85%)
  other arithmetic  16.9 us (6%)
  local copies, waits for them, and re-layouts  13 us (5%)
  matrix products  12.1 us (4%)
    pallas_call x1, Pallas kernels, sum_over_seq(): pl.pallas_call(functools.partial(sum_rows, jobs, order, lines, peers_head...  151 us
    pallas_call x1, Pallas kernels, mix(): pl.pallas_call(functools.partial(mixer_kernel, count, peers_head, inner),...  65.7 us
    pallas_call x1, Pallas kernels, gather_heads(): pl.pallas_call(functools.partial(gather_kernel, peers_head, flat, count),...  28.5 us
    dot_general x4, matrix products, project(): return jnp.dot(normed, weight, preferred_element_type=F32)  9.52 us

profile of v3, /device:TPU:0, one launch (start us, length us, event | category | flops | bytes accessed | tf_op | source)
XLA Modules:
  0.0 287.6 jit_solution(8859501856250393755)
XLA Ops:
  0.6 1.3 broadcast_in_dim.27.refs_2_
  1.9 28.5 %shard_map.288 = (bf16[512,1536]{1,0:T(8,128)(2,1)}, bf16[512,1536]{1,0:T(8,128)(2,1)}, f32[8,1536]{1,0:T(8,128)}) custom-call(bf16[512,384]{1,0:T(8,128)(2,1)} %refs_0_.1, bf16[512,384]{1,0:T(8,128)(2,1)} %refs_1_.1, f32[8,384]{1,0:T(8,128)} %broadcast_in_dim.27.refs_2_), custom_call_target="tpu_custom_call" | custom-call | tf_op jit(solution)/shard_map/pallas_call | solution.py:82
  30.4 1.9 fusion
  32.3 1.4 fusion.8
  33.7 0.0 copy-done.1
  33.7 0.4 fusion.2.refs_0_
  34.2 0.4 copy-done.13
  34.5 0.2 copy.36
  34.8 1.3 fusion.6.t_in
  36.1 4.3 %fusion.10.v_in = f32[512,768]{1,0:T(8,128)} fusion(bf16[512,1536]{1,0:T(8,128)(2,1)S(1)} %fusion.2.refs_0_, bf16[1536,768]{1,0:T(8,128)(2,1)} %refs_14_.1), kind=kOutput, calls=%fused_computation.29 | convolution fusion | flops 1207959552 | bytes 5505024 | tf_op jit(solution)/shard_map/dot_general | solution.py:1310
  40.4 2.5 fusion.12.g_in
  42.9 0.0 copy-done.2
  42.9 1.4 fusion.11.s_in
  44.3 0.0 copy-done.9
  44.3 0.5 copy-done.6
  44.8 0.0 copy-start.15
  44.8 2.6 fusion.13.d_mix
  47.4 0.0 copy-done.19
  47.4 0.5 pad_bitcast_fusion
  47.9 0.1 broadcast_in_dim.32
  48.0 0.7 broadcast_in_dim_reshape.3.skip
  48.6 0.0 copy-done.14
  48.6 0.6 broadcast_in_dim.28.off_v
  49.2 0.0 copy-done.15
  49.2 0.6 broadcast_in_dim.33.gain
  49.8 65.7 %shard_map.289 = (bf16[512,768]{1,0:T(8,128)(2,1)}, bf16[512,768]{1,0:T(8,128)(2,1)}, bf16[512,768]{1,0:T(8,128)(2,1)}, bf16[512,256]{1,0:T(8,128)(2,1)}, bf16[5...) custom-call(s32[4]{0:T(128)} %lengths.1, f32[512,768]{1,0:T(8,128)} %fusion.10.v_in, ...), custom_call_target="tpu_custom_call" | custom-call | tf_op jit(solution)/shard_map/pallas_call | solution.py:739
  115.5 0.9 copy.37.refs_3_
  116.3 0.8 pad.11.refs_17_
  117.2 150.6 %shard_map.290 = (bf16[512,256]{1,0:T(8,128)(2,1)}, bf16[768,1536]{1,0:T(8,128)(2,1)}, bf16[1536,768]{1,0:T(8,128)(2,1)}, bf16[1536,768]{1,0:T(8,128)(2,1)}, bf1...) custom-call(bf16[512,1536]{1,0:T(8,128)(2,1)} %copy-done, ...), custom_call_target="tpu_custom_call" | custom-call | tf_op jit(solution)/shard_map/pallas_call | solution.py:1234
  267.8 4.4 %convert_element_type.49 = f32[1536,768]{1,0:T(8,128)} convert(bf16[1536,768]{1,0:T(8,128)(2,1)} %get-tuple-element.50) | non-fusion elementwise | flops 1179648 | bytes 7077888 | tf_op jit(solution)/shard_map/convert_element_type | solution.py:1371
  272.2 0.0 copy-done.4
  272.2 2.5 convert_element_type.50
  274.7 2.8 convert_element_type.53
  277.6 1.3 bitcast_convert_fusion
  278.9 0.7 slice_multiply_fusion
  279.7 0.1 copy-done.11
  279.8 1.4 fusion.5
  281.1 0.8 slice_convert_fusion
  282.1 0.7 copy.39
  282.8 0.1 reshape_squeeze.3
  282.9 0.6 reduce_sum.19
  283.5 0.6 squeeze.16
  284.1 0.6 squeeze.20
  284.7 0.6 slice.69
  285.3 0.7 dynamic_slice.3
  286.0 0.6 slice.71
  286.5 0.5 slice_bitcast_fusion.1
  287.1 0.6 slice.72
  (39 shorter events, 0.2 us)
Async XLA Ops:
  30.4 3.3 %copy-start.1 = (bf16[512,1536]{1,0:T(8,128)(2,1)S(1)}, bf16[512,1536]{1,0:T(8,128)(2,1)}, u32[]{:S(2)}) copy-start(bf16[512,1536]{1,0:T(8,128)(2,1)} %get-tuple-element.35.refs_2_) | copy-start | bytes 4718596
  33.7 0.8 copy-start.13
  34.5 8.4 %copy-start = (bf16[512,1536]{1,0:T(8,128)(2,1)}, bf16[512,1536]{1,0:T(8,128)(2,1)S(1)}, u32[]{:S(2)}) copy-start(bf16[512,1536]{1,0:T(8,128)(2,1)S(1)} %fusion.2.refs_0_) | copy-start | bytes 4718596
  36.1 4.3 %copy-start.5 = (bf16[1536,768]{1,0:T(8,128)(2,1)S(1)}, bf16[1536,768]{1,0:T(8,128)(2,1)}, u32[]{:S(2)}) copy-start(bf16[1536,768]{1,0:T(8,128)(2,1)} %refs_13_.1) | copy-start | bytes 7077892
  40.4 2.5 copy-start.2
  40.4 3.9 %copy-start.9 = (bf16[512,1536]{1,0:T(8,128)(2,1)S(1)}, bf16[512,1536]{1,0:T(8,128)(2,1)}, u32[]{:S(2)}) copy-start(bf16[512,1536]{1,0:T(8,128)(2,1)} %get-tuple-element.37.refs_1_) | copy-start | bytes 4718596
  42.9 1.9 copy-start.6
  44.8 2.6 copy-start.18
  44.8 2.6 copy-start.19
  44.8 3.1 %copy-start.17 = (f32[12]{0:T(128)S(1)}, f32[12]{0:T(128)}, u32[]{:S(2)}) copy-start(f32[12]{0:T(128)} %param.29) | copy-start | bytes 148
  44.8 3.8 %copy-start.14 = (f32[768]{0:T(1024)S(1)}, f32[768]{0:T(1024)}, u32[]{:S(2)}) copy-start(f32[768]{0:T(1024)} %param.24) | copy-start | bytes 9220
  44.8 4.4 %copy-start.15 = (f32[768]{0:T(1024)S(1)}, f32[768]{0:T(1024)}, u32[]{:S(2)}) copy-start(f32[768]{0:T(1024)} %param.30) | copy-start | bytes 9220
  267.8 4.4 %copy-start.4 = (bf16[1536,768]{1,0:T(8,128)(2,1)S(1)}, bf16[1536,768]{1,0:T(8,128)(2,1)}, u32[]{:S(2)}) copy-start(bf16[1536,768]{1,0:T(8,128)(2,1)} %get-tuple-element.51) | copy-start | bytes 7077892
  272.2 2.5 copy-start.3
  274.7 2.9 copy-start.12
  277.6 2.1 copy-start.16
  277.6 2.1 copy-start.7
  277.6 2.1 copy-start.8
  277.6 2.1 copy-start.10
  277.6 2.2 copy-start.11

commit v4 on v2

v4 whole, which is shorter than its diff:
```python
import functools

import jax
import jax.numpy as jnp
from jax import lax
from jax.experimental import pallas as pl
from jax.experimental.pallas import tpu as pltpu
from jax.sharding import PartitionSpec as P

MESH = pl.DeviceIdType.MESH
F32, BF16 = jnp.float32, jnp.bfloat16
HIGH = lax.Precision.HIGHEST
EPS = 1e-05
Q = 128
LANES = 128
HEAD = 64
SUB = 8
FAR = -1e30
LINE = 4


def add_rows(target, terms, rows, dtype=BF16):
    tile = next(t for t in (32, 16, 8) if rows % t == 0)

    @pl.loop(0, rows // tile)
    def _(i):
        def at(start):
            return pl.ds(pl.multiple_of(start + i * tile, 8), tile)

        total = terms[0][0][at(terms[0][1])].astype(F32)
        for ref, start in terms[1:]:
            total = total + ref[at(start)].astype(F32)
        target[0][at(target[1])] = total.astype(dtype)


def outer(left_ref, rights, target, start, rows):
    tall = 128 if rows % 128 == 0 else rows
    for r in range(start, start + rows, tall):
        turned = left_ref[:, pl.ds(r, tall)].T
        for n, right_ref in enumerate(rights):
            columns = right_ref.shape[1]
            target[pl.ds(r, tall), pl.ds(n * columns, columns)] = jnp.dot(
                turned, right_ref[...], preferred_element_type=F32
            ).astype(target.dtype)


class Job:
    def __init__(self, index, y_first, src, dst, start, rows, lines, y_in, right, left, total, final, sems, where, mode=0):
        self.index, self.y_first, self.src, self.dst, self.start = index, y_first, src, dst, start
        self.lines, self.y_in, self.right, self.left = lines, y_in, right, left
        self.total, self.final = total, final
        self.sems, self.mode = sems, mode
        self.seq, self.z, self.y = where
        self.part = rows // lines
        self.chunk = rows // lines // LINE if y_first else rows // LINE
        self.piece = rows // lines // LINE
        self.rows = rows
        self.base = 0 if mode == 2 else start + self.y * self.part if y_first else start

    def remote(self, src, dst, name, slot, device):
        send, recv = self.sems[name]
        return pltpu.make_async_remote_copy(
            src_ref=src, dst_ref=dst, send_sem=send.at[(self.index,) + slot],
            recv_sem=recv.at[(self.index,) + slot], device_id={"seq": device}, device_id_type=MESH,
        )

    def seat(self, z, y):
        return z * self.lines + y

    def peer_y(self, d):
        return lax.rem(self.y + d, self.lines)

    def swap(self, d):
        to = self.peer_y(d)
        if self.y_first:
            src = self.src.at[pl.ds(self.start + to * self.part, self.part)]
        else:
            src = self.total.at[pl.ds(to * self.piece, self.piece)]
        return self.remote(src, self.y_in.at[d - 1], "swap", (d - 1,), self.seat(self.z, to))

    def swaps(self):
        for d in range(1, self.lines):
            self.swap(d).start()

    def join_y(self):
        for d in range(1, self.lines):
            self.swap(d).wait_recv()
        others = [(self.y_in.at[d], 0) for d in range(self.lines - 1)]
        if self.y_first:
            target = (self.final, 0) if self.mode == 1 else (self.src, self.base)
            add_rows(target, [(self.src, self.base)] + others, self.part)
        else:
            mine = self.y * self.piece
            add_rows((self.final, mine), [(self.total, mine)] + others, self.piece)

    def pass_on(self, c, z, direction, first):
        box = self.right if direction > 0 else self.left
        src = self.src.at[pl.ds(self.base + c * self.chunk, self.chunk)] if first else box.at[c]
        name = "right" if direction > 0 else "left"
        return self.remote(src, box.at[c], name, (c,), self.seat(z + direction, self.y))

    def come(self, c, direction):
        box = self.right if direction > 0 else self.left
        return self.remote(box.at[c], box.at[c], "right" if direction > 0 else "left", (c,), self.seq)

    def chain_start(self):
        @pl.when(self.z == 0)
        def _():
            for c in (3, 2, 1):
                self.pass_on(c, 0, 1, True).start()

        @pl.when(self.z == 3)
        def _():
            for c in (0, 1, 2):
                self.pass_on(c, 3, -1, True).start()

    def chain_hop(self, h):
        for z, direction, last in ((h, 1, 3), (3 - h, -1, 0)):
            box = self.right if direction > 0 else self.left

            @pl.when(self.z == z)
            def _(z=z, direction=direction, last=last, box=box):
                for c in range(last, z - direction, -direction):
                    self.come(c, direction).wait_recv()
                    if c != z:
                        add_rows((box.at[c], 0), [(box.at[c], 0), (self.src, self.base + c * self.chunk)], self.chunk)
                        self.pass_on(c, z, direction, False).start()

    def chain_end(self, seats):
        for z in seats:
            @pl.when(self.z == z)
            def _(z=z):
                terms = [(self.src, self.base + z * self.chunk)]
                if z > 0:
                    terms.append((self.right.at[z], 0))
                if z < LINE - 1:
                    terms.append((self.left.at[z], 0))
                add_rows((self.final if self.y_first else self.total, 0), terms, self.chunk)
                self.chain_done()

    def chain_done(self):
        if self.y_first:
            self.keep().start()
            self.spread_start()
            for d in range(1, self.lines):
                self.share(0, d).start()
        else:
            self.swaps()

    def place(self, z):
        first = self.y * self.part if self.y_first else 0
        return self.dst.at[pl.ds(self.start + first + z * self.chunk, self.chunk)]

    def keep(self):
        return pltpu.make_async_copy(self.final, self.place(self.z), self.sems["keep"].at[self.index])

    def spread(self, direction, h):
        src = self.final if h == 1 else self.place(self.z - direction * (h - 1))
        slot = h if direction > 0 else LINE - 1 + h
        device = self.seat(self.z + direction, self.y)
        return self.remote(src, self.place(self.z - direction * (h - 1)), "spread", (slot,), device)

    def spread_from(self, direction, h):
        slot = h if direction > 0 else LINE - 1 + h
        there = self.place(self.z - direction * h)
        return self.remote(there, there, "spread", (slot,), self.seq)

    def goes(self, direction):
        return self.z < LINE - 1 if direction > 0 else self.z > 0

    def comes(self, direction, h):
        return self.z >= h if direction > 0 else self.z < LINE - h

    def spread_start(self):
        for direction in (1, -1):
            @pl.when(self.goes(direction))
            def _(direction=direction):
                self.spread(direction, 1).start()

    def spread_hop(self, h):
        for direction in (1, -1):
            @pl.when(self.comes(direction, h))
            def _(direction=direction):
                self.spread_from(direction, h).wait_recv()
                if h < LINE - 1:
                    @pl.when(self.goes(direction))
                    def _():
                        self.spread(direction, h + 1).start()

                if self.y_first:
                    for d in range(1, self.lines):
                        self.share(h if direction > 0 else LINE - 1 + h, d).start()

    def share(self, slot, d):
        to = self.seat(self.z, self.peer_y(d))
        if self.y_first:
            if slot == 0:
                src, there = self.final, self.place(self.z)
            else:
                z = self.z - slot if slot < LINE else self.z + (slot - LINE + 1)
                src = there = self.place(z)
        else:
            src = there = self.final.at[pl.ds(self.y * self.piece, self.piece)]
        return self.remote(src, there, "share", (slot, d - 1), to)

    def share_all(self):
        for d in range(1, self.lines):
            self.share(0, d).start()

    def shared(self):
        for d in range(1, self.lines):
            self.share(0, d).wait_recv()
        self.keep().start()
        self.spread_start()

    def stages(self, make):
        def enter():
            make()
            if self.y_first:
                self.swaps()
            else:
                self.chain_start()

        def joined():
            self.join_y()
            self.chain_start()

        def second():
            self.chain_hop(2)
            self.chain_end((1, 2))

        def third():
            self.chain_hop(3)
            self.chain_end((0, 3))

        def turn():
            self.join_y()
            self.share_all()

        hops = [functools.partial(self.spread_hop, h) for h in range(1, LINE)]
        chain = [functools.partial(self.chain_hop, 1), second, third]
        if self.mode == 1:
            return [enter, self.join_y]
        if self.mode == 2:
            return [self.chain_start] + chain + hops
        if self.y_first:
            return [enter, joined] + chain + hops
        return [enter] + chain + [turn, self.shared] + hops

    def close_chain(self):
        for h in range(1, LINE):
            for direction in (1, -1):
                @pl.when(self.z == (h - 1 if direction > 0 else LINE - h))
                def _(h=h, direction=direction):
                    z = h - 1 if direction > 0 else LINE - h
                    last = LINE - 1 if direction > 0 else 0
                    for c in range(last, z, -direction):
                        self.pass_on(c, z, direction, h == 1).wait_send()

    def arrived(self):
        if not self.y_first:
            return
        for d in range(1, self.lines):
            self.share(0, d).wait_recv()
        for h in range(1, LINE):
            for direction in (1, -1):
                @pl.when(self.comes(direction, h))
                def _(h=h, direction=direction):
                    for d in range(1, self.lines):
                        self.share(h if direction > 0 else LINE - 1 + h, d).wait_recv()

    def close(self, kept=False):
        if self.mode < 2:
            for d in range(1, self.lines):
                self.swap(d).wait_send()
        if self.mode == 1:
            return
        self.close_chain()
        if not kept:
            self.keep().wait()
            self.arrived()
        for d in range(1, self.lines):
            self.share(0, d).wait_send()
        for h in range(1, LINE):
            for direction in (1, -1):
                there = self.comes(direction, h - 1) if h > 1 else True

                @pl.when(jnp.logical_and(there, self.goes(direction)))
                def _(h=h, direction=direction):
                    self.spread(direction, h).wait_send()

                if self.y_first:
                    @pl.when(self.comes(direction, h))
                    def _(h=h, direction=direction):
                        for d in range(1, self.lines):
                            self.share(h if direction > 0 else LINE - 1 + h, d).wait_send()


def job_scratch(jobs, widths, lines, gathered=0, swaps=False):
    dma, groups = pltpu.SemaphoreType.DMA, [[] for _ in range(5)]
    for j, (which, start, rows, y_first) in enumerate(jobs):
        part, piece = rows // lines, rows // lines // LINE
        chunk = piece if y_first else rows // LINE
        sizes = (
            (lines - 1, part if y_first else piece), (LINE, chunk), (LINE, chunk),
            (8 if y_first else chunk,), (chunk,),
        )
        if j < gathered:
            sizes = ((1, 8),) + sizes[1:]
        if swaps:
            sizes = sizes[:1] + ((1, 8), (1, 8), (8,), (8,))
        for group, size in zip(groups, sizes):
            group.append(pltpu.VMEM(size + (widths[which],), BF16))
    scratch = [one for group in groups for one in group]
    for slots in ((lines - 1,), (LINE,), (LINE,), (2 * LINE - 1,), (2 * LINE - 1, lines - 1)):
        scratch += [dma((len(jobs),) + slots)] * 2
    return scratch


def rows_of(plan, heights):
    jobs = []
    for which, number, parts, y_first in plan:
        rows = heights[which] // parts
        jobs.append((which, number * rows, rows, y_first))
    return jobs


def mm(left, right, contract=((1,), (0,)), precision=None):
    return lax.dot_general(
        left, right, (contract, ((), ())), precision=precision, preferred_element_type=F32
    )


def split(value):
    high = value.astype(BF16)
    return high, (value - high.astype(F32)).astype(BF16)


def twice(value, axis):
    return jnp.concatenate([value, value], axis=axis)


def sigmoid(v):
    return 1.0 / (1.0 + jnp.exp(-v))


def mixer_kernel(
    count, peers_head, inner, jobs, waves,
    lengths, hidden_in, cot_in, gate_w, value_w, state_w, out_w, step_w,
    taps_v, taps_s, gain_in, off_v_in, gain_mix_in, off_s_in, bias_own, rate_own, skip_own,
    normed, scale_in, hidden, cot, gain_full, mix_out, d_gate, d_value, d_state, d_step,
    grads_v, grads_s, grads_h, *refs,
):
    finals, refs = refs[: len(jobs)], refs[len(jobs) :]
    (
    v_in, s_in, g_in, t_in, d_mix, gate_m, value_m, state_m, out_m, step_m, off_v, gain, off_s, bias_in, rate_in, skip_in, gain_own, bias, rate, skip,
    edge_v, edge_s, first_v, first_s, val, inf, inf_low, rea, rea_low, slope_v, slope_s, segs, mask_f, mask_b,
    step, sig, logs, run, run_t, tail, into, passing, pair, scaled, scaled_low, out, inter, d_u,
    states, starts, starts_low, before, total, factors, push, got, kept, prefix, spread_sum,
    rows_out, rows_in, pre_v, pre_s, back_v, back_s, back_in_v, back_in_s,
    local_sem, gather_send, gather_recv, edge_sems, p_send, p_recv, carry_send, carry_recv, row_send, row_recv, back_sems, parts_out, parts_gate,
    ) = refs[:80]
    rest = refs[80:]
    tokens, channels = v_in.shape
    chunks, pairs, heads = tokens // Q, channels // LANES, channels // HEAD
    seq, head = lax.axis_index("seq"), lax.axis_index("head")
    window = count // 2
    steps = []
    width = window // 2
    while width >= 2:
        steps.append(width)
        width //= 2

    def remote(src, dst, send, recv, device):
        return pltpu.make_async_remote_copy(
            src_ref=src, dst_ref=dst, send_sem=send, recv_sem=recv, device_id=device, device_id_type=MESH
        )

    lines, held_jobs = count // LINE, len(jobs)
    z, y = seq // lines, lax.rem(seq, lines)
    pairs_of = rest[5 * held_jobs :]
    sems = {
        name: (pairs_of[2 * k], pairs_of[2 * k + 1])
        for k, name in enumerate(("swap", "right", "left", "spread", "share"))
    }
    work = [
        Job(j, y_first, (None, parts_out, parts_gate)[which], None, start, rows, lines,
            *(rest[k * held_jobs + j] for k in range(4)), finals[j], sems, (seq, z, y), 1)
        for j, (which, start, rows, y_first) in enumerate(jobs)
    ]

    def make(j):
        which, start, rows, y_first = jobs[j]
        if which == 1:
            return lambda: outer(mix_out, [cot.at[h] for h in range(peers_head)], parts_out, start, rows)
        return lambda: outer(normed, [d_gate], parts_gate, start, rows)

    plans = [job.stages(make(job.index)) for job in work]
    turns = list(waves)

    def wave():
        if turns:
            for j, stage in turns.pop(0):
                plans[j][stage]()

    barrier = pltpu.get_barrier_semaphore()
    others = [{"seq": lax.rem(seq + d, count)} for d in range(1, count)]
    others += [{"head": lax.rem(head + d, peers_head)} for d in range(1, peers_head)]
    for other in others:
        pl.semaphore_signal(barrier, inc=1, device_id=other, device_id_type=MESH)
    pl.semaphore_wait(barrier, len(others))

    def edge_copies():
        there = {"seq": lax.rem(seq + 1, count)}
        return [
            remote(v_in.at[pl.ds(tokens - SUB, SUB)], edge_v, edge_sems.at[0], edge_sems.at[1], there),
            remote(s_in.at[pl.ds(tokens - SUB, SUB)], edge_s, edge_sems.at[2], edge_sems.at[3], there),
        ]

    chips = peers_head // 2
    x, core = head // 2, lax.rem(head, 2)
    gain_own[...] = jnp.broadcast_to(gain_in[...].astype(F32).reshape(1, -1), gain_own.shape)
    sources, boxes = (hidden_in, gain_own, cot_in), (hidden, gain_full, cot)

    def gather(k, slot):
        mine, src = head, sources[k]
        if slot == 0 or slot >= chips:
            device = x * 2 + (1 - core)
        else:
            device = lax.rem(x + slot, chips) * 2 + core
        if slot >= chips:
            mine = lax.rem(x + 2 * chips - 1 - slot, chips) * 2 + core
            src = boxes[k].at[mine]
        return remote(
            src, boxes[k].at[mine], gather_send.at[k, slot], gather_recv.at[k, slot], {"head": device}
        )

    def gather_start(k):
        for slot in range(1, chips):
            gather(k, slot).start()
        gather(k, 0).start()

    def gather_forward(k):
        for slot in range(1, chips):
            gather(k, slot).wait_recv()
            gather(k, chips - 1 + slot).start()

    def gather_end(k):
        own[k].wait()
        gather(k, 0).wait_recv()
        for slot in range(chips, 2 * chips - 1):
            gather(k, slot).wait_recv()

    weights = [
        pltpu.make_async_copy(src, dst, local_sem.at[n])
        for n, (src, dst) in enumerate(
            (
                (value_w, value_m), (state_w, state_m), (step_w, step_m), (gate_w, gate_m), (out_w, out_m),
                (off_v_in, off_v.at[0]), (gain_mix_in, gain.at[0]), (off_s_in, off_s.at[0]),
                (bias_own, bias_in.at[0]), (rate_own, rate_in.at[0]), (skip_own, skip_in.at[0]),
            )
        )
    ]
    own = [
        pltpu.make_async_copy(sources[k], boxes[k].at[head], local_sem.at[len(weights) + k]) for k in range(3)
    ]
    gather_start(0)
    gather_start(1)
    for copy in own[:2] + weights:
        copy.start()
    gather_start(2)
    own[2].start()

    lane = lax.broadcasted_iota(jnp.int32, (Q, LANES), 1)
    row = lax.broadcasted_iota(jnp.int32, (Q, LANES), 0)
    left = lane < HEAD

    anchor = seq * tokens
    bounds, bound = [], 0
    for k in range(lengths.shape[0]):
        bound = bound + lengths[k]
        bounds.append(bound)

    def sequence(places):
        number = jnp.zeros(places.shape, F32)
        for bound in bounds:
            number = number + jnp.where(places >= bound, 1.0, 0.0)
        return number

    places = lax.broadcasted_iota(jnp.int32, (tokens + 2 * SUB, LANES), 0) + (anchor - SUB)
    segs[...] = sequence(places)
    for k in range(3):
        same = segs[pl.ds(SUB, tokens)] == segs[pl.ds(SUB - 3 + k, tokens)]
        mask_f[k] = jnp.where(same, 1.0, 0.0)
        same = segs[pl.ds(0, tokens + SUB)] == segs[pl.ds(3 - k, tokens + SUB)]
        mask_b[k] = jnp.where(same, 1.0, 0.0)
    head_of = lax.broadcasted_iota(jnp.int32, (channels, LANES), 0) // HEAD
    column = lax.broadcasted_iota(jnp.int32, (channels, LANES), 1)
    spread_sum[...] = jnp.where(head_of == column, 1.0, 0.0).astype(BF16)
    grads_v[...] = jnp.zeros_like(grads_v)
    grads_s[...] = jnp.zeros_like(grads_s)

    for copy in weights[5:]:
        copy.wait()
    bias[...] = jnp.zeros_like(bias)
    rate[...] = jnp.zeros_like(rate)
    bias[:, 0:heads] = bias_in[...]
    rate[:, 0:heads] = rate_in[...]
    t_in[...] = jnp.zeros_like(t_in)
    for p in range(pairs):
        skip[:, pl.ds(p * LANES, LANES)] = jnp.where(
            left[:1], skip_in[:, 2 * p : 2 * p + 1], skip_in[:, 2 * p + 1 : 2 * p + 2]
        )

    gather_forward(0)
    gather_forward(1)
    gather_end(0)
    gather_end(1)
    width = hidden_in.shape[1]

    @pl.loop(0, chunks)
    def _(c):
        here = pl.ds(pl.multiple_of(c * Q, Q), Q)
        squares = jnp.zeros((Q, 1), F32)
        for h in range(peers_head):
            rows = hidden[h, here].astype(F32)
            squares = squares + jnp.sum(rows * rows, axis=1, keepdims=True)
        scale = lax.rsqrt(squares / (width * peers_head) + EPS)
        scale_in[here] = scale
        for h in range(peers_head):
            rows = hidden[h, here].astype(F32)
            normed[here, pl.ds(h * width, width)] = (rows * scale * gain_full[h, 0:1]).astype(BF16)

    def project(weight, target):
        columns = weight.shape[1]
        tile = next(t for t in (256, 128, columns) if columns % t == 0)

        @pl.loop(0, columns // tile)
        def _(n):
            lanes = pl.ds(pl.multiple_of(n * tile, tile), tile)
            target[:, lanes] = mm(normed[...], weight[:, lanes])

    for copy in weights[:2]:
        copy.wait()
    project(value_m, v_in)
    project(state_m, s_in)

    @pl.when(seq < count - 1)
    def _():
        for copy in edge_copies():
            copy.start()

    weights[2].wait()
    t_in[:, 0:heads] = mm(normed[...], step_m[...], ((1,), (1,)))
    weights[3].wait()
    project(gate_m, g_in)
    gather_forward(2)

    raw = t_in[...] + bias[...]
    step[...] = jnp.maximum(raw, 0.0) + jnp.log1p(jnp.exp(-jnp.abs(raw)))
    sig[...] = sigmoid(raw)
    logs[...] = -jnp.exp(rate[...]) * step[...]
    lower = jnp.where(row >= lane, 1.0, 0.0)

    @pl.loop(0, chunks)
    def _(c):
        here = pl.ds(pl.multiple_of(c * Q, Q), Q)
        run[here] = mm(lower, logs[here], precision=HIGH)
        summed = run[here]
        run_t[c] = summed.T[:16]
        last = run[pl.ds(c * Q + Q - 1, 1)]
        mine = segs[pl.ds(pl.multiple_of(c * Q + SUB, SUB), Q)]
        at_end = segs[pl.ds(c * Q + SUB + Q - 1, 1)]
        entering = segs[pl.ds(c * Q + SUB - 1, 1)]
        tail[here] = jnp.exp(last - summed) * jnp.where(mine == at_end, 1.0, 0.0)
        into[here] = jnp.exp(summed) * jnp.where(mine == entering, 1.0, 0.0)
        through = jnp.exp(last) * jnp.where(at_end == entering, 1.0, 0.0)
        passing[c] = jnp.broadcast_to(through, (Q, LANES)).T[:16]

    product = jnp.ones((16, LANES), F32)
    for c in range(chunks):
        before[c] = product
        product = product * passing[c]
    factors[seq] = product

    def factor_copies():
        return [
            remote(
                factors.at[seq], factors.at[seq], p_send.at[d - 1], p_recv.at[d - 1],
                {"seq": lax.rem(seq + d, count)},
            )
            for d in range(1, count)
        ]

    for copy in factor_copies():
        copy.start()

    def convolve(source, base, rows, lanes, taps, offset):
        begin, size = rows
        summed = offset[:, lanes] + taps[3:4, lanes] * source[pl.ds(base, size), lanes]
        for k in range(3):
            term = taps[k : k + 1, lanes] * source[pl.ds(base - 3 + k, size), lanes]
            summed = summed + term * mask_f[k, pl.ds(begin, size)]
        s = sigmoid(summed)
        return summed * s, s * (1.0 + summed * (1.0 - s))

    def convolve_rows(c):
        rows = (c * Q, Q)
        span = pl.ds(c * Q, Q)

        @pl.loop(0, pairs)
        def _(b):
            lanes = pl.ds(pl.multiple_of(b * LANES, LANES), LANES)
            source, base = (v_in, c * Q) if c else (first_v, SUB)
            val[span, lanes], slope_v[span, lanes] = convolve(source, base, rows, lanes, taps_v, off_v)

        for b, (target, low) in enumerate(((inf, inf_low), (rea, rea_low))):
            lanes = pl.ds(b * LANES, LANES)
            source, base = (s_in, c * Q) if c else (first_s, SUB)
            active, slope_s[span, lanes] = convolve(source, base, rows, lanes, taps_s, off_s)
            target[span], low[span] = split(active)

    for c in range(1, chunks):
        convolve_rows(c)

    @pl.when(seq > 0)
    def _():
        for copy in edge_copies():
            copy.wait_recv()

    @pl.when(seq == 0)
    def _():
        edge_v[...] = jnp.zeros_like(edge_v)
        edge_s[...] = jnp.zeros_like(edge_s)

    first_v[pl.ds(0, SUB)] = edge_v[...]
    first_s[pl.ds(0, SUB)] = edge_s[...]
    first_v[pl.ds(SUB, Q)] = v_in[pl.ds(0, Q)]
    first_s[pl.ds(SUB, Q)] = s_in[pl.ds(0, Q)]
    convolve_rows(0)

    def both(ref, here, p):
        return jnp.where(left, ref[here, 2 * p : 2 * p + 1], ref[here, 2 * p + 1 : 2 * p + 2])

    def halves(value):
        return jnp.concatenate(
            [jnp.where(left, value, 0.0), jnp.where(left, 0.0, value)], axis=0
        ).astype(BF16)

    @pl.loop(0, chunks)
    def _(c):
        here = pl.ds(pl.multiple_of(c * Q, Q), Q)
        for p in range(pairs):
            lanes = pl.ds(p * LANES, LANES)
            weighted = both(step, here, p) * val[here, lanes]
            scaled[here, lanes], scaled_low[here, lanes] = split(both(tail, here, p) * weighted)
        states[c] = mm(
            twice(scaled[here], 0), jnp.concatenate([inf[here], inf_low[here]], axis=0), ((0,), (0,))
        )

    def pass_chunks(h):
        rows = pl.ds(h * HEAD, HEAD)
        held = jnp.zeros((HEAD, LANES), F32)
        for c in range(chunks):
            added = states[c, rows]
            states[c, rows] = held
            held = passing[c, h : h + 1] * held + added
        total[rows] = held

    share = channels // 2
    heads_of = (range(heads // 2), range(heads // 2, heads))

    def carry(direction):
        bank = 0 if direction == 1 else 1

        def reach(d):
            there = seq + direction * d
            return jnp.logical_and(there >= 0, there < count)

        def heard(d):
            there = seq - direction * d
            return jnp.logical_and(there >= 0, there < count)

        def copy(slot, d, half):
            source, rows = min(slot, len(steps)), pl.ds(half * share, share)
            return remote(
                push.at[bank, source, rows], got.at[bank, slot, rows],
                carry_send.at[bank, slot, half], carry_recv.at[bank, slot, half],
                {"seq": lax.rem(seq + direction * d + count, count)},
            )

        plan = [(k, d) for k, d in enumerate(steps)]
        ends = [(len(steps), 1), (len(steps) + 1, 2)]

        def send(slot, d, half):
            @pl.when(reach(d))
            def _():
                copy(slot, d, half).start()

        def factor(first, many, h):
            product = factors[first, h : h + 1]
            for i in range(1, many):
                product = product * factors[first - direction * i, h : h + 1]
            return product

        def launch(slot, half):
            rows = pl.ds(half * share, share)
            push[bank, slot, rows] = total[rows].astype(BF16)
            if slot < len(steps):
                send(*plan[slot], half)
            else:
                for end in ends:
                    send(*end, half)

        def join(slot, half):
            d = plan[slot][1]

            @pl.when(heard(d))
            def _():
                copy(slot, d, half).wait_recv()
                for h in heads_of[half]:
                    rows = pl.ds(h * HEAD, HEAD)
                    total[rows] = total[rows] + factor(seq, d, h) * got[bank, slot, rows].astype(F32)

            launch(slot + 1, half)

        def finish(half):
            part = pl.ds(half * share, share)
            total[part] = jnp.zeros((share, LANES), F32)

            @pl.when(heard(1))
            def _():
                copy(*ends[0], half).wait_recv()
                total[part] = got[bank, ends[0][0], part].astype(F32)

            @pl.when(heard(2))
            def _():
                copy(*ends[1], half).wait_recv()
                for h in heads_of[half]:
                    rows = pl.ds(h * HEAD, HEAD)
                    far = got[bank, ends[1][0], rows].astype(F32)
                    total[rows] = total[rows] + factor(seq - direction, 1, h) * far

        def close():
            for slot, d in plan + ends:
                @pl.when(reach(d))
                def _(slot=slot, d=d):
                    for half in range(2):
                        copy(slot, d, half).wait_send()

        return launch, join, finish, close

    launch, join, finish, close_forward = carry(1)
    for half in range(2):
        for h in heads_of[half]:
            pass_chunks(h)
        launch(0, half)
    gather_end(2)
    weights[4].wait()

    @pl.loop(0, tokens // (2 * Q))
    def _(n):
        here = pl.ds(pl.multiple_of(n * 2 * Q, 2 * Q), 2 * Q)
        result = jnp.zeros((2 * Q, channels), F32)
        for h in range(peers_head):
            result = result + mm(cot[h, here], out_m[:, pl.ds(h * width, width)], ((1,), (1,)))
        d_mix[here] = result

    def products(here):
        read = jnp.concatenate([rea[here], rea[here], rea_low[here]], axis=1)
        return mm(read, jnp.concatenate([inf[here], inf_low[here], inf[here]], axis=1), ((1,), (1,)))

    def from_state(high, low, c, lanes):
        state = jnp.concatenate([starts[c, lanes], starts_low[c, lanes], starts[c, lanes]], axis=1)
        return mm(jnp.concatenate([high, high, low], axis=1), state, ((1,), (1,)))

    def with_state(high, low, c, lanes):
        state = jnp.concatenate([starts[c, lanes], starts_low[c, lanes], starts[c, lanes]], axis=0)
        return mm(jnp.concatenate([high, high, low], axis=1), state)

    def within(c):
        here = pl.ds(pl.multiple_of(c * Q, Q), Q)
        mine = segs[pl.ds(pl.multiple_of(c * Q + SUB, SUB), Q)]
        across = sequence(lane + (anchor + c * Q))
        hidden = jnp.where(jnp.logical_and(mine == across, row >= lane), 0.0, FAR)
        cross = products(here)
        for p in range(pairs):
            lanes = pl.ds(p * LANES, LANES)
            mixing = []
            for h in (2 * p, 2 * p + 1):
                gap = (run[here, h : h + 1] - run_t[c, h : h + 1]) + hidden
                decay = jnp.exp(gap)
                pair[c * heads + h] = decay
                mixing.append((decay * cross).astype(BF16))
            weighted = both(step, here, p) * val[here, lanes]
            out[here, lanes] = mm(jnp.concatenate(mixing, axis=1), halves(weighted))

    @pl.loop(0, chunks // 2)
    def _(c):
        within(c)

    for copy in factor_copies():
        copy.wait_recv()
    for k in range(len(steps)):
        for half in range(2):
            join(k, half)

    @pl.loop(chunks // 2, chunks)
    def _(c):
        within(c)

    for h in range(heads):
        if h * 2 % heads == 0:
            finish(h * 2 // heads)
        rows = pl.ds(h * HEAD, HEAD)
        incoming = total[rows]
        for c in range(chunks):
            starts[c, rows], starts_low[c, rows] = split(
                states[c, rows] + before[c, h : h + 1] * incoming
            )

    rows_out[...] = jnp.zeros_like(rows_out)

    @pl.loop(0, chunks)
    def _(c):
        here = pl.ds(pl.multiple_of(c * Q, Q), Q)
        squares, dots = jnp.zeros((Q, LANES), F32), jnp.zeros((Q, LANES), F32)
        for p in range(pairs):
            lanes = pl.ds(p * LANES, LANES)
            reached = from_state(rea[here], rea_low[here], c, lanes)
            reached = reached * both(into, here, p)
            inter[here, lanes] = reached
            mixed = out[here, lanes] + reached + skip[:, lanes] * val[here, lanes]
            out[here, lanes] = mixed
            gate = g_in[here, lanes]
            gated = mixed * (gate * sigmoid(gate))
            squares = squares + gated * gated
            dots = dots + d_mix[here, lanes] * gain[:, lanes] * gated
        rows_out[0:1, here] = jnp.sum(squares.T, axis=0, keepdims=True)
        rows_out[1:2, here] = jnp.sum(dots.T, axis=0, keepdims=True)

    row_copies = [
        remote(
            rows_out, rows_in.at[d - 1], row_send.at[d - 1], row_recv.at[d - 1],
            {"head": lax.rem(head + d, peers_head)},
        )
        for d in range(1, peers_head)
    ]
    for copy in row_copies:
        copy.start()
    summed = rows_out[...]
    for d, copy in enumerate(row_copies):
        copy.wait_recv()
        summed = summed + rows_in[d]
    for copy in row_copies:
        copy.wait_send()
    rows_out[0:1] = lax.rsqrt(summed[0:1] / inner + EPS)
    rows_out[1:2] = summed[1:2] / inner

    @pl.loop(0, chunks)
    def _(c):
        here = pl.ds(pl.multiple_of(c * Q, Q), Q)
        scale = jnp.broadcast_to(rows_out[0:1, here], (Q, LANES)).T
        dot = jnp.broadcast_to(rows_out[1:2, here], (Q, LANES)).T
        cubed = scale * scale * scale * dot
        for p in range(pairs):
            lanes = pl.ds(p * LANES, LANES)
            gate, mixed, slope = g_in[here, lanes], out[here, lanes], d_mix[here, lanes]
            s = sigmoid(gate)
            opened = gate * s
            gated = mixed * opened
            normed = gated * scale
            mix_out[here, lanes] = (normed * gain[:, lanes]).astype(BF16)
            d_gated = scale * (slope * gain[:, lanes]) - gated * cubed
            d_mixer = d_gated * opened
            d_gate[here, lanes] = (d_gated * mixed * (s * (1.0 + gate * (1.0 - s)))).astype(BF16)
            out[here, lanes] = d_mixer
            d_u[here, lanes] = both(into, here, p) * d_mixer
            grads_v[5:6, lanes] = grads_v[5:6, lanes] + jnp.sum(slope * normed, axis=0, keepdims=True)
            grads_v[6:7, lanes] = grads_v[6:7, lanes] + jnp.sum(
                d_mixer * val[here, lanes], axis=0, keepdims=True
            )
        carried = d_u[here].astype(BF16)
        states[c] = mm(
            twice(carried, 0), jnp.concatenate([rea[here], rea_low[here]], axis=0), ((0,), (0,))
        )
        d_read = jnp.zeros((Q, LANES), F32)
        for p in range(pairs):
            lanes = pl.ds(p * LANES, LANES)
            d_read = d_read + with_state(*split(d_u[here, lanes]), c, lanes)
        pre_s[pl.ds(pl.multiple_of(c * Q + SUB, SUB), Q), pl.ds(LANES, LANES)] = d_read

    launch, join, finish, close_backward = carry(-1)
    for half in range(2):
        for h in heads_of[half]:
            rows = pl.ds(h * HEAD, HEAD)
            held = jnp.zeros((HEAD, LANES), F32)
            for c in reversed(range(chunks)):
                held = states[c, rows] + passing[c, h : h + 1] * held
            total[rows] = held
        launch(0, half)
    wave()
    upper = jnp.where(row < lane, 1.0, 0.0).astype(BF16)

    def within_back(c):
        here = pl.ds(pl.multiple_of(c * Q, Q), Q)
        padded = pl.ds(pl.multiple_of(c * Q + SUB, SUB), Q)
        cross = products(here)
        d_cross = jnp.zeros((Q, LANES), F32)
        from_inter = jnp.zeros((Q, LANES), F32)
        for p in range(pairs):
            lanes = pl.ds(p * LANES, LANES)
            weighted = (both(step, here, p) * val[here, lanes]).astype(BF16)
            d_out = out[here, lanes]
            d_halves = halves(d_out)
            d_pair = mm(d_halves, weighted, ((1,), (1,)))
            mixing, terms = [], []
            for i, h in enumerate((2 * p, 2 * p + 1)):
                decay = pair[c * heads + h]
                shared = d_pair[i * Q : (i + 1) * Q] * decay
                d_cross = d_cross + shared
                terms.append((shared * cross).astype(BF16))
                mixing.append((decay * cross).astype(BF16))
            d_u[here, lanes] = mm(jnp.concatenate(mixing, axis=0), d_halves, ((0,), (0,)))
            ahead = mm(jnp.concatenate(terms, axis=0), upper)
            for i, h in enumerate((2 * p, 2 * p + 1)):
                crossing = jnp.where(row >= lane, ahead[i * Q : (i + 1) * Q], 0.0)
                prefix[c, h : h + 1] = jnp.sum(crossing, axis=0, keepdims=True)
            from_inter = from_inter + mm(
                (d_out * inter[here, lanes]).astype(BF16), spread_sum[lanes]
            )
        kept[0, here] = from_inter
        d_cross = d_cross.astype(BF16)
        pre_s[padded, pl.ds(LANES, LANES)] = pre_s[padded, pl.ds(LANES, LANES)] + mm(
            d_cross, inf[here]
        )
        pre_s[padded, pl.ds(0, LANES)] = mm(d_cross, rea[here], ((0,), (0,)))

    prefix[...] = jnp.zeros_like(prefix)

    for c in range(chunks):
        if c == chunks // 2:
            for k in range(len(steps)):
                for half in range(2):
                    join(k, half)
            wave()
        within_back(c)
        wave()
    for h in range(heads):
        if h * 2 % heads == 0:
            finish(h * 2 // heads)
        rows = pl.ds(h * HEAD, HEAD)
        held = total[rows]
        for c in reversed(range(chunks)):
            start = starts[c, rows].astype(F32) + starts_low[c, rows].astype(F32)
            met = jnp.sum(held * start, axis=0, keepdims=True)
            met = jnp.sum(met, axis=1, keepdims=True) * passing[c, h : h + 1]
            prefix[c, h : h + 1] = prefix[c, h : h + 1] + met
            added = states[c, rows]
            starts[c, rows], starts_low[c, rows] = split(held)
            held = added + passing[c, h : h + 1] * held

    wave()
    from_here = jnp.where(row <= lane, 1.0, 0.0)
    under = jnp.where(row > lane, 1.0, 0.0)
    rates = -jnp.exp(rate[...])
    grads_h[...] = jnp.zeros_like(grads_h)
    pre_v[pl.ds(0, SUB)] = jnp.zeros((SUB, channels), F32)
    pre_v[pl.ds(tokens + SUB, SUB)] = jnp.zeros((SUB, channels), F32)
    pre_s[pl.ds(0, SUB)] = jnp.zeros((SUB, 2 * LANES), F32)
    pre_s[pl.ds(tokens + SUB, SUB)] = jnp.zeros((SUB, 2 * LANES), F32)

    @pl.loop(0, chunks)
    def _(c):
        here = pl.ds(pl.multiple_of(c * Q, Q), Q)
        padded = pl.ds(pl.multiple_of(c * Q + SUB, SUB), Q)
        from_tail, from_step = jnp.zeros((Q, LANES), F32), jnp.zeros((Q, LANES), F32)
        d_in = jnp.zeros((Q, LANES), F32)
        for p in range(pairs):
            lanes = pl.ds(p * LANES, LANES)
            sizes = both(step, here, p)
            value = val[here, lanes]
            d_tail = from_state(inf[here], inf_low[here], c, lanes)
            d_tail = d_tail * both(tail, here, p)
            d_weighted = d_u[here, lanes] + d_tail
            from_tail = from_tail + mm((sizes * value * d_tail).astype(BF16), spread_sum[lanes])
            from_step = from_step + mm((value * d_weighted).astype(BF16), spread_sum[lanes])
            d_val = sizes * d_weighted + skip[:, lanes] * out[here, lanes]
            pre_v[padded, lanes] = d_val * slope_v[here, lanes]
            d_in = d_in + with_state(scaled[here, lanes], scaled_low[here, lanes], c, lanes)
        inflow, readout = pl.ds(0, LANES), pl.ds(LANES, LANES)
        pre_s[padded, inflow] = (pre_s[padded, inflow] + d_in) * slope_s[here, inflow]
        pre_s[padded, readout] = pre_s[padded, readout] * slope_s[here, readout]
        d_log = mm(from_here, kept[0, here], precision=HIGH) + mm(under, from_tail, precision=HIGH)
        filled = jnp.concatenate([prefix[c], jnp.zeros((Q - 16, LANES), F32)], axis=0)
        d_log = d_log + filled.T
        d_size = (from_step + rates * d_log) * sig[here]
        d_step[here] = d_size.astype(BF16)
        grads_h[0:1] = grads_h[0:1] + jnp.sum(d_size, axis=0, keepdims=True)
        grads_h[1:2] = grads_h[1:2] + jnp.sum(d_log * logs[here], axis=0, keepdims=True)

    wave()

    def back(source, base, size, lanes, taps):
        summed = taps[3:4, lanes] * source[pl.ds(base, size), lanes]
        for k in range(3):
            term = taps[k : k + 1, lanes] * source[pl.ds(base + 3 - k, size), lanes]
            summed = summed + term * mask_b[k, pl.ds(base, size)]
        return summed

    def back_copies():
        there = {"seq": lax.rem(seq + count - 1, count)}
        return [
            remote(back_v, back_in_v, back_sems.at[0], back_sems.at[1], there),
            remote(back_s, back_in_s, back_sems.at[2], back_sems.at[3], there),
        ]

    for b in range(pairs):
        lanes = pl.ds(b * LANES, LANES)
        back_v[:, lanes] = back(pre_v, 0, SUB, lanes, taps_v)
    for b in range(2):
        lanes = pl.ds(b * LANES, LANES)
        back_s[:, lanes] = back(pre_s, 0, SUB, lanes, taps_s)

    @pl.when(seq > 0)
    def _():
        for copy in back_copies():
            copy.start()

    def filter_grads(pre, source, base, c, lanes, grads):
        rows = pl.ds(c * Q + SUB, Q)
        slope = pre[rows, lanes]
        for k in range(3):
            term = slope * mask_f[k, pl.ds(c * Q, Q)] * source[pl.ds(base - 3 + k, Q), lanes]
            grads[k : k + 1, lanes] = grads[k : k + 1, lanes] + jnp.sum(term, axis=0, keepdims=True)
        term = slope * source[pl.ds(base, Q), lanes]
        grads[3:4, lanes] = grads[3:4, lanes] + jnp.sum(term, axis=0, keepdims=True)
        grads[4:5, lanes] = grads[4:5, lanes] + jnp.sum(slope, axis=0, keepdims=True)

    for c in range(chunks):
        if c == chunks - 1:
            @pl.when(seq < count - 1)
            def _():
                for copy in back_copies():
                    copy.wait_recv()

            @pl.when(seq == count - 1)
            def _():
                back_in_v[...] = jnp.zeros_like(back_in_v)
                back_in_s[...] = jnp.zeros_like(back_in_s)

        def one(pre, source, base, c, lanes, taps, grads, target, received):
            result = back(pre, c * Q + SUB, Q, lanes, taps)
            if c == chunks - 1:
                result = jnp.concatenate(
                    [result[: Q - SUB], result[Q - SUB :] + received[:, lanes]], axis=0
                )
            target[pl.ds(c * Q, Q), lanes] = result.astype(BF16)
            filter_grads(pre, source, base, c, lanes, grads)

        @pl.loop(0, pairs)
        def _(b, c=c):
            lanes = pl.ds(pl.multiple_of(b * LANES, LANES), LANES)
            source, base = (v_in, c * Q) if c else (first_v, SUB)
            one(pre_v, source, base, c, lanes, taps_v, grads_v, d_value, back_in_v)

        wave()
        for b in range(2):
            lanes = pl.ds(b * LANES, LANES)
            source, base = (s_in, c * Q) if c else (first_s, SUB)
            one(pre_s, source, base, c, lanes, taps_s, grads_s, d_state, back_in_s)

    @pl.when(seq < count - 1)
    def _():
        for copy in edge_copies():
            copy.wait_send()

    @pl.when(seq > 0)
    def _():
        for copy in back_copies():
            copy.wait_send()

    while turns:
        wave()
    for job in work:
        job.close()
    for k in range(3):
        for slot in range(2 * chips - 1):
            gather(k, slot).wait_send()
    for copy in factor_copies():
        copy.wait_send()
    close_forward()
    close_backward()


def mix(count, peers_head, lengths, hidden, cot, weights, filters, gain, vectors, plan, waves, collective_id):
    tokens, width = hidden.shape
    channels = weights[0].shape[1]
    chunks, heads, inner = tokens // Q, channels // HEAD, channels * peers_head
    chips = peers_head // 2
    slots = 1
    reach = count // 4
    while reach >= 2:
        slots += 1
        reach //= 2
    vmem, dma = pltpu.VMEM, pltpu.SemaphoreType.DMA
    shape = jax.ShapeDtypeStruct
    outs = [
        shape((tokens, width * peers_head), BF16), shape((tokens, 1), F32),
        shape((peers_head, tokens, width), BF16), shape((peers_head, tokens, width), BF16),
        shape((peers_head, 8, width), F32),
        shape((tokens, channels), BF16), shape((tokens, channels), BF16),
        shape((tokens, channels), BF16), shape((tokens, 2 * LANES), BF16),
        shape((tokens, LANES), BF16),
        shape((8, channels), F32), shape((8, 2 * LANES), F32), shape((8, LANES), F32),
    ]
    features = width * peers_head
    jobs = rows_of(plan, (0, channels, features))
    for which, start, rows, y_first in jobs:
        outs.append(shape((rows // (count // LINE), (0, features, channels)[which]), BF16))
    wide, narrow = (tokens, channels), (tokens, LANES)
    scratch = [
        vmem(wide, F32), vmem((tokens, 2 * LANES), F32), vmem(wide, F32), vmem(narrow, F32), vmem(wide, F32),
    ]
    scratch += [vmem(weight.shape, BF16) for weight in weights]
    scratch += [vmem((1,) + vector.shape, F32) for vector in vectors]
    scratch += [
        vmem((8, width), F32), vmem((1, LANES), F32), vmem((1, LANES), F32), vmem((1, channels), F32),
        vmem((SUB, channels), F32), vmem((SUB, 2 * LANES), F32),
        vmem((Q + SUB, channels), F32), vmem((Q + SUB, 2 * LANES), F32),
        vmem(wide, F32), vmem(narrow, BF16), vmem(narrow, BF16), vmem(narrow, BF16), vmem(narrow, BF16),
        vmem(wide, F32), vmem((tokens, 2 * LANES), F32),
        vmem((tokens + 2 * SUB, LANES), F32),
        vmem((3, tokens, LANES), F32), vmem((3, tokens + SUB, LANES), F32),
        vmem(narrow, F32), vmem(narrow, F32), vmem(narrow, F32), vmem(narrow, F32),
        vmem((chunks, 16, LANES), F32), vmem(narrow, F32), vmem(narrow, F32),
        vmem((chunks, 16, LANES), F32),
        vmem((chunks * heads, Q, LANES), F32), vmem(wide, BF16), vmem(wide, BF16),
        vmem(wide, F32), vmem(wide, F32), vmem(wide, F32),
        vmem((chunks, channels, LANES), F32),
        vmem((chunks, channels, LANES), BF16), vmem((chunks, channels, LANES), BF16),
        vmem((chunks, 16, LANES), F32), vmem((channels, LANES), F32),
        vmem((count, 16, LANES), F32),
        vmem((2, slots, channels, LANES), BF16), vmem((2, slots + 1, channels, LANES), BF16),
        vmem((1, tokens, LANES), F32), vmem((chunks, 16, LANES), F32),
        vmem((channels, LANES), BF16),
        vmem((8, tokens), F32), vmem((peers_head - 1, 8, tokens), F32),
        vmem((tokens + 2 * SUB, channels), F32), vmem((tokens + 2 * SUB, 2 * LANES), F32),
        vmem((SUB, channels), F32), vmem((SUB, 2 * LANES), F32),
        vmem((SUB, channels), F32), vmem((SUB, 2 * LANES), F32),
        dma((14,)), dma((3, 2 * chips - 1)), dma((3, 2 * chips - 1)),
        dma((4,)), dma((count - 1,)), dma((count - 1,)),
        dma((2, slots + 1, 2)), dma((2, slots + 1, 2)),
        dma((peers_head - 1,)), dma((peers_head - 1,)), dma((4,)),
        vmem((channels, features), BF16),
        vmem((max([start + rows for which, start, rows, _ in jobs if which == 2] + [8]), channels), BF16),
    ]
    scratch += job_scratch(jobs, (0, features, channels), count // LINE, 0, True)
    inside, anywhere = pl.BlockSpec(memory_space=pltpu.VMEM), pl.BlockSpec(memory_space=pl.ANY)
    return pl.pallas_call(
        functools.partial(mixer_kernel, count, peers_head, inner, jobs, waves),
        out_shape=outs,
        in_specs=[pl.BlockSpec(memory_space=pltpu.SMEM)]
        + [anywhere] * 7 + [inside] * 3 + [anywhere] * len(vectors),
        out_specs=[inside] * len(outs),
        scratch_shapes=scratch,
        compiler_params=pltpu.CompilerParams(
            collective_id=collective_id, has_side_effects=True, vmem_limit_bytes=61 * 1024 * 1024
        ),
    )(lengths, hidden, cot, *weights, *filters, gain, *vectors)


def sum_rows(jobs, order, lines, peers_head, early, *refs):
    (normed, cot, hidden, scale, gain, mix_out, d_gate, d_value, d_state, d_step, grads_v, grads_s, grads_h,
     gate_w, value_w, out_w, state_w, step_w) = refs[:18]
    given, refs = refs[18 : 18 + early], refs[18 + early :]
    outs, (every, normed_sum, mixed_sum, dots_sum) = refs[:4], refs[4:8]
    scratch = refs[8:]
    count = len(jobs)
    y_in, right, left, total, final = (scratch[k * count : (k + 1) * count] for k in range(5))
    names = ("swap", "right", "left", "spread", "share")
    pairs = scratch[5 * count : 5 * count + 10]
    sems = {name: (pairs[2 * k], pairs[2 * k + 1]) for k, name in enumerate(names)}
    (sems["keep"], packed, out_part, gate_part, value_part, gate_m, value_m, out_m, state_m, step_m,
     blocks, block_in, normed_part, normed_in, mixed_part, mixed_in, dots, dots_in, gain_part, rest, product,
     local_sem, hs, hr) = scratch[5 * count + 10 :]
    parts = [packed, out_part, gate_part, value_part]
    tokens, features = normed.shape
    width, channels = features // peers_head, d_gate.shape[1]
    heads = channels // HEAD
    seq, head = lax.axis_index("seq"), lax.axis_index("head")
    z, y = seq // lines, lax.rem(seq, lines)
    work = [
        Job(j, y_first, given[j] if j < early else parts[which], outs[which], start, rows, lines,
            y_in[j], right[j], left[j], total[j], final[j], sems, (seq, z, y), 2 if j < early else 0)
        for j, (which, start, rows, y_first) in enumerate(jobs)
    ]
    shared = [j for j in range(count) if not jobs[j][0]][0]

    loads = [
        pltpu.make_async_copy(src, dst, local_sem.at[k])
        for k, (src, dst) in enumerate(
            ((gate_w, gate_m), (value_w, value_m), (out_w, out_m), (state_w, state_m), (step_w, step_m))
        )
    ]
    for copy in loads:
        copy.start()

    barrier = pltpu.get_barrier_semaphore()
    peers = [{"seq": z * lines + lax.rem(y + d, lines)} for d in range(1, lines)]
    peers += [{"head": lax.rem(head + d, peers_head)} for d in range(1, peers_head)]
    for peer in peers:
        pl.semaphore_signal(barrier, inc=1, device_id=peer, device_id_type=MESH)
    for direction in (1, -1):
        @pl.when(z < LINE - 1 if direction > 0 else z > 0)
        def _(direction=direction):
            pl.semaphore_signal(
                barrier, inc=1, device_id={"seq": (z + direction) * lines + y}, device_id_type=MESH
            )

    ends = jnp.logical_or(z == 0, z == LINE - 1)

    @pl.when(ends)
    def _():
        pl.semaphore_wait(barrier, len(peers) + 1)

    @pl.when(jnp.logical_not(ends))
    def _():
        pl.semaphore_wait(barrier, len(peers) + 2)

    block = blocks.shape[1]

    def head_copies(kind):
        for d in range(1, peers_head):
            to = lax.rem(head + d, peers_head)
            if kind < 4:
                src = (blocks.at[to], dots, normed_part.at[to], mixed_part.at[to])[kind]
                dst = (block_in, dots_in, normed_in, mixed_in)[kind].at[d - 1]
            else:
                src, dst = outs[0].at[pl.ds(0, width)], every.at[head]
            yield pltpu.make_async_remote_copy(
                src_ref=src, dst_ref=dst, send_sem=hs.at[kind, d - 1], recv_sem=hr.at[kind, d - 1],
                device_id={"head": to}, device_id_type=MESH,
            )

    def start(copies):
        for copy in copies:
            copy.start()

    def received(copies):
        for copy in copies:
            copy.wait_recv()

    def make(j):
        which, begin, rows, y_first = jobs[j]
        if j < early:
            return None
        if not which:
            return pack
        if which == 1:
            return lambda: outer(mix_out, [cot.at[h] for h in range(peers_head)], out_part, begin, rows)
        return lambda: outer(normed, [(d_gate, d_value)[which - 2]], parts[which], begin, rows)

    def over_head(quarter):
        if quarter == 0:
            for copy in loads:
                copy.wait()
            dots[...] = jnp.zeros_like(dots)
            gain_part[...] = jnp.zeros_like(gain_part)

        def by_head(h):
            mine = pl.ds(h * width, width)
            result = jnp.zeros((tokens, width), F32)
            for left_ref, right_ref in (
                (d_gate, gate_m), (d_value, value_m), (d_state, state_m)
            ):
                result = result + lax.dot_general(
                    left_ref[...], right_ref[mine], (((1,), (1,)), ((), ())), preferred_element_type=F32
                )
            result = result + jnp.dot(d_step[:, 0:heads], step_m[:, mine], preferred_element_type=F32)
            product[...] = result
            mixed_part[h] = jnp.dot(
                mix_out[...], out_m[:, mine], preferred_element_type=F32
            ).astype(BF16)

            @pl.loop(0, tokens // Q)
            def _(c):
                here = pl.ds(pl.multiple_of(c * Q, Q), Q)
                result = product[here]
                normed_part[h, here] = result.astype(BF16)
                rows = result * hidden[h, here].astype(F32)
                gain_part[:, mine] = gain_part[:, mine] + jnp.sum(
                    rows * scale[here], axis=0, keepdims=True
                )
                dot = jnp.sum(rows * gain[h, 0:1], axis=1, keepdims=True)
                dot = jnp.broadcast_to(dot, (Q, LANES)).T
                dots[:, here] = dots[:, here] + dot[:8]

        for h in range(quarter * peers_head // 4, (quarter + 1) * peers_head // 4):
            by_head(h)

    def over_head_send():
        states = blocks.shape[2]
        rest[...] = jnp.zeros_like(rest)
        rest[0:8] = grads_s[...]
        for k in range(features // states):
            rest[8 + k : 9 + k] = gain_part[:, pl.ds(k * states, states)]
        for h in range(peers_head):
            turned = normed[:, pl.ds(h * width, width)].T
            blocks[h, pl.ds(0, width)] = jnp.dot(
                turned, d_state[...], preferred_element_type=F32
            ).astype(BF16)
            blocks[h, pl.ds(width, 16)] = rest[0:16].astype(BF16)
        for kind in range(4):
            start(head_copies(kind))
        steps = lax.dot_general(
            d_step[...], normed[...], (((0,), (0,)), ((), ())), preferred_element_type=F32
        )
        for k in range(features // states):
            rest[16 + k * heads : 16 + (k + 1) * heads] = steps[:heads, k * states : (k + 1) * states]
        at = 16 + heads * (features // states)
        for k in range(0, channels, states):
            lanes = min(states, channels - k)
            rest[at : at + 8, 0:lanes] = grads_v[:, pl.ds(k, lanes)]
            at += 8
        rest[at : at + 2, 0:LANES] = grads_h[0:2]
        packed[pl.ds(block, rest.shape[0] - 16)] = rest[16:].astype(BF16)

    def pack():
        received(head_copies(0))
        others = [(block_in.at[d], 0) for d in range(peers_head - 1)]
        add_rows((packed, 0), [(blocks.at[head], 0)] + others, block)

    def sum_heads():
        received(head_copies(1))
        summed = dots[...]
        for d in range(peers_head - 1):
            summed = summed + dots_in[d]
        dots_sum[...] = summed
        for kind, mine, boxes, target in (
            (2, normed_part, normed_in, normed_sum), (3, mixed_part, mixed_in, mixed_sum)
        ):
            received(head_copies(kind))
            others = [(boxes.at[d], 0) for d in range(peers_head - 1)]
            add_rows((target, 0), [(mine.at[head], 0)] + others, tokens, F32)

    plans = [job.stages(make(job.index)) for job in work]

    def give():
        work[shared].keep().wait()
        work[shared].arrived()
        mine = pltpu.make_async_copy(outs[0].at[pl.ds(0, width)], every.at[head], local_sem.at[0])
        mine.start()
        start(head_copies(4))
        mine.wait()

    plans[shared].append(give)
    plans.append([functools.partial(over_head, q) for q in range(4)] + [over_head_send, sum_heads])
    for j, stage in order:
        plans[j][stage]()
    for job in work:
        job.close(job.index == shared)
    received(head_copies(4))
    for kind in range(5):
        for copy in head_copies(kind):
            copy.wait_send()


def sum_over_seq(plan, order, values, grads, weights, given, lines, peers_head, collective_id):
    normed, d_gate, d_state = values[0], values[6], values[8]
    tokens, features = normed.shape
    channels, states, width = d_gate.shape[1], d_state.shape[1], normed.shape[1] // peers_head
    heads = channels // HEAD
    shape, dma, vmem = jax.ShapeDtypeStruct, pltpu.SemaphoreType.DMA, pltpu.VMEM
    extra = heads * (features // states) + 8 * -(-channels // states) + 8
    total = -(-(width + 16 + extra) // (8 * lines * LINE)) * 8 * lines * LINE
    whole = [
        shape((total, states), BF16), shape((channels, features), BF16),
        shape((features, channels), BF16), shape((features, channels), BF16),
    ]
    jobs = rows_of(plan, [one.shape[0] for one in whole])
    count = len(jobs)
    scratch = job_scratch(jobs, [one.shape[1] for one in whole], lines, len(given))
    others = peers_head - 1
    scratch += [dma((count,))]
    scratch += [vmem(one.shape, BF16) for one in whole]
    scratch += [vmem(one.shape, BF16) for one in weights]
    scratch += [
        vmem((peers_head, width + 16, states), BF16), vmem((others, width + 16, states), BF16),
        vmem((peers_head, tokens, width), BF16), vmem((others, tokens, width), BF16),
        vmem((peers_head, tokens, width), BF16), vmem((others, tokens, width), BF16),
        vmem((8, tokens), F32), vmem((others, 8, tokens), F32), vmem((1, features), F32),
        vmem((total - width, states), F32), vmem((tokens, width), F32),
        dma((5,)), dma((5, others)), dma((5, others)),
    ]
    anywhere, inside = pl.BlockSpec(memory_space=pl.ANY), pl.BlockSpec(memory_space=pltpu.VMEM)
    operands = list(values) + list(grads)
    return pl.pallas_call(
        functools.partial(sum_rows, jobs, order, lines, peers_head, len(given)),
        out_shape=whole
        + [shape((peers_head, width, states), BF16)]
        + [shape((tokens, width), F32)] * 2
        + [shape((8, tokens), F32)],
        in_specs=[inside] * len(operands) + [anywhere] * 5 + [inside] * len(given),
        out_specs=[anywhere] * 5 + [inside] * 3,
        scratch_shapes=scratch,
        compiler_params=pltpu.CompilerParams(
            collective_id=collective_id, has_side_effects=True, vmem_limit_bytes=61 * 1024 * 1024
        ),
    )(*operands, *weights, *given)


def finish_kernel(
    features, steps, out_sum, gate_sum, value_sum, state_sum, hidden, cot, scale, gain, normed_sum, mixed_sum,
    dots, extra,
    out_grad, gate_grad, value_grad, state_grad, block_out, delta_hidden, step_grad, filter_v, filter_s,
    norm_grad, offset_v, offset_s, bias_grad, decay_grad, skip_grad, mix_grad,
    small, row, flat, head_row, column,
):
    step = pl.program_id(0)
    width, channels = hidden.shape[1], filter_v.shape[1]
    heads, states = channels // HEAD, extra.shape[1]
    for source, target in (
        (out_sum, out_grad), (gate_sum, gate_grad), (value_sum, value_grad), (state_sum, state_grad)
    ):
        target[...] = source[...].astype(F32)
    rows = hidden[...].astype(F32)
    block_out[...] = (rows + mixed_sum[...]).astype(BF16)

    @pl.when(step == 0)
    def _():
        dot = jnp.broadcast_to(dots[0:1] / features, (Q, dots.shape[1]))
        column[...] = jnp.concatenate(
            [dot[:, c * Q : (c + 1) * Q].T for c in range(dots.shape[1] // Q)], axis=0
        )[:, 0:1]

    count = rows.shape[0]
    mine = column[pl.ds(pl.multiple_of(step * count, count), count)]
    size = scale[...]
    delta_hidden[...] = (
        cot[...].astype(F32)
        + size * (normed_sum[...] * gain[...].astype(F32).reshape(1, width))
        - rows * (size * size * size) * mine
    )

    @pl.when(step == 1)
    def _():
        small[...] = extra[...].astype(F32)
        at = width + 16
        tiles = features // states
        for k in range(tiles):
            step_grad[:, pl.ds(k * states, states)] = small[at + k * heads : at + (k + 1) * heads]
            flat[0:1, pl.ds(k * states, states)] = small[width + 8 + k : width + 9 + k]
        at += tiles * heads
        for k in range(0, channels, states):
            lanes = min(states, channels - k)
            row[:, pl.ds(k, lanes)] = small[at : at + 8, 0:lanes]
            at += 8
        filter_v[...] = row[0:4]
        filter_s[...] = small[width : width + 4]
        head = lax.axis_index("head")
        chosen = flat[0:1, 0:width]
        for h in range(1, features // width):
            chosen = jnp.where(head == h, flat[0:1, pl.ds(h * width, width)], chosen)
        norm_grad[...] = chosen.reshape(width)
        offset_v[...] = row[4:5].reshape(channels)
        offset_s[...] = small[width + 4 : width + 5].reshape(states)
        mix_grad[...] = row[5:6].reshape(channels)
        of_head = lax.broadcasted_iota(jnp.int32, (channels, LANES), 0) // HEAD
        lane = lax.broadcasted_iota(jnp.int32, (channels, LANES), 1)
        gather = jnp.where(of_head == lane, 1.0, 0.0)
        summed = jnp.dot(row[...], gather, precision=HIGH, preferred_element_type=F32)
        head_row[0:1] = small[at : at + 1, 0:LANES]
        head_row[1:2] = small[at + 1 : at + 2, 0:LANES]
        head_row[2:3] = summed[6:7]
        for k, target in enumerate((bias_grad, decay_grad, skip_grad)):
            target[...] = head_row[k : k + 1, 0:heads].reshape(heads)


def finish(out_sum, gate_sum, value_sum, state_sum, hidden, cot, scale, gain, normed_sum, mixed_sum, dots, extra):
    tokens, width = hidden.shape
    channels, features = out_sum.shape
    heads, states, steps = channels // HEAD, extra.shape[1], 8
    shape = jax.ShapeDtypeStruct

    def tiles(array):
        return pl.BlockSpec((array.shape[0] // steps, array.shape[1]), lambda k: (k, 0))

    def all_of(array):
        return pl.BlockSpec(array.shape, lambda k: (0,) * len(array.shape))

    state_sum = state_sum.reshape(features, states)
    tiled = [out_sum, gate_sum, value_sum, state_sum]
    rows = [hidden, cot, scale]
    outs = [shape(one.shape, F32) for one in tiled]
    outs += [shape(hidden.shape, BF16), shape(hidden.shape, F32)]
    small = [(heads, features), (4, channels), (4, states)]
    small += [(width,), (channels,), (states,), (heads,), (heads,), (heads,), (channels,)]
    small = [shape(one, F32) for one in small]
    return pl.pallas_call(
        functools.partial(finish_kernel, features, steps),
        grid=(steps,),
        out_shape=outs + small,
        in_specs=[tiles(one) for one in tiled + rows]
        + [all_of(gain), tiles(normed_sum), tiles(mixed_sum), all_of(dots), all_of(extra)],
        out_specs=[tiles(one) for one in outs] + [all_of(one) for one in small],
        scratch_shapes=[
            pltpu.VMEM(extra.shape, F32), pltpu.VMEM((8, channels), F32), pltpu.VMEM((8, features), F32),
            pltpu.VMEM((8, LANES), F32), pltpu.VMEM((tokens, 1), F32),
        ],
        compiler_params=pltpu.CompilerParams(dimension_semantics=("arbitrary",)),
    )(*tiled, *rows, gain, normed_sum, mixed_sum, dots, extra)


PLAN = (
    (1, 0, 3, True), (1, 1, 3, True), (1, 2, 3, True), (2, 0, 3, False),
    (2, 1, 3, True), (2, 2, 3, True), (0, 0, 1, True), (3, 0, 3, False),
    (3, 1, 3, True), (3, 2, 3, True),
)
EARLY = 2
WAVES = (
    ((0, 0),), (), (), ((1, 0),),
    (), (), (), ((0, 1),),
    (), (), (), ((1, 1),),
)
ORDER = (
    (0, 0), (2, 0), (10, 0), (3, 0), (5, 0), (0, 1), (4, 0), (0, 2), (10, 1), (0, 3),
    (10, 2), (3, 1), (0, 4), (10, 3), (2, 1), (3, 2), (5, 1), (2, 2), (10, 4), (9, 0),
    (5, 2), (3, 3), (2, 3), (5, 3), (4, 1), (4, 2), (2, 4), (3, 4), (1, 0), (5, 4),
    (2, 5), (6, 0), (4, 3), (3, 5), (0, 5), (4, 4), (9, 1), (1, 1), (8, 0), (3, 6),
    (1, 2), (0, 6), (7, 0), (3, 7), (1, 3), (9, 2), (5, 5), (6, 1), (2, 6), (9, 3),
    (7, 1), (4, 5), (5, 6), (9, 4), (7, 2), (6, 2), (9, 5), (6, 3), (8, 1), (4, 6),
    (7, 3), (8, 2), (5, 7), (2, 7), (3, 8), (9, 6), (6, 4), (7, 4), (6, 5), (8, 3),
    (8, 4), (1, 4), (6, 6), (1, 5), (7, 5), (6, 7), (9, 7), (4, 7), (10, 5), (8, 5),
    (7, 6), (1, 6), (6, 8), (8, 6), (8, 7), (7, 7), (7, 8),
)


def contract_rows(left, right):
    return lax.dot_general(
        left, right, (((0,), (0,)), ((), ())), preferred_element_type=jnp.float32
    )


def contract_cols(left, right):
    return lax.dot_general(
        left, right, (((1,), (1,)), ((), ())), preferred_element_type=jnp.float32
    )


def local(
    hidden_in,
    norm_gain,
    gate_weight,
    value_weight,
    step_weight,
    state_weight,
    value_filter,
    value_offset,
    state_filter,
    state_offset,
    step_bias,
    decay_log,
    skip_gain,
    mix_gain,
    out_weight,
    lengths,
    cotangent,
):
    tokens, width = hidden_in.shape
    heads, channels = step_weight.shape[1], value_weight.shape[1]
    count, peers_head = lax.axis_size("seq"), lax.axis_size("head")
    features = width * peers_head
    step_turned = step_weight.T
    normed, scale_in, *values = mix(
        count,
        peers_head,
        lengths,
        hidden_in,
        cotangent,
        (gate_weight, value_weight, state_weight, out_weight, step_turned),
        (value_filter, state_filter),
        norm_gain,
        (value_offset, mix_gain, state_offset, step_bias, decay_log, skip_gain),
        PLAN[:EARLY],
        WAVES,
        collective_id=2,
    )
    hidden_full, cot_full, gain_full, mix_out, d_gate, d_value, d_state, d_step = values[:8]
    grads_v, grads_s, grads_h = values[8:11]
    extra, out_sum, gate_sum, value_sum, state_sum, normed_sum, mixed_sum, dot_sum = sum_over_seq(
        PLAN,
        ORDER,
        (normed, cot_full, hidden_full, scale_in, gain_full, mix_out, d_gate, d_value, d_state, d_step),
        (grads_v, grads_s, grads_h),
        (gate_weight, value_weight, out_weight, state_weight, step_turned),
        values[11:],
        count // LINE,
        peers_head,
        3,
    )
    (
        out_grad, gate_grad, value_grad, state_grad, block_out, delta_hidden, step_grad, filter_v, filter_s,
        norm_grad, offset_v, offset_s, bias_grad, decay_grad, skip_grad, mix_grad,
    ) = finish(
        out_sum, gate_sum, value_sum, state_sum, hidden_in, cotangent, scale_in, norm_gain,
        normed_sum, mixed_sum, dot_sum, extra,
    )
    return (
        block_out,
        delta_hidden,
        norm_grad,
        gate_grad,
        value_grad,
        step_grad.T,
        state_grad,
        filter_v,
        offset_v,
        filter_s,
        offset_s,
        bias_grad,
        decay_grad,
        skip_grad,
        mix_grad,
        out_grad,
    )


def solution(mesh):
    in_specs = (
        P("seq", "head"),
        P("head"),
        P(None, "head"),
        P(None, "head"),
        P(None, "head"),
        P(),
        P(None, "head"),
        P("head"),
        P(),
        P(),
        P("head"),
        P("head"),
        P("head"),
        P("head"),
        P("head", None),
        P(),
        P("seq", "head"),
    )
    out_specs = (
        P("seq", "head"),
        P("seq", "head"),
        P("head"),
        P(None, "head"),
        P(None, "head"),
        P(None, "head"),
        P(),
        P(None, "head"),
        P("head"),
        P(),
        P(),
        P("head"),
        P("head"),
        P("head"),
        P("head"),
        P("head", None),
    )
    return jax.shard_map(local, mesh=mesh, in_specs=in_specs, out_specs=out_specs, check_vma=False)
```

time: 397 us -> 239 us (0.60)
  Pallas kernels: 324 us -> 238 us
  matrix products: 32.4 us -> 0 us
  local copies, waits for them, and re-layouts: 22.1 us -> 0 us
  other arithmetic: 16.8 us -> 0 us
    pallas_call x3, Pallas kernels: 324 us -> 238 us  [the longest x1 140 us: sum_over_seq(): pl.pallas_call(functools.partial(sum_rows, jobs, order, lines, peers_head...]
    dot_general x16 -> x0, matrix products: 32.4 us -> none  [the longest x4 10.4 us: project(): return jnp.dot(normed, weight, preferred_element_type=F32)]
    convert_element_type x6 -> x0, other arithmetic: 10.1 us -> none  [the longest x1 2.83 us: local(): jnp.concatenate(jnp.split(out_sum, 2, axis=0), axis=1).astype(F32)]
    unnamed x75 -> x0, local copies, waits for them, and re-layouts: 5.27 us -> none
    slice x16 -> x0, local copies, waits for them, and re-layouts: 4.17 us -> none  [the longest x6 1.87 us: local(): pieces.append(jnp.reshape(packed[start:start + part.size], part.shape))]
where the time goes in v4:
time: 239 us
  Pallas kernels  238 us (100%)
    pallas_call x1, Pallas kernels, sum_over_seq(): pl.pallas_call(functools.partial(sum_rows, jobs, order, lines, peers_head...  140 us
    pallas_call x1, Pallas kernels, mix(): pl.pallas_call(functools.partial(mixer_kernel, count, peers_head, inner,...  85.7 us
    pallas_call x1, Pallas kernels, finish(): pl.pallas_call(functools.partial(finish_kernel, features, steps), grid=(s...  12.3 us

profile of v4, /device:TPU:0, one launch (start us, length us, event | category | flops | bytes accessed | tf_op | source)
XLA Modules:
  0.0 238.7 jit_solution(6503507778914963229)
XLA Ops:
  0.7 85.7 %shard_map.288 = (bf16[512,1536]{1,0:T(8,128)(2,1)}, f32[512,1]{1,0:T(8,128)}, bf16[4,512,384]{2,1,0:T(8,128)(2,1)}, bf16[4,512,384]{2,1,0:T(8,128)(2,1)}, f32[4...) custom-call(s32[4]{0:T(128)} %lengths.1, ...), custom_call_target="tpu_custom_call" | custom-call | tf_op jit(solution)/shard_map/pallas_call | solution.py:1160
  86.4 139.8 %shard_map.289 = (bf16[512,256]{1,0:T(8,128)(2,1)}, bf16[768,1536]{1,0:T(8,128)(2,1)}, bf16[1536,768]{1,0:T(8,128)(2,1)}, bf16[1536,768]{1,0:T(8,128)(2,1)}, bf1...) custom-call(bf16[512,1536]{1,0:T(8,128)(2,1)} %get-tuple-element.55.refs_0_, ...), custom_call_target="tpu_custom_call" | custom-call | tf_op jit(solution)/shard_map/pallas_call | solution.py:1398
  226.2 12.3 %shard_map.290 = (f32[768,1536]{1,0:T(8,128)}, f32[1536,768]{1,0:T(8,128)}, f32[1536,768]{1,0:T(8,128)}, f32[1536,256]{1,0:T(8,128)}, bf16[512,384]{1,0:T(8,128)...) custom-call(bf16[768,1536]{1,0:T(8,128)(2,1)} %get-tuple-element.70., ...), custom_call_target="tpu_custom_call" | custom-call | tf_op jit(solution)/shard_map/pallas_call | solution.py:1500

commit v5 on v4

--- a/solution.py
+++ b/solution.py
@@ -348,19 +348,19 @@
     count, peers_head, inner, jobs, waves,
     lengths, hidden_in, cot_in, gate_w, value_w, state_w, out_w, step_w,
     taps_v, taps_s, gain_in, off_v_in, gain_mix_in, off_s_in, bias_own, rate_own, skip_own,
-    normed, scale_in, hidden, cot, gain_full, mix_out, d_gate, d_value, d_state, d_step,
+    normed_out, scale_in, hidden_out, cot_out, gain_full, mix_out_out, d_gate_out, d_value, d_state, d_step,
     grads_v, grads_s, grads_h, *refs,
 ):
     finals, refs = refs[: len(jobs)], refs[len(jobs) :]
     (
-    v_in, s_in, g_in, t_in, d_mix, gate_m, value_m, state_m, out_m, step_m, off_v, gain, off_s, bias_in, rate_in, skip_in, gain_own, bias, rate, skip,
+    normed, hidden, cot, mix_out, d_gate, out_sem, v_in, s_in, g_in, t_in, d_mix, gate_m, value_m, state_m, out_m, step_m, off_v, gain, off_s, bias_in, rate_in, skip_in, gain_own, bias, rate, skip,
     edge_v, edge_s, first_v, first_s, val, inf, inf_low, rea, rea_low, slope_v, slope_s, segs, mask_f, mask_b,
     step, sig, logs, run, run_t, tail, into, passing, pair, scaled, scaled_low, out, inter, d_u,
     states, starts, starts_low, before, total, factors, push, got, kept, prefix, spread_sum,
     rows_out, rows_in, pre_v, pre_s, back_v, back_s, back_in_v, back_in_s,
     local_sem, gather_send, gather_recv, edge_sems, p_send, p_recv, carry_send, carry_recv, row_send, row_recv, back_sems, parts_out, parts_gate,
-    ) = refs[:80]
-    rest = refs[80:]
+    ) = refs[:86]
+    rest = refs[86:]
     tokens, channels = v_in.shape
     chunks, pairs, heads = tokens // Q, channels // LANES, channels // HEAD
     seq, head = lax.axis_index("seq"), lax.axis_index("head")
@@ -512,6 +512,16 @@
             left[:1], skip_in[:, 2 * p : 2 * p + 1], skip_in[:, 2 * p + 1 : 2 * p + 2]
         )
 
+    leave = [
+        pltpu.make_async_copy(src, dst, out_sem.at[n])
+        for n, (src, dst) in enumerate(
+            (
+                (normed, normed_out), (hidden, hidden_out), (cot, cot_out), (mix_out, mix_out_out),
+                (d_gate, d_gate_out),
+            )
+        )
+    ]
+
     gather_forward(0)
     gather_forward(1)
     gather_end(0)
@@ -530,6 +540,9 @@
         for h in range(peers_head):
             rows = hidden[h, here].astype(F32)
             normed[here, pl.ds(h * width, width)] = (rows * scale * gain_full[h, 0:1]).astype(BF16)
+
+    for copy in leave[:2]:
+        copy.start()
 
     def project(weight, target):
         columns = weight.shape[1]
@@ -642,10 +655,8 @@
     def both(ref, here, p):
         return jnp.where(left, ref[here, 2 * p : 2 * p + 1], ref[here, 2 * p + 1 : 2 * p + 2])
 
-    def halves(value):
-        return jnp.concatenate(
-            [jnp.where(left, value, 0.0), jnp.where(left, 0.0, value)], axis=0
-        ).astype(BF16)
+    def halves_split(value):
+        return split(jnp.concatenate([jnp.where(left, value, 0.0), jnp.where(left, 0.0, value)], axis=0))
 
     @pl.loop(0, chunks)
     def _(c):
@@ -756,6 +767,7 @@
             pass_chunks(h)
         launch(0, half)
     gather_end(2)
+    leave[2].start()
     weights[4].wait()
 
     @pl.loop(0, tokens // (2 * Q))
@@ -791,9 +803,13 @@
                 gap = (run[here, h : h + 1] - run_t[c, h : h + 1]) + hidden
                 decay = jnp.exp(gap)
                 pair[c * heads + h] = decay
-                mixing.append((decay * cross).astype(BF16))
-            weighted = both(step, here, p) * val[here, lanes]
-            out[here, lanes] = mm(jnp.concatenate(mixing, axis=1), halves(weighted))
+                mixing.append(decay * cross)
+            high, low = split(jnp.concatenate(mixing, axis=1))
+            first, rest_of = halves_split(both(step, here, p) * val[here, lanes])
+            out[here, lanes] = mm(
+                jnp.concatenate([high, high, low], axis=1),
+                jnp.concatenate([first, rest_of, first], axis=0),
+            )
 
     @pl.loop(0, chunks // 2)
     def _(c):
@@ -890,6 +906,8 @@
             d_read = d_read + with_state(*split(d_u[here, lanes]), c, lanes)
         pre_s[pl.ds(pl.multiple_of(c * Q + SUB, SUB), Q), pl.ds(LANES, LANES)] = d_read
 
+    for copy in leave[3:]:
+        copy.start()
     launch, join, finish, close_backward = carry(-1)
     for half in range(2):
         for h in heads_of[half]:
@@ -910,10 +928,14 @@
         from_inter = jnp.zeros((Q, LANES), F32)
         for p in range(pairs):
             lanes = pl.ds(p * LANES, LANES)
-            weighted = (both(step, here, p) * val[here, lanes]).astype(BF16)
+            weighted, weighted_low = split(both(step, here, p) * val[here, lanes])
             d_out = out[here, lanes]
-            d_halves = halves(d_out)
-            d_pair = mm(d_halves, weighted, ((1,), (1,)))
+            d_halves, d_low = halves_split(d_out)
+            d_pair = mm(
+                jnp.concatenate([d_halves, d_halves, d_low], axis=1),
+                jnp.concatenate([weighted, weighted_low, weighted], axis=1),
+                ((1,), (1,)),
+            )
             mixing, terms = [], []
             for i, h in enumerate((2 * p, 2 * p + 1)):
                 decay = pair[c * heads + h]
@@ -930,11 +952,16 @@
                 (d_out * inter[here, lanes]).astype(BF16), spread_sum[lanes]
             )
         kept[0, here] = from_inter
-        d_cross = d_cross.astype(BF16)
+        high, low = split(d_cross)
         pre_s[padded, pl.ds(LANES, LANES)] = pre_s[padded, pl.ds(LANES, LANES)] + mm(
-            d_cross, inf[here]
+            jnp.concatenate([high, high, low], axis=1),
+            jnp.concatenate([inf[here], inf_low[here], inf[here]], axis=0),
         )
-        pre_s[padded, pl.ds(0, LANES)] = mm(d_cross, rea[here], ((0,), (0,)))
+        pre_s[padded, pl.ds(0, LANES)] = mm(
+            jnp.concatenate([high, high, low], axis=0),
+            jnp.concatenate([rea[here], rea_low[here], rea[here]], axis=0),
+            ((0,), (0,)),
+        )
 
     prefix[...] = jnp.zeros_like(prefix)
 
@@ -1082,6 +1109,8 @@
 
     while turns:
         wave()
+    for copy in leave:
+        copy.wait()
     for job in work:
         job.close()
     for k in range(3):
@@ -1119,7 +1148,9 @@
     for which, start, rows, y_first in jobs:
         outs.append(shape((rows // (count // LINE), (0, features, channels)[which]), BF16))
     wide, narrow = (tokens, channels), (tokens, LANES)
-    scratch = [
+    early = (0, 2, 3, 5, 6)
+    scratch = [vmem(outs[k].shape, BF16) for k in early] + [dma((5,))]
+    scratch += [
         vmem(wide, F32), vmem((tokens, 2 * LANES), F32), vmem(wide, F32), vmem(narrow, F32), vmem(wide, F32),
     ]
     scratch += [vmem(weight.shape, BF16) for weight in weights]
@@ -1162,7 +1193,7 @@
         out_shape=outs,
         in_specs=[pl.BlockSpec(memory_space=pltpu.SMEM)]
         + [anywhere] * 7 + [inside] * 3 + [anywhere] * len(vectors),
-        out_specs=[inside] * len(outs),
+        out_specs=[anywhere if k in early else inside for k in range(len(outs))],
         scratch_shapes=scratch,
         compiler_params=pltpu.CompilerParams(
             collective_id=collective_id, has_side_effects=True, vmem_limit_bytes=61 * 1024 * 1024
@@ -1171,8 +1202,8 @@
 
 
 def sum_rows(jobs, order, lines, peers_head, early, *refs):
-    (normed, cot, hidden, scale, gain, mix_out, d_gate, d_value, d_state, d_step, grads_v, grads_s, grads_h,
-     gate_w, value_w, out_w, state_w, step_w) = refs[:18]
+    (scale, gain, grads_v, grads_s, grads_h, normed_in_, cot_in, hidden_in, mix_out_in, d_gate_in, d_value_in,
+     d_state_in, d_step_in, gate_w, value_w, out_w, state_w, step_w) = refs[:18]
     given, refs = refs[18 : 18 + early], refs[18 + early :]
     outs, (every, normed_sum, mixed_sum, dots_sum) = refs[:4], refs[4:8]
     scratch = refs[8:]
@@ -1183,7 +1214,7 @@
     sems = {name: (pairs[2 * k], pairs[2 * k + 1]) for k, name in enumerate(names)}
     (sems["keep"], packed, out_part, gate_part, value_part, gate_m, value_m, out_m, state_m, step_m,
      blocks, block_in, normed_part, normed_in, mixed_part, mixed_in, dots, dots_in, gain_part, rest, product,
-     local_sem, hs, hr) = scratch[5 * count + 10 :]
+     local_sem, hs, hr, normed, cot, hidden, mix_out, d_gate, d_value, d_state, d_step) = scratch[5 * count + 10 :]
     parts = [packed, out_part, gate_part, value_part]
     tokens, features = normed.shape
     width, channels = features // peers_head, d_gate.shape[1]
@@ -1203,8 +1234,23 @@
             ((gate_w, gate_m), (value_w, value_m), (out_w, out_m), (state_w, state_m), (step_w, step_m))
         )
     ]
-    for copy in loads:
+    operands = {
+        name: pltpu.make_async_copy(src, dst, local_sem.at[5 + n])
+        for n, (name, src, dst) in enumerate(
+            (
+                ("mix_out", mix_out_in, mix_out), ("cot", cot_in, cot), ("normed", normed_in_, normed),
+                ("d_gate", d_gate_in, d_gate), ("d_value", d_value_in, d_value), ("d_state", d_state_in, d_state),
+                ("d_step", d_step_in, d_step), ("hidden", hidden_in, hidden),
+            )
+        )
+    }
+    for copy in list(operands.values()) + loads:
         copy.start()
+
+    def need(*names):
+        for name in names:
+            if name in operands:
+                operands.pop(name).wait()
 
     barrier = pltpu.get_barrier_semaphore()
     peers = [{"seq": z * lines + lax.rem(y + d, lines)} for d in range(1, lines)]
@@ -1257,12 +1303,20 @@
             return None
         if not which:
             return pack
-        if which == 1:
-            return lambda: outer(mix_out, [cot.at[h] for h in range(peers_head)], out_part, begin, rows)
-        return lambda: outer(normed, [(d_gate, d_value)[which - 2]], parts[which], begin, rows)
+
+        def compute():
+            if which == 1:
+                need("mix_out", "cot")
+                outer(mix_out, [cot.at[h] for h in range(peers_head)], out_part, begin, rows)
+            else:
+                need("normed", ("d_gate", "d_value")[which - 2])
+                outer(normed, [(d_gate, d_value)[which - 2]], parts[which], begin, rows)
+
+        return compute
 
     def over_head(quarter):
         if quarter == 0:
+            need(*list(operands))
             for copy in loads:
                 copy.wait()
             dots[...] = jnp.zeros_like(dots)
@@ -1294,7 +1348,7 @@
                 )
                 dot = jnp.sum(rows * gain[h, 0:1], axis=1, keepdims=True)
                 dot = jnp.broadcast_to(dot, (Q, LANES)).T
-                dots[:, here] = dots[:, here] + dot[:8]
+                dots[0:8, here] = dots[0:8, here] + dot[:8]
 
         for h in range(quarter * peers_head // 4, (quarter + 1) * peers_head // 4):
             by_head(h)
@@ -1311,6 +1365,7 @@
                 turned, d_state[...], preferred_element_type=F32
             ).astype(BF16)
             blocks[h, pl.ds(width, 16)] = rest[0:16].astype(BF16)
+        dots[8:16, 0:states] = grads_s[...]
         for kind in range(4):
             start(head_copies(kind))
         steps = lax.dot_general(
@@ -1326,17 +1381,26 @@
         rest[at : at + 2, 0:LANES] = grads_h[0:2]
         packed[pl.ds(block, rest.shape[0] - 16)] = rest[16:].astype(BF16)
 
+    waited = []
+
+    def dots_total():
+        if not waited:
+            waited.append(received(head_copies(1)))
+        summed = dots[...]
+        for d in range(peers_head - 1):
+            summed = summed + dots_in[d]
+        return summed
+
     def pack():
         received(head_copies(0))
         others = [(block_in.at[d], 0) for d in range(peers_head - 1)]
         add_rows((packed, 0), [(blocks.at[head], 0)] + others, block)
+        filters = dots_total()[8:16, 0 : packed.shape[1]]
+        kept = packed[pl.ds(width, 16)].astype(F32)
+        packed[pl.ds(width, 16)] = jnp.concatenate([filters, kept[8:16]], axis=0).astype(BF16)
 
     def sum_heads():
-        received(head_copies(1))
-        summed = dots[...]
-        for d in range(peers_head - 1):
-            summed = summed + dots_in[d]
-        dots_sum[...] = summed
+        dots_sum[...] = dots_total()[0:8]
         for kind, mine, boxes, target in (
             (2, normed_part, normed_in, normed_sum), (3, mixed_part, mixed_in, mixed_sum)
         ):
@@ -1389,19 +1453,21 @@
         vmem((peers_head, width + 16, states), BF16), vmem((others, width + 16, states), BF16),
         vmem((peers_head, tokens, width), BF16), vmem((others, tokens, width), BF16),
         vmem((peers_head, tokens, width), BF16), vmem((others, tokens, width), BF16),
-        vmem((8, tokens), F32), vmem((others, 8, tokens), F32), vmem((1, features), F32),
+        vmem((16, tokens), F32), vmem((others, 16, tokens), F32), vmem((1, features), F32),
         vmem((total - width, states), F32), vmem((tokens, width), F32),
-        dma((5,)), dma((5, others)), dma((5, others)),
+        dma((13,)), dma((5, others)), dma((5, others)),
     ]
+    large = [0, 1, 2, 5, 6, 7, 8, 9]
+    scratch += [vmem(values[k].shape, BF16) for k in large]
     anywhere, inside = pl.BlockSpec(memory_space=pl.ANY), pl.BlockSpec(memory_space=pltpu.VMEM)
-    operands = list(values) + list(grads)
+    operands = [values[3], values[4], *grads] + [values[k] for k in large]
     return pl.pallas_call(
         functools.partial(sum_rows, jobs, order, lines, peers_head, len(given)),
         out_shape=whole
         + [shape((peers_head, width, states), BF16)]
         + [shape((tokens, width), F32)] * 2
         + [shape((8, tokens), F32)],
-        in_specs=[inside] * len(operands) + [anywhere] * 5 + [inside] * len(given),
+        in_specs=[inside] * 5 + [anywhere] * 13 + [inside] * len(given),
         out_specs=[anywhere] * 5 + [inside] * 3,
         scratch_shapes=scratch,
         compiler_params=pltpu.CompilerParams(

time: 239 us -> 236 us (0.987)
  Pallas kernels: 238 us -> 234 us
where the time goes in v5:
time: 236 us; the launch traced here: 235 us
  Pallas kernels  234 us (99%)
    pallas_call x1, Pallas kernels, sum_over_seq(): pl.pallas_call(functools.partial(sum_rows, jobs, order, lines, peers_head...  138 us
    pallas_call x1, Pallas kernels, mix(): pl.pallas_call(functools.partial(mixer_kernel, count, peers_head, inner,...  83.8 us
    pallas_call x1, Pallas kernels, finish(): pl.pallas_call(functools.partial(finish_kernel, features, steps), grid=(s...  12.3 us

profile of v5, /device:TPU:0, one launch (start us, length us, event | category | flops | bytes accessed | tf_op | source)
XLA Modules:
  0.0 235.3 jit_solution(17164962575189284071)
XLA Ops:
  0.7 83.8 %shard_map.288 = (bf16[512,1536]{1,0:T(8,128)(2,1)}, f32[512,1]{1,0:T(8,128)}, bf16[4,512,384]{2,1,0:T(8,128)(2,1)}, bf16[4,512,384]{2,1,0:T(8,128)(2,1)}, f32[4...) custom-call(s32[4]{0:T(128)} %lengths.1, ...), custom_call_target="tpu_custom_call" | custom-call | tf_op jit(solution)/shard_map/pallas_call | solution.py:1191
  84.4 138.4 %shard_map.289 = (bf16[512,256]{1,0:T(8,128)(2,1)}, bf16[768,1536]{1,0:T(8,128)(2,1)}, bf16[1536,768]{1,0:T(8,128)(2,1)}, bf16[1536,768]{1,0:T(8,128)(2,1)}, bf1...) custom-call(f32[512,1]{1,0:T(8,128)} %get-tuple-element.55.refs_0_.scale, ...), custom_call_target="tpu_custom_call" | custom-call | tf_op jit(solution)/shard_map/pallas_call | solution.py:1464
  222.8 12.3 %shard_map.290 = (f32[768,1536]{1,0:T(8,128)}, f32[1536,768]{1,0:T(8,128)}, f32[1536,768]{1,0:T(8,128)}, f32[1536,256]{1,0:T(8,128)}, bf16[512,384]{1,0:T(8,128)...) custom-call(bf16[768,1536]{1,0:T(8,128)(2,1)} %get-tuple-element.70., ...), custom_call_target="tpu_custom_call" | custom-call | tf_op jit(solution)/shard_map/pallas_call | solution.py:1566
